TPU v7x, 256 devices: a 4x2x16 block of a 4x16x16 slice. The times are simulated.
256 devices in a mesh: parts: 2 (over y), seq: 16 (over z), head: 4 (over x), rep: 2 (over core).
Axes of the slice: x: 4, y: 2, z: 16, core: 2. Of those that a mesh axis runs over, the one named last changes fastest.
The devices are a block of a 4x16x16 slice.
Arguments:
- queries: bfloat16 [4, 4096, 2048], P(('parts', 'rep'), 'seq', 'head'), parts along dimension 0, may hold values from -6 to 6
- reflect_keys: bfloat16 [4, 4096, 2, 2048], P(('parts', 'rep'), 'seq', None, 'head'), parts along dimension 0, may hold values from -6 to 6
- reflect_values: bfloat16 [4, 4096, 2, 2048], P(('parts', 'rep'), 'seq', None, 'head'), parts along dimension 0, may hold values from -6 to 6
- reflect_beta: float32 [4, 4096, 2, 16], P(('parts', 'rep'), 'seq', None, 'head'), parts along dimension 0, may hold values from 0.2 to 2
- log_decay: float32 [4, 4096, 16], P(('parts', 'rep'), 'seq', 'head'), parts along dimension 0, may hold values from -2.5 to 0
- prompt_lengths: int32 [4, 6], P(('parts', 'rep')), parts along dimension 0, may hold values from 1 to 2048, 4096 in all within a row
- norm_gain: float32 [128], replicated, may hold values from 0.1 to 1.9
- out_weight: bfloat16 [2048, 2048], P('head'), may hold values from -0.125 to 0.125
Outputs:
- layer_out: bfloat16 [4, 4096, 2048], P(('parts', 'rep'), ('seq', 'head')), parts along dimension 0
There are 2 independent parts, one for each index of `parts`. A program takes and returns all parts, laid end to end along the dimension named above; an argument that names none is the same for every part. Nothing has to cross between parts.
Inputs may be any that keep to these rules, and one draw needn't show every extreme that they name: `prompt_lengths`: the 6 prompts of a pack lie end to end from its first token and cover all 4096 tokens; the longest has exactly 2048.
All inputs are finite; a program needn't handle non-finite values.
Results may differ from a plain program's by a relative error of at most 0.0095.
Values may be sent and summed in bfloat16 or wider, within the bound.
No kernel may reach another device: no remote copies, remote signals or barrier semaphores. Data moves between devices by JAX's collectives and lax.ppermute only.
A program may use at most 64 MiB of HBM per device.

v0:
```python
import jax
import jax.numpy as jnp
from jax import lax
from jax.sharding import PartitionSpec as P

BLOCK = 64


highest = lax.Precision.HIGHEST
epsilon = 1e-06


def shifted(value, axis, steps):
    count = lax.axis_size(axis)
    initial, last = (max(0, -steps), min(count, count - steps))
    return lax.ppermute(value, axis, [(source, source + steps) for source in range(initial, last)])


def cut_along(array, dim, length):
    lengths = array.shape
    parts = array.reshape(*lengths[:dim], length, lengths[dim] // length, *lengths[dim + 1 :])
    return jnp.moveaxis(parts, dim, 0)


def summed_on_arrival(array, axis, dim):
    parts = cut_along(array, dim, lax.axis_size(axis))
    arrived = lax.all_to_all(parts, axis, split_axis=0, concat_axis=0, tiled=True)
    return arrived.astype(jnp.float32).sum(axis=0)


def unit_rows(vectors):
    return vectors * lax.rsqrt(jnp.sum(vectors * vectors, axis=-1, keepdims=True) + epsilon)


def block_parts(key_rows, value_rows, beta_rows, decay_rows, seg_rows, seg_before):
    steps_here = key_rows.shape[-2]
    cum_decay = jnp.cumsum(decay_rows, axis=-1)
    ordinal = jnp.arange(steps_here)
    incl_mask = ordinal[:, None] >= ordinal[None, :]
    strict_mask = ordinal[:, None] > ordinal[None, :]
    same_doc = seg_rows[:, None, :, None] == seg_rows[:, None, None, :]
    decay_gap = cum_decay[..., :, None] - cum_decay[..., None, :]
    decay_ratio = jnp.where(incl_mask & same_doc, jnp.exp(jnp.minimum(decay_gap, 0.0)), 0.0)
    carry_in = jnp.where(seg_rows[:, None, :] == seg_before[:, None, None], jnp.exp(cum_decay), 0.0)
    key_inner = jnp.einsum("bhik,bhjk->bhij", key_rows, key_rows, precision=highest)
    system = jnp.eye(steps_here, dtype=key_rows.dtype) + jnp.where(
        strict_mask, beta_rows[..., :, None] * decay_ratio * key_inner, 0.0
    )
    right_side = jnp.concatenate(
        [beta_rows[..., None] * value_rows, (beta_rows * carry_in)[..., None] * key_rows], axis=-1
    )
    solved = lax.linalg.triangular_solve(
        system, right_side, left_side=True, lower=True, unit_diagonal=True
    )
    val_width = value_rows.shape[-1]
    return (decay_ratio, carry_in, solved[..., :val_width], solved[..., val_width:])


def heads_product(left_maps, right_maps):
    return jnp.einsum("hij,hjk->hik", left_maps, right_maps, precision=highest)


def body(
    queries,
    reflect_keys,
    reflect_values,
    reflect_beta,
    log_decay,
    prompt_lengths,
    norm_gain,
    out_weight,
):
    tokens_here = queries.shape[1]
    refl_count = reflect_keys.shape[2]
    heads_here = reflect_beta.shape[3]
    head_width = queries.shape[2] // heads_here
    blocks = tokens_here // BLOCK
    sub_steps = refl_count * BLOCK
    offset = lax.axis_index("seq") * tokens_here
    doc_ends = jnp.cumsum(prompt_lengths[0])
    positions = offset + jnp.arange(tokens_here, dtype=jnp.int32)
    segment = jnp.sum((positions[:, None] >= doc_ends[None, :]).astype(jnp.int32), axis=-1)
    block_starts = positions[::BLOCK] - 1
    earlier_seg = jnp.sum((block_starts[:, None] >= doc_ends[None, :]).astype(jnp.int32), axis=-1)
    seg_before = jnp.where(block_starts < 0, -1, earlier_seg)
    seg_rows = jnp.repeat(segment.reshape(blocks, BLOCK), refl_count, axis=-1)
    query_rows = unit_rows(
        queries[0].astype(jnp.float32).reshape(blocks, BLOCK, heads_here, head_width)
    ) * head_width ** (-0.5)
    query_rows = query_rows.transpose(0, 2, 1, 3)
    key_rows = unit_rows(
        reflect_keys[0]
        .astype(jnp.float32)
        .reshape(blocks, BLOCK, refl_count, heads_here, head_width)
    )
    key_rows = key_rows.transpose(0, 3, 1, 2, 4).reshape(blocks, heads_here, sub_steps, head_width)
    value_rows = (
        reflect_values[0]
        .astype(jnp.float32)
        .reshape(blocks, BLOCK, refl_count, heads_here, head_width)
    )
    value_rows = value_rows.transpose(0, 3, 1, 2, 4).reshape(
        blocks, heads_here, sub_steps, head_width
    )
    beta_rows = (
        reflect_beta[0]
        .reshape(blocks, BLOCK, refl_count, heads_here)
        .transpose(0, 3, 1, 2)
        .reshape(blocks, heads_here, sub_steps)
    )
    gate_rows = log_decay[0].reshape(blocks, BLOCK, heads_here).transpose(0, 2, 1)
    decay_rows = jnp.concatenate(
        [gate_rows[..., None], jnp.zeros(gate_rows.shape + (refl_count - 1,), jnp.float32)], axis=-1
    ).reshape(blocks, heads_here, sub_steps)
    decay_ratio, carry_in, write_vals, write_keys = block_parts(
        key_rows, value_rows, beta_rows, decay_rows, seg_rows, seg_before
    )
    last_row = refl_count - 1
    read_weights = decay_ratio[..., last_row::refl_count, :] * jnp.einsum(
        "bhik,bhjk->bhij", query_rows, key_rows, precision=highest
    )
    carry_read = carry_in[..., last_row::refl_count]
    end_keys = decay_ratio[..., -1, :, None] * key_rows
    block_maps = carry_in[..., -1, None, None] * jnp.eye(
        head_width, dtype=jnp.float32
    ) - jnp.einsum("bhjk,bhjl->bhkl", end_keys, write_keys, precision=highest)
    block_adds = jnp.einsum("bhjk,bhjl->bhkl", end_keys, write_vals, precision=highest)
    identity_maps = jnp.broadcast_to(
        jnp.eye(head_width, dtype=jnp.float32), (heads_here, head_width, head_width)
    )
    zero_states = jnp.zeros((heads_here, head_width, head_width), jnp.float32)

    def compose_only(totals, step_pair):
        joined = (
            heads_product(step_pair[0], totals[0]),
            heads_product(step_pair[0], totals[1]) + step_pair[1],
        )
        return (joined, None)

    (device_map, device_add), unused = lax.scan(
        compose_only, (identity_maps, zero_states), (block_maps, block_adds)
    )

    def advance_hop(turn_index, current):
        return shifted(
            (heads_product(device_map, current) + device_add).astype(jnp.bfloat16), "seq", 1
        ).astype(jnp.float32)

    incoming = lax.fori_loop(0, lax.axis_size("seq") - 1, advance_hop, zero_states)

    def advance_block(current, step_pair):
        return (heads_product(step_pair[0], current) + step_pair[1], current)

    finished, block_start = lax.scan(advance_block, incoming, (block_maps, block_adds))
    updates = write_vals - jnp.einsum("bhck,bhkv->bhcv", write_keys, block_start, precision=highest)
    head_out = carry_read[..., None] * jnp.einsum(
        "bhik,bhkv->bhiv", query_rows, block_start, precision=highest
    ) + jnp.einsum("bhij,bhjv->bhiv", read_weights, updates, precision=highest)
    normed = (
        head_out
        * lax.rsqrt(jnp.mean(head_out * head_out, axis=-1, keepdims=True) + epsilon)
        * norm_gain
    ).astype(jnp.bfloat16)
    flat_rows = normed.transpose(0, 2, 1, 3).reshape(tokens_here, heads_here * head_width)
    layer_out = summed_on_arrival(
        jnp.dot(flat_rows, out_weight, preferred_element_type=jnp.float32).astype(jnp.bfloat16),
        "head",
        0,
    )
    return layer_out.astype(jnp.bfloat16)[None]


def solution(mesh):
    in_specs = (
        P(("parts", "rep"), "seq", "head"),
        P(("parts", "rep"), "seq", None, "head"),
        P(("parts", "rep"), "seq", None, "head"),
        P(("parts", "rep"), "seq", None, "head"),
        P(("parts", "rep"), "seq", "head"),
        P(("parts", "rep"), None),
        P(),
        P("head", None),
    )
    out_specs = P(("parts", "rep"), ("seq", "head"), None)
    return jax.shard_map(body, mesh=mesh, in_specs=in_specs, out_specs=out_specs, check_vma=False)
```

profile of v0, /device:TPU:40, one launch (start us, length us, event | category | flops | bytes accessed | tf_op | source)
XLA Modules:
  0.0 371.1 jit_solution(6007310271413440816)
XLA Ops:
  9.2 3.2 slice.31
  21.8 3.4 fusion.27
  25.2 158.7 %custom-call.3 = f32[4,4,1,128,128]{3,4,2,1,0:T(8,128)} custom-call(f32[4,4,1,128,128]{4,3,2,1,0:T(8,128)} %fusion.27), custom_call_target="InvertDiagBlocksLowerTriangular" | custom-call | tf_op jit(solution)/shard_map/triangular_solve | solution.py:52
  190.5 3.2 fusion.29
  193.7 3.3 convolution_subtract_fusion.1
  196.9 11.4 %while.40 = (s32[]{:T(128)}, f32[4,128,128]{2,1,0:T(8,128)S(1)}, f32[4,128,128]{2,1,0:T(8,128)S(1)}, f32[4,4,128,128]{3,2,1,0:T(8,128)}, f32[4,4,128,128]{3,2,1,0:T(8,128)}) while((s32[]{:T(128)}, f32[4,128,128]{2,1,0:T(8,128)S(1)}, f32[4,128,128]{2,1,0:T(8,128)S(1)}, f32[4,4,128,128]{3,2,1,0:T(8,128)}, ...), condition=%wide.region_7.8_spmd.clone.clone, body=%wide.region_6.7_spmd.clone.sunk.clone | while | flops 201457664 | bytes 2885202 | solution.py:140
  208.4 128.4 %while.41 = (s32[]{:T(128)}, f32[4,128,128]{2,1,0:T(8,128)S(1)}, f32[4,128,128]{2,1,0:T(8,128)S(1)}, f32[4,128,128]{2,1,0:T(8,128)S(1)}) while((s32[]{:T(128)}, f32[4,128,128]{2,1,0:T(8,128)S(1)}, f32[4,128,128]{2,1,0:T(8,128)S(1)}, f32[4,128,128]{2,1,0:T(8,128)S(1)}) %tuple.69), condition=%wide.region_9.10_spmd.clone.clone, body=%wide.region_8.9_spmd.clone.sunk.clone | while | flops 100925440 | bytes 1835111 | solution.py:149
  208.8 4.7 %collective-permute-start = (bf16[4,128,128]{2,1,0:T(8,128)(2,1)S(1)}, bf16[4,128,128]{2,1,0:T(8,128)(2,1)S(1)}, u32[]{:S(2)}, u32[]{:S(2)}) collective-permute-start(bf16[4,128,128]{2,1,0:T(8,128)(2,1)S(1)} %fusion.89), channel_id=1, source_target_pairs={{0,8},{8,16},{16,24},{24,32},{32,40},{40,48},{48,56},{56,64},{64,7... | collective-permute-start | bytes 393224 | tf_op jit(solution)/shard_map/while/body/eval_jaxpr/ppermute | solution.py:16
  213.5 2.8 collective-permute-done
  216.8 4.7 %collective-permute-start = (bf16[4,128,128]{2,1,0:T(8,128)(2,1)S(1)}, bf16[4,128,128]{2,1,0:T(8,128)(2,1)S(1)}, u32[]{:S(2)}, u32[]{:S(2)}) collective-permute-start(bf16[4,128,128]{2,1,0:T(8,128)(2,1)S(1)} %fusion.89), channel_id=1, source_target_pairs={{0,8},{8,16},{16,24},{24,32},{32,40},{40,48},{48,56},{56,64},{64,7... | collective-permute-start | bytes 393224 | tf_op jit(solution)/shard_map/while/body/eval_jaxpr/ppermute | solution.py:16
  221.5 2.5 collective-permute-done
  224.4 4.7 %collective-permute-start = (bf16[4,128,128]{2,1,0:T(8,128)(2,1)S(1)}, bf16[4,128,128]{2,1,0:T(8,128)(2,1)S(1)}, u32[]{:S(2)}, u32[]{:S(2)}) collective-permute-start(bf16[4,128,128]{2,1,0:T(8,128)(2,1)S(1)} %fusion.89), channel_id=1, source_target_pairs={{0,8},{8,16},{16,24},{24,32},{32,40},{40,48},{48,56},{56,64},{64,7... | collective-permute-start | bytes 393224 | tf_op jit(solution)/shard_map/while/body/eval_jaxpr/ppermute | solution.py:16
  232.1 5.9 %collective-permute-start = (bf16[4,128,128]{2,1,0:T(8,128)(2,1)S(1)}, bf16[4,128,128]{2,1,0:T(8,128)(2,1)S(1)}, u32[]{:S(2)}, u32[]{:S(2)}) collective-permute-start(bf16[4,128,128]{2,1,0:T(8,128)(2,1)S(1)} %fusion.89), channel_id=1, source_target_pairs={{0,8},{8,16},{16,24},{24,32},{32,40},{40,48},{48,56},{56,64},{64,7... | collective-permute-start | bytes 393224 | tf_op jit(solution)/shard_map/while/body/eval_jaxpr/ppermute | solution.py:16
  238.0 2.5 collective-permute-done
  241.0 5.6 %collective-permute-start = (bf16[4,128,128]{2,1,0:T(8,128)(2,1)S(1)}, bf16[4,128,128]{2,1,0:T(8,128)(2,1)S(1)}, u32[]{:S(2)}, u32[]{:S(2)}) collective-permute-start(bf16[4,128,128]{2,1,0:T(8,128)(2,1)S(1)} %fusion.89), channel_id=1, source_target_pairs={{0,8},{8,16},{16,24},{24,32},{32,40},{40,48},{48,56},{56,64},{64,7... | collective-permute-start | bytes 393224 | tf_op jit(solution)/shard_map/while/body/eval_jaxpr/ppermute | solution.py:16
  246.6 2.5 collective-permute-done
  249.5 5.6 %collective-permute-start = (bf16[4,128,128]{2,1,0:T(8,128)(2,1)S(1)}, bf16[4,128,128]{2,1,0:T(8,128)(2,1)S(1)}, u32[]{:S(2)}, u32[]{:S(2)}) collective-permute-start(bf16[4,128,128]{2,1,0:T(8,128)(2,1)S(1)} %fusion.89), channel_id=1, source_target_pairs={{0,8},{8,16},{16,24},{24,32},{32,40},{40,48},{48,56},{56,64},{64,7... | collective-permute-start | bytes 393224 | tf_op jit(solution)/shard_map/while/body/eval_jaxpr/ppermute | solution.py:16
  255.1 2.5 collective-permute-done
  258.1 5.6 %collective-permute-start = (bf16[4,128,128]{2,1,0:T(8,128)(2,1)S(1)}, bf16[4,128,128]{2,1,0:T(8,128)(2,1)S(1)}, u32[]{:S(2)}, u32[]{:S(2)}) collective-permute-start(bf16[4,128,128]{2,1,0:T(8,128)(2,1)S(1)} %fusion.89), channel_id=1, source_target_pairs={{0,8},{8,16},{16,24},{24,32},{32,40},{40,48},{48,56},{56,64},{64,7... | collective-permute-start | bytes 393224 | tf_op jit(solution)/shard_map/while/body/eval_jaxpr/ppermute | solution.py:16
  263.7 3.3 collective-permute-done
  267.4 6.1 %collective-permute-start = (bf16[4,128,128]{2,1,0:T(8,128)(2,1)S(1)}, bf16[4,128,128]{2,1,0:T(8,128)(2,1)S(1)}, u32[]{:S(2)}, u32[]{:S(2)}) collective-permute-start(bf16[4,128,128]{2,1,0:T(8,128)(2,1)S(1)} %fusion.89), channel_id=1, source_target_pairs={{0,8},{8,16},{16,24},{24,32},{32,40},{40,48},{48,56},{56,64},{64,7... | collective-permute-start | bytes 393224 | tf_op jit(solution)/shard_map/while/body/eval_jaxpr/ppermute | solution.py:16
  273.5 3.3 collective-permute-done
  277.3 5.9 %collective-permute-start = (bf16[4,128,128]{2,1,0:T(8,128)(2,1)S(1)}, bf16[4,128,128]{2,1,0:T(8,128)(2,1)S(1)}, u32[]{:S(2)}, u32[]{:S(2)}) collective-permute-start(bf16[4,128,128]{2,1,0:T(8,128)(2,1)S(1)} %fusion.89), channel_id=1, source_target_pairs={{0,8},{8,16},{16,24},{24,32},{32,40},{40,48},{48,56},{56,64},{64,7... | collective-permute-start | bytes 393224 | tf_op jit(solution)/shard_map/while/body/eval_jaxpr/ppermute | solution.py:16
  286.1 5.1 %collective-permute-start = (bf16[4,128,128]{2,1,0:T(8,128)(2,1)S(1)}, bf16[4,128,128]{2,1,0:T(8,128)(2,1)S(1)}, u32[]{:S(2)}, u32[]{:S(2)}) collective-permute-start(bf16[4,128,128]{2,1,0:T(8,128)(2,1)S(1)} %fusion.89), channel_id=1, source_target_pairs={{0,8},{8,16},{16,24},{24,32},{32,40},{40,48},{48,56},{56,64},{64,7... | collective-permute-start | bytes 393224 | tf_op jit(solution)/shard_map/while/body/eval_jaxpr/ppermute | solution.py:16
  294.1 5.6 %collective-permute-start = (bf16[4,128,128]{2,1,0:T(8,128)(2,1)S(1)}, bf16[4,128,128]{2,1,0:T(8,128)(2,1)S(1)}, u32[]{:S(2)}, u32[]{:S(2)}) collective-permute-start(bf16[4,128,128]{2,1,0:T(8,128)(2,1)S(1)} %fusion.89), channel_id=1, source_target_pairs={{0,8},{8,16},{16,24},{24,32},{32,40},{40,48},{48,56},{56,64},{64,7... | collective-permute-start | bytes 393224 | tf_op jit(solution)/shard_map/while/body/eval_jaxpr/ppermute | solution.py:16
  302.7 5.6 %collective-permute-start = (bf16[4,128,128]{2,1,0:T(8,128)(2,1)S(1)}, bf16[4,128,128]{2,1,0:T(8,128)(2,1)S(1)}, u32[]{:S(2)}, u32[]{:S(2)}) collective-permute-start(bf16[4,128,128]{2,1,0:T(8,128)(2,1)S(1)} %fusion.89), channel_id=1, source_target_pairs={{0,8},{8,16},{16,24},{24,32},{32,40},{40,48},{48,56},{56,64},{64,7... | collective-permute-start | bytes 393224 | tf_op jit(solution)/shard_map/while/body/eval_jaxpr/ppermute | solution.py:16
  311.3 5.6 %collective-permute-start = (bf16[4,128,128]{2,1,0:T(8,128)(2,1)S(1)}, bf16[4,128,128]{2,1,0:T(8,128)(2,1)S(1)}, u32[]{:S(2)}, u32[]{:S(2)}) collective-permute-start(bf16[4,128,128]{2,1,0:T(8,128)(2,1)S(1)} %fusion.89), channel_id=1, source_target_pairs={{0,8},{8,16},{16,24},{24,32},{32,40},{40,48},{48,56},{56,64},{64,7... | collective-permute-start | bytes 393224 | tf_op jit(solution)/shard_map/while/body/eval_jaxpr/ppermute | solution.py:16
  319.8 5.6 %collective-permute-start = (bf16[4,128,128]{2,1,0:T(8,128)(2,1)S(1)}, bf16[4,128,128]{2,1,0:T(8,128)(2,1)S(1)}, u32[]{:S(2)}, u32[]{:S(2)}) collective-permute-start(bf16[4,128,128]{2,1,0:T(8,128)(2,1)S(1)} %fusion.89), channel_id=1, source_target_pairs={{0,8},{8,16},{16,24},{24,32},{32,40},{40,48},{48,56},{56,64},{64,7... | collective-permute-start | bytes 393224 | tf_op jit(solution)/shard_map/while/body/eval_jaxpr/ppermute | solution.py:16
  328.4 5.9 %collective-permute-start = (bf16[4,128,128]{2,1,0:T(8,128)(2,1)S(1)}, bf16[4,128,128]{2,1,0:T(8,128)(2,1)S(1)}, u32[]{:S(2)}, u32[]{:S(2)}) collective-permute-start(bf16[4,128,128]{2,1,0:T(8,128)(2,1)S(1)} %fusion.89), channel_id=1, source_target_pairs={{0,8},{8,16},{16,24},{24,32},{32,40},{40,48},{48,56},{56,64},{64,7... | collective-permute-start | bytes 393224 | tf_op jit(solution)/shard_map/while/body/eval_jaxpr/ppermute | solution.py:16
  336.8 9.0 %while.39 = (s32[]{:T(128)}, f32[4,128,128]{2,1,0:T(8,128)S(1)}, f32[4,4,128,128]{3,2,1,0:T(8,128)}, f32[4,4,128,128]{3,2,1,0:T(8,128)}, f32[4,4,128,128]{3,2,1,0:T(8,128)}) while((s32[]{:T(128)}, f32[4,128,128]{2,1,0:T(8,128)S(1)}, f32[4,4,128,128]{3,2,1,0:T(8,128)}, f32[4,4,128,128]{3,2,1,0:T(8,128)}, ...), condition=%wide.region_11.12_spmd.clone, body=%wide.region_10.11_spmd.sunk.clone | while | flops 100728832 | bytes 2098249 | solution.py:154
  345.8 3.2 convolution_subtract_fusion
  354.9 15.3 %all_to_all.5 = bf16[4,64,2048]{2,1,0:T(8,128)(2,1)S(1)} all-to-all(bf16[4,64,2048]{2,1,0:T(8,128)(2,1)S(1)} %bitcast.107), channel_id=1, replica_groups=mesh['parts'=2,'seq'=16,'head'=4,'rep'=2] {'head'}, dimensions={0} | all-to-all | bytes 2097152 | tf_op jit(solution)/shard_map/all_to_all | solution.py:27
  (164 shorter events, 77.6 us)
Async XLA Ops:
  0.0 354.2 %copy-start = (bf16[512,2048]{1,0:T(8,128)(2,1)S(1)}, bf16[512,2048]{1,0:T(8,128)(2,1)}, u32[]{:S(2)}) copy-start(bf16[512,2048]{1,0:T(8,128)(2,1)} %param.21) | copy-start | bytes 6291460
  0.0 13.1 %copy-start.12 = (bf16[1,256,512]{2,1,0:T(8,128)(2,1)S(1)}, bf16[1,256,512]{2,1,0:T(8,128)(2,1)}, u32[]{:S(2)}) copy-start(bf16[1,256,512]{2,1,0:T(8,128)(2,1)} %param.14) | copy-start | bytes 786436
  17.3 2.2 copy-start.5
  19.6 2.2 copy-start.15
  19.6 2.2 copy-start.16
  19.6 2.2 copy-start.18
  19.6 2.2 copy-start.19
  20.8 163.1 %copy-start.11 = (bf16[1,256,2,512]{3,2,1,0:T(2,128)(2,1)S(1)}, bf16[1,256,2,512]{3,2,1,0:T(2,128)(2,1)}, u32[]{:S(2)}) copy-start(bf16[1,256,2,512]{3,2,1,0:T(2,128)(2,1)} %param.16) | copy-start | bytes 1572868
  25.2 162.0 %copy-start.17 = (f32[4,4,128]{2,1,0:T(4,128)S(1)}, f32[4,4,128]{2,1,0:T(4,128)}, u32[]{:S(2)}) copy-start(f32[4,4,128]{2,1,0:T(4,128)} %get-tuple-element.147) | copy-start | bytes 24580
  188.4 2.0 copy-start.13
  190.4 6.5 %copy-start.4 = (f32[4,4,128,256]{3,2,1,0:T(8,128)}, f32[4,4,128,256]{3,2,1,0:T(8,128)S(1)}, u32[]{:S(2)}) copy-start(f32[4,4,128,256]{3,2,1,0:T(8,128)S(1)} %fusion.19) | copy-start | bytes 6291460
  190.4 3.2 copy-start.20
  208.8 7.5 %collective-permute-start = (bf16[4,128,128]{2,1,0:T(8,128)(2,1)S(1)}, bf16[4,128,128]{2,1,0:T(8,128)(2,1)S(1)}, u32[]{:S(2)}, u32[]{:S(2)}) collective-permute-start(bf16[4,128,128]{2,1,0:T(8,128)(2,1)S(1)} %fusion.89), channel_id=1, source_target_pairs={{0,8},{8,16},{16,24},{24,32},{32,40},{40,48},{48,56},{56,64},{64,7... | collective-permute-start | bytes 393224 | tf_op jit(solution)/shard_map/while/body/eval_jaxpr/ppermute | solution.py:16
  216.8 7.2 %collective-permute-start = (bf16[4,128,128]{2,1,0:T(8,128)(2,1)S(1)}, bf16[4,128,128]{2,1,0:T(8,128)(2,1)S(1)}, u32[]{:S(2)}, u32[]{:S(2)}) collective-permute-start(bf16[4,128,128]{2,1,0:T(8,128)(2,1)S(1)} %fusion.89), channel_id=1, source_target_pairs={{0,8},{8,16},{16,24},{24,32},{32,40},{40,48},{48,56},{56,64},{64,7... | collective-permute-start | bytes 393224 | tf_op jit(solution)/shard_map/while/body/eval_jaxpr/ppermute | solution.py:16
  224.4 7.2 %collective-permute-start = (bf16[4,128,128]{2,1,0:T(8,128)(2,1)S(1)}, bf16[4,128,128]{2,1,0:T(8,128)(2,1)S(1)}, u32[]{:S(2)}, u32[]{:S(2)}) collective-permute-start(bf16[4,128,128]{2,1,0:T(8,128)(2,1)S(1)} %fusion.89), channel_id=1, source_target_pairs={{0,8},{8,16},{16,24},{24,32},{32,40},{40,48},{48,56},{56,64},{64,7... | collective-permute-start | bytes 393224 | tf_op jit(solution)/shard_map/while/body/eval_jaxpr/ppermute | solution.py:16
  232.1 8.4 %collective-permute-start = (bf16[4,128,128]{2,1,0:T(8,128)(2,1)S(1)}, bf16[4,128,128]{2,1,0:T(8,128)(2,1)S(1)}, u32[]{:S(2)}, u32[]{:S(2)}) collective-permute-start(bf16[4,128,128]{2,1,0:T(8,128)(2,1)S(1)} %fusion.89), channel_id=1, source_target_pairs={{0,8},{8,16},{16,24},{24,32},{32,40},{40,48},{48,56},{56,64},{64,7... | collective-permute-start | bytes 393224 | tf_op jit(solution)/shard_map/while/body/eval_jaxpr/ppermute | solution.py:16
  241.0 8.1 %collective-permute-start = (bf16[4,128,128]{2,1,0:T(8,128)(2,1)S(1)}, bf16[4,128,128]{2,1,0:T(8,128)(2,1)S(1)}, u32[]{:S(2)}, u32[]{:S(2)}) collective-permute-start(bf16[4,128,128]{2,1,0:T(8,128)(2,1)S(1)} %fusion.89), channel_id=1, source_target_pairs={{0,8},{8,16},{16,24},{24,32},{32,40},{40,48},{48,56},{56,64},{64,7... | collective-permute-start | bytes 393224 | tf_op jit(solution)/shard_map/while/body/eval_jaxpr/ppermute | solution.py:16
  249.5 8.1 %collective-permute-start = (bf16[4,128,128]{2,1,0:T(8,128)(2,1)S(1)}, bf16[4,128,128]{2,1,0:T(8,128)(2,1)S(1)}, u32[]{:S(2)}, u32[]{:S(2)}) collective-permute-start(bf16[4,128,128]{2,1,0:T(8,128)(2,1)S(1)} %fusion.89), channel_id=1, source_target_pairs={{0,8},{8,16},{16,24},{24,32},{32,40},{40,48},{48,56},{56,64},{64,7... | collective-permute-start | bytes 393224 | tf_op jit(solution)/shard_map/while/body/eval_jaxpr/ppermute | solution.py:16
  258.1 8.9 %collective-permute-start = (bf16[4,128,128]{2,1,0:T(8,128)(2,1)S(1)}, bf16[4,128,128]{2,1,0:T(8,128)(2,1)S(1)}, u32[]{:S(2)}, u32[]{:S(2)}) collective-permute-start(bf16[4,128,128]{2,1,0:T(8,128)(2,1)S(1)} %fusion.89), channel_id=1, source_target_pairs={{0,8},{8,16},{16,24},{24,32},{32,40},{40,48},{48,56},{56,64},{64,7... | collective-permute-start | bytes 393224 | tf_op jit(solution)/shard_map/while/body/eval_jaxpr/ppermute | solution.py:16
  267.4 9.4 %collective-permute-start = (bf16[4,128,128]{2,1,0:T(8,128)(2,1)S(1)}, bf16[4,128,128]{2,1,0:T(8,128)(2,1)S(1)}, u32[]{:S(2)}, u32[]{:S(2)}) collective-permute-start(bf16[4,128,128]{2,1,0:T(8,128)(2,1)S(1)} %fusion.89), channel_id=1, source_target_pairs={{0,8},{8,16},{16,24},{24,32},{32,40},{40,48},{48,56},{56,64},{64,7... | collective-permute-start | bytes 393224 | tf_op jit(solution)/shard_map/while/body/eval_jaxpr/ppermute | solution.py:16
  277.3 8.4 %collective-permute-start = (bf16[4,128,128]{2,1,0:T(8,128)(2,1)S(1)}, bf16[4,128,128]{2,1,0:T(8,128)(2,1)S(1)}, u32[]{:S(2)}, u32[]{:S(2)}) collective-permute-start(bf16[4,128,128]{2,1,0:T(8,128)(2,1)S(1)} %fusion.89), channel_id=1, source_target_pairs={{0,8},{8,16},{16,24},{24,32},{32,40},{40,48},{48,56},{56,64},{64,7... | collective-permute-start | bytes 393224 | tf_op jit(solution)/shard_map/while/body/eval_jaxpr/ppermute | solution.py:16
  286.1 7.6 %collective-permute-start = (bf16[4,128,128]{2,1,0:T(8,128)(2,1)S(1)}, bf16[4,128,128]{2,1,0:T(8,128)(2,1)S(1)}, u32[]{:S(2)}, u32[]{:S(2)}) collective-permute-start(bf16[4,128,128]{2,1,0:T(8,128)(2,1)S(1)} %fusion.89), channel_id=1, source_target_pairs={{0,8},{8,16},{16,24},{24,32},{32,40},{40,48},{48,56},{56,64},{64,7... | collective-permute-start | bytes 393224 | tf_op jit(solution)/shard_map/while/body/eval_jaxpr/ppermute | solution.py:16
  294.1 8.1 %collective-permute-start = (bf16[4,128,128]{2,1,0:T(8,128)(2,1)S(1)}, bf16[4,128,128]{2,1,0:T(8,128)(2,1)S(1)}, u32[]{:S(2)}, u32[]{:S(2)}) collective-permute-start(bf16[4,128,128]{2,1,0:T(8,128)(2,1)S(1)} %fusion.89), channel_id=1, source_target_pairs={{0,8},{8,16},{16,24},{24,32},{32,40},{40,48},{48,56},{56,64},{64,7... | collective-permute-start | bytes 393224 | tf_op jit(solution)/shard_map/while/body/eval_jaxpr/ppermute | solution.py:16
  302.7 8.1 %collective-permute-start = (bf16[4,128,128]{2,1,0:T(8,128)(2,1)S(1)}, bf16[4,128,128]{2,1,0:T(8,128)(2,1)S(1)}, u32[]{:S(2)}, u32[]{:S(2)}) collective-permute-start(bf16[4,128,128]{2,1,0:T(8,128)(2,1)S(1)} %fusion.89), channel_id=1, source_target_pairs={{0,8},{8,16},{16,24},{24,32},{32,40},{40,48},{48,56},{56,64},{64,7... | collective-permute-start | bytes 393224 | tf_op jit(solution)/shard_map/while/body/eval_jaxpr/ppermute | solution.py:16
  311.3 8.1 %collective-permute-start = (bf16[4,128,128]{2,1,0:T(8,128)(2,1)S(1)}, bf16[4,128,128]{2,1,0:T(8,128)(2,1)S(1)}, u32[]{:S(2)}, u32[]{:S(2)}) collective-permute-start(bf16[4,128,128]{2,1,0:T(8,128)(2,1)S(1)} %fusion.89), channel_id=1, source_target_pairs={{0,8},{8,16},{16,24},{24,32},{32,40},{40,48},{48,56},{56,64},{64,7... | collective-permute-start | bytes 393224 | tf_op jit(solution)/shard_map/while/body/eval_jaxpr/ppermute | solution.py:16
  319.8 8.1 %collective-permute-start = (bf16[4,128,128]{2,1,0:T(8,128)(2,1)S(1)}, bf16[4,128,128]{2,1,0:T(8,128)(2,1)S(1)}, u32[]{:S(2)}, u32[]{:S(2)}) collective-permute-start(bf16[4,128,128]{2,1,0:T(8,128)(2,1)S(1)} %fusion.89), channel_id=1, source_target_pairs={{0,8},{8,16},{16,24},{24,32},{32,40},{40,48},{48,56},{56,64},{64,7... | collective-permute-start | bytes 393224 | tf_op jit(solution)/shard_map/while/body/eval_jaxpr/ppermute | solution.py:16
  328.4 8.4 %collective-permute-start = (bf16[4,128,128]{2,1,0:T(8,128)(2,1)S(1)}, bf16[4,128,128]{2,1,0:T(8,128)(2,1)S(1)}, u32[]{:S(2)}, u32[]{:S(2)}) collective-permute-start(bf16[4,128,128]{2,1,0:T(8,128)(2,1)S(1)} %fusion.89), channel_id=1, source_target_pairs={{0,8},{8,16},{16,24},{24,32},{32,40},{40,48},{48,56},{56,64},{64,7... | collective-permute-start | bytes 393224 | tf_op jit(solution)/shard_map/while/body/eval_jaxpr/ppermute | solution.py:16
  345.8 3.3 copy-start.6
  345.8 3.3 copy-start.7
  345.8 4.4 %copy-start.3 = (f32[4,4,64,2,128]{4,3,2,1,0:T(2,128)S(1)}, f32[4,4,64,2,128]{4,3,2,1,0:T(2,128)}, u32[]{:S(2)}) copy-start(f32[4,4,64,2,128]{4,3,2,1,0:T(2,128)} %copy-done.1) | copy-start | bytes 3145732
  345.8 4.4 %copy-start.9 = (f32[4,4,64,128]{3,2,1,0:T(8,128)S(1)}, f32[4,4,64,128]{3,2,1,0:T(8,128)}, u32[]{:S(2)}) copy-start(f32[4,4,64,128]{3,2,1,0:T(8,128)} %slice.31) | copy-start | bytes 1572868
  350.2 3.4 copy-start.21
  (5 other events, 6.6 us)
where the time goes:
time: 377 us; the launch traced here: 371 us
  other arithmetic  170 us (45%)
  starting transfers between devices  82.3 us (22%)
  matrix products  43 us (11%)
  waiting for transfers between devices  39.3 us (10%)
  local copies, waits for them, and re-layouts  19.7 us (5%)
  blocking collectives  15.3 us (4%)
    another operation x2, other arithmetic, block_parts(): lax.linalg.triangular_solve(system, right_side, left_side=True, lower=Tru...  159 us
    ppermute x15, starting transfers between devices, shifted(): lax.ppermute(value, axis, [(source, source + steps) for source in range(i...  82.3 us
    ppermute x15, waiting for transfers between devices, shifted(): lax.ppermute(value, axis, [(source, source + steps) for source in range(i...  39.3 us
    dot_general x27, matrix products, heads_product(): return jnp.einsum('hij,hjk->hik', left_maps, right_maps, precision=highest)  22.7 us
    all_to_all x1, blocking collectives, summed_on_arrival(): lax.all_to_all(parts, axis, split_axis=0, concat_axis=0, tiled=True)  15.3 us
  transfers between devices with their start and end apart: 15, of which 15 were waited for; matrix products, arithmetic and copies ran while one was open for 0% of the time, Pallas kernels for 0%

commit v1 on v0

v1 whole, which is shorter than its diff:
```python
import jax
import jax.numpy as jnp
from jax import lax
from jax.experimental import pallas as pl
from jax.experimental.pallas import tpu as pltpu
from jax.sharding import PartitionSpec as P

BLOCK = 64
MOST_LEN = 2048
epsilon = 1e-06
f32 = jnp.float32
bf16 = jnp.bfloat16


def dot_nn(left, right):
    return lax.dot_general(left, right, (((1,), (0,)), ((), ())), preferred_element_type=f32)


def dot_nt(left, right):
    return lax.dot_general(left, right, (((1,), (1,)), ((), ())), preferred_element_type=f32)


def dot_tn(left, right):
    return lax.dot_general(left, right, (((0,), (0,)), ((), ())), preferred_element_type=f32)


def halves(value):
    top = value.astype(bf16)
    return top, (value - top.astype(f32)).astype(bf16)


def square_product(left, right):
    width = right[0].shape[1]
    side = jnp.concatenate([right[0], right[1]], axis=1)
    both = dot_nn(
        jnp.concatenate([left[0], left[1]], axis=1), jnp.concatenate([side, side], axis=0)
    )
    return both[:, :width] + both[:, width:]


def iota(shape, dim):
    return lax.broadcasted_iota(jnp.int32, shape, dim)


def local_kernel(
    lengths, query, keys, values, beta, decay, reads, offsets, maps, adds, whole_map, whole_add
):
    head = pl.program_id(0)
    tokens = query.shape[1]
    width = query.shape[2]
    refl = keys.shape[2]
    steps = BLOCK * refl
    blocks = tokens // BLOCK
    first = lax.axis_index("seq") * tokens
    ends, end = [], jnp.int32(0)
    for doc in range(lengths.shape[1]):
        end = end + lengths[0, doc]
        ends.append(end)

    def start_of(position):
        start = jnp.zeros_like(position)
        for end in ends:
            start = jnp.where(end <= position, end, start)
        return start

    key_all = keys[0].reshape(tokens * refl, width)
    value_all = values[0].reshape(tokens * refl, width)
    row = iota((steps, steps), 0)
    col = iota((steps, steps), 1)
    eye = row == col
    incl = col <= row
    strict = col < row
    unit = jnp.where(eye, 1.0, 0.0).astype(f32)
    step_col = iota((steps, 1), 0)
    token_col = step_col // refl
    refl_col = step_col % refl
    token_lane = iota((steps, BLOCK), 1)
    read_col = iota((BLOCK, 1), 0)
    read_lane = iota((BLOCK, BLOCK), 1)
    read_step = iota((BLOCK, steps), 1)

    def to_row(column):
        return jnp.sum(jnp.where(eye, column, 0.0), axis=0, keepdims=True)

    gate_all = decay[pl.ds(head, 1), :]
    beta_all = [beta[j, pl.ds(head, 1), :] for j in range(refl)]
    chains = []
    for block in range(blocks):
        at = block * BLOCK
        begin = first + at
        key = key_all[at * refl : at * refl + steps]
        gate = gate_all[:, at : at + BLOCK]
        cum = jnp.sum(jnp.where(token_lane <= token_col, gate, 0.0), axis=1, keepdims=True)
        beta_here = beta_all[refl - 1][:, at : at + BLOCK]
        for j in range(refl - 1):
            beta_here = jnp.where(refl_col == j, beta_all[j][:, at : at + BLOCK], beta_here)
        strength = jnp.sum(
            jnp.where(token_lane == token_col, beta_here, 0.0), axis=1, keepdims=True
        )
        start = start_of(begin + token_col)
        gram = dot_nt(key, key)
        diagonal = jnp.where(eye, gram, 0.0)
        scale = lax.rsqrt(jnp.sum(diagonal, axis=1, keepdims=True) + epsilon)
        scale_row = lax.rsqrt(jnp.sum(diagonal, axis=0, keepdims=True) + epsilon)
        carry = jnp.where(start < begin, jnp.exp(cum), 0.0)
        cum_row = to_row(cum)
        ratio = jnp.where(
            strict & (begin + col // refl >= start),
            jnp.exp(jnp.minimum(cum - cum_row, 0.0)),
            0.0,
        )
        system = (strength * scale) * ratio * gram * scale_row
        chains.append(
            dict(
                at=at,
                begin=begin,
                key=key,
                gate=gate,
                cum=cum,
                cum_row=cum_row,
                strength=strength,
                scale=scale,
                scale_row=scale_row,
                carry=carry,
                system=halves(system),
                inverse=unit - jnp.where((row ^ col) == 1, system, 0.0),
            )
        )
    size = 2
    while size < steps:
        mask = ((row // size) ^ (col // size)) == 1
        for c in chains:
            inverse = halves(c["inverse"])
            corner = tuple(
                jnp.where(mask, part, jnp.zeros_like(part)) for part in c["system"]
            )
            moved = square_product(corner, inverse)
            c["inverse"] = c["inverse"] - square_product(inverse, halves(moved))
        size *= 2
    total = None
    for block, c in enumerate(chains):
        at, begin, key, cum = c["at"], c["begin"], c["key"], c["cum"]
        value = value_all[at * refl : at * refl + steps]
        strength_row = to_row(c["strength"])
        carry_row = to_row(c["carry"])
        value_side = jnp.concatenate(halves(c["inverse"] * strength_row), axis=1)
        key_side = jnp.concatenate(
            halves(c["inverse"] * (strength_row * carry_row * c["scale_row"])), axis=1
        )
        writes = jnp.concatenate(
            [
                dot_nn(value_side, jnp.concatenate([value, value], axis=0)),
                dot_nn(key_side, jnp.concatenate([key, key], axis=0)),
            ],
            axis=1,
        )
        last = begin + BLOCK - 1
        last_start = start_of(last)
        fade = c["scale"] * jnp.where(
            begin + token_col >= last_start,
            jnp.exp(jnp.minimum(cum[steps - 1 :, :] - cum, 0.0)),
            0.0,
        )
        faded = jnp.concatenate(halves(fade * writes), axis=0)
        summed = dot_tn(jnp.concatenate([key, key], axis=0), faded)
        block_add = summed[:, :width]
        block_map = c["carry"][steps - 1 :, :] * unit - summed[:, width:]
        query_here = query[0, at : at + BLOCK, :]
        query_f = query_here.astype(f32)
        query_scale = lax.rsqrt(
            jnp.sum(query_f * query_f, axis=1, keepdims=True) + epsilon
        ) * (width ** (-0.5))
        read_cum = jnp.sum(jnp.where(read_lane <= read_col, c["gate"], 0.0), axis=1, keepdims=True)
        read_start = start_of(begin + read_col)
        read_token = read_step // refl
        weights = jnp.where(
            (read_token <= read_col) & (begin + read_token >= read_start),
            jnp.exp(jnp.minimum(read_cum - c["cum_row"], 0.0)),
            0.0,
        )
        weights = weights * dot_nt(query_here, key) * query_scale * c["scale_row"]
        writes_top = writes.astype(bf16)
        seen = dot_nn(
            jnp.concatenate(halves(weights), axis=1),
            jnp.concatenate([writes_top, writes_top], axis=0),
        )
        read_carry = jnp.where(read_start < begin, jnp.exp(read_cum), 0.0)
        offsets[0, at : at + BLOCK, :] = seen[:, :width]
        reads[0, at : at + BLOCK, :] = (
            (read_carry * query_scale) * query_f - seen[:, width:]
        ).astype(bf16)
        maps[0, block] = block_map.astype(bf16)
        adds[0, block] = block_add
        if total is None:
            total = jnp.concatenate([block_map, block_add], axis=1)
        else:
            top, low = halves(block_map)
            tall = jnp.concatenate(
                [
                    jnp.concatenate([top, top], axis=1),
                    jnp.concatenate([low, jnp.zeros_like(low)], axis=1),
                ],
                axis=0,
            )
            joined = dot_nn(tall, jnp.concatenate(halves(total), axis=0))
            joined = joined[:width] + joined[width:]
            total = jnp.concatenate(
                [joined[:, :width], joined[:, width:] + block_add], axis=1
            )
    whole_map[0] = total[:, :width].astype(bf16)
    whole_add[0] = total[:, width:]


def final_kernel(
    lo_state, hi_state, reads, offsets, maps, adds, gain, weight, *rest
):
    outs, normed = rest[:-1], rest[-1]
    heads, tokens, width = reads.shape
    blocks = tokens // BLOCK
    half = lo_state.shape[0]
    for head in range(heads):
        state = lo_state[head] if head < half else hi_state[head - half]
        for block in range(blocks):
            at = block * BLOCK
            out = dot_nn(reads[head, at : at + BLOCK, :], state) + offsets[head, at : at + BLOCK, :]
            out = out * lax.rsqrt(jnp.mean(out * out, axis=1, keepdims=True) + epsilon)
            normed[at : at + BLOCK, head * width : (head + 1) * width] = (
                out * gain[...]
            ).astype(bf16)
            if block + 1 < blocks:
                state = (dot_nn(maps[head, block], state) + adds[head, block]).astype(bf16)
    peers = len(outs)
    rows = tokens // peers
    me = lax.axis_index("head")
    for turn in range(peers):
        chunk = lax.rem(me + turn, peers)
        here = normed[pl.ds(chunk * rows, rows), :]
        outs[turn][...] = dot_nn(here, weight[...]).astype(bf16)


def shifted(value, axis, steps):
    count = lax.axis_size(axis)
    return lax.ppermute(value, axis, [(source, source + steps) for source in range(count - steps)])


def rotated(value, axis, steps):
    count = lax.axis_size(axis)
    return lax.ppermute(value, axis, [(source, (source + steps) % count) for source in range(count)])


def body(
    queries,
    reflect_keys,
    reflect_values,
    reflect_beta,
    log_decay,
    prompt_lengths,
    norm_gain,
    out_weight,
):
    tokens = queries.shape[1]
    refl = reflect_keys.shape[2]
    heads = reflect_beta.shape[3]
    width = queries.shape[2] // heads
    blocks = tokens // BLOCK
    beta = reflect_beta[0].transpose(1, 2, 0)
    decay = log_decay[0].transpose(1, 0)
    rows_spec = pl.BlockSpec((1, tokens, width), lambda h: (h, 0, 0))
    square_spec = pl.BlockSpec((1, blocks, width, width), lambda h: (h, 0, 0, 0))
    whole_spec = pl.BlockSpec((1, width, width), lambda h: (h, 0, 0))
    reads, offsets, maps, adds, whole_map, whole_add = pl.pallas_call(
        local_kernel,
        grid=(heads,),
        in_specs=[
            pl.BlockSpec(memory_space=pltpu.SMEM),
            pl.BlockSpec((1, tokens, width), lambda h: (0, 0, h)),
            pl.BlockSpec((1, tokens, refl, width), lambda h: (0, 0, 0, h)),
            pl.BlockSpec((1, tokens, refl, width), lambda h: (0, 0, 0, h)),
            pl.BlockSpec((refl, heads, tokens), lambda h: (0, 0, 0)),
            pl.BlockSpec((heads, tokens), lambda h: (0, 0)),
        ],
        out_specs=[rows_spec, rows_spec, square_spec, square_spec, whole_spec, whole_spec],
        out_shape=[
            jax.ShapeDtypeStruct((heads, tokens, width), bf16),
            jax.ShapeDtypeStruct((heads, tokens, width), f32),
            jax.ShapeDtypeStruct((heads, blocks, width, width), bf16),
            jax.ShapeDtypeStruct((heads, blocks, width, width), f32),
            jax.ShapeDtypeStruct((heads, width, width), bf16),
            jax.ShapeDtypeStruct((heads, width, width), f32),
        ],
        name="local_blocks",
    )(prompt_lengths, queries, reflect_keys, reflect_values, beta, decay)

    hops = min(lax.axis_size("seq") - 1, -(-(MOST_LEN - 1) // tokens))
    half = heads // 2
    parts = [slice(0, half), slice(half, heads)]
    part_maps = [whole_map[p] for p in parts]
    part_adds = [whole_add[p] for p in parts]
    states = [shifted(add.astype(bf16), "seq", 1) for add in part_adds]
    for hop in range(hops - 1):
        sent = [
            (
                jnp.einsum("hij,hjk->hik", m, s, preferred_element_type=f32) + a
            ).astype(bf16)
            for m, s, a in zip(part_maps, states, part_adds)
        ]
        states = [shifted(value, "seq", 1) for value in sent]

    peers = lax.axis_size("head")
    rows = tokens // peers
    pieces = pl.pallas_call(
        final_kernel,
        out_shape=[jax.ShapeDtypeStruct((rows, out_weight.shape[1]), bf16)] * peers,
        scratch_shapes=[pltpu.VMEM((tokens, heads * width), bf16)],
        name="read_and_project",
    )(states[0], states[1], reads, offsets, maps, adds, norm_gain[None], out_weight)
    total = pieces[0].astype(f32)
    for turn in range(1, peers):
        total = total + rotated(pieces[turn], "head", turn).astype(f32)
    return total.astype(bf16)[None]


def solution(mesh):
    in_specs = (
        P(("parts", "rep"), "seq", "head"),
        P(("parts", "rep"), "seq", None, "head"),
        P(("parts", "rep"), "seq", None, "head"),
        P(("parts", "rep"), "seq", None, "head"),
        P(("parts", "rep"), "seq", "head"),
        P(("parts", "rep"), None),
        P(),
        P("head", None),
    )
    out_specs = P(("parts", "rep"), ("seq", "head"), None)
    return jax.shard_map(body, mesh=mesh, in_specs=in_specs, out_specs=out_specs, check_vma=False)
```

time: 377 us -> 121 us (0.32); the launches traced: 371 us -> 120 us
  other arithmetic: 170 us -> 1.79 us
  matrix products: 43 us -> 6.92 us
  waiting for transfers between devices: 39.3 us -> 7.97 us
  Pallas kernels: 0 us -> 24.4 us
  local copies, waits for them, and re-layouts: 19.7 us -> 1.66 us
  blocking collectives: 15.3 us -> 0 us
  starting transfers between devices: 82.3 us -> 76.7 us
    another operation x5 -> x0, other arithmetic: 161 us -> none  [the longest x2 159 us: block_parts(): lax.linalg.triangular_solve(system, right_side, left_side=True, lower=Tru...]
    dot_general x35 -> x14, matrix products: 41 us -> 6.92 us  [body(): jnp.einsum('hij,hjk->hik', m, s, preferred_element_type=f32) + a]
    ppermute x15 -> x19, waiting for transfers between devices: 39.3 us -> 7.97 us  [the longest x3 6.07 us: rotated(): lax.ppermute(value, axis, [(source, (source + steps) % count) for source...]
    pallas_call x0 -> x2, Pallas kernels: none -> 24.4 us  [the longest x1 17.8 us: body(): pl.pallas_call(local_kernel, grid=(heads,), in_specs=[pl.BlockSpec(memory...]
    all_to_all x1 -> x0, blocking collectives: 15.3 us -> none  [summed_on_arrival(): lax.all_to_all(parts, axis, split_axis=0, concat_axis=0, tiled=True)]
    ppermute x15 -> x19, starting transfers between devices: 82.3 us -> 76.7 us  [the longest x16 70.7 us: shifted(): lax.ppermute(value, axis, [(source, source + steps) for source in range(c...]
    slice x5 -> x1, local copies, waits for them, and re-layouts: 4.9 us -> 1.04 us  [body(): part_adds = [whole_add[p] for p in parts]]
  transfers between devices with their start and end apart: 15 -> 19, of which waited for: 15 -> 3; matrix products, arithmetic and copies ran while one was open for 0% -> 6% of each run, Pallas kernels for 0% -> 0%
where the time goes in v1:
time: 121 us; the launch traced here: 120 us
  starting transfers between devices  76.7 us (63%)
  Pallas kernels  24.4 us (20%)
  waiting for transfers between devices  7.97 us (7%)
  matrix products  6.92 us (6%)
  other arithmetic  1.79 us (1%)
  local copies, waits for them, and re-layouts  1.66 us (1%)
    ppermute x16, starting transfers between devices, shifted(): lax.ppermute(value, axis, [(source, source + steps) for source in range(c...  70.7 us
    pallas_call x1, Pallas kernels, body(): pl.pallas_call(local_kernel, grid=(heads,), in_specs=[pl.BlockSpec(memory...  17.8 us
    dot_general x14, matrix products, body(): jnp.einsum('hij,hjk->hik', m, s, preferred_element_type=f32) + a  6.92 us
    pallas_call x1, Pallas kernels, body(): pl.pallas_call(final_kernel, out_shape=[jax.ShapeDtypeStruct((rows, out_w...  6.53 us
    ppermute x3, waiting for transfers between devices, rotated(): lax.ppermute(value, axis, [(source, (source + steps) % count) for source...  6.07 us
    ppermute x3, starting transfers between devices, rotated(): lax.ppermute(value, axis, [(source, (source + steps) % count) for source...  5.93 us
  transfers between devices with their start and end apart: 19, of which 3 were waited for; matrix products, arithmetic and copies ran while one was open for 6% of the time, Pallas kernels for 0%

profile of v1, /device:TPU:40, one launch (start us, length us, event | category | flops | bytes accessed | tf_op | source)
XLA Modules:
  0.0 119.7 jit_solution(9540474248303644667)
XLA Ops:
  0.0 17.8 %local_blocks.1 = (bf16[4,256,128]{2,1,0:T(8,128)(2,1)}, f32[4,256,128]{2,1,0:T(8,128)}, bf16[4,4,128,128]{3,2,1,0:T(8,128)(2,1)}, f32[4,4,128,128]{3,2,1,0:T(8,...) custom-call(s32[1,6]{1,0:T(1,128)} %lengths.1, bf16[1,256,512]{2,1,0:T(8,128)(2,1)} %query.1, ...), custom_call_target="tpu_custom_call" | custom-call | tf_op jit(solution)/shard_map/local_blocks/pallas_call | solution.py:271
  17.9 1.0 fusion.15
  18.9 4.7 %collective-permute-start.8 = (bf16[2,128,128]{2,1,0:T(8,128)(2,1)S(1)}, bf16[2,128,128]{2,1,0:T(8,128)(2,1)S(1)}, u32[]{:S(2)}, u32[]{:S(2)}) collective-permute-start(bf16[2,128,128]{2,1,0:T(8,128)(2,1)S(1)} %get-tuple-element.25), channel_id=1, source_target_pairs={{0,8},{8,16},{16,24},{24,32},{32,40},{40,48},{48,56},{56,64},{64,7... | collective-permute-start | bytes 196616 | tf_op jit(solution)/shard_map/ppermute | solution.py:243
  23.6 4.7 %collective-permute-start = (bf16[2,128,128]{2,1,0:T(8,128)(2,1)S(1)}, bf16[2,128,128]{2,1,0:T(8,128)(2,1)S(1)}, u32[]{:S(2)}, u32[]{:S(2)}) collective-permute-start(bf16[2,128,128]{2,1,0:T(8,128)(2,1)S(1)} %get-tuple-element.26), channel_id=1, source_target_pairs={{0,8},{8,16},{16,24},{24,32},{32,40},{40,48},{48,56},{56,64},{64,7... | collective-permute-start | bytes 196616 | tf_op jit(solution)/shard_map/ppermute | solution.py:243
  28.4 1.1 fusion.7
  29.5 4.7 %collective-permute-start.9 = (bf16[2,128,128]{2,1,0:T(8,128)(2,1)S(1)}, bf16[2,128,128]{2,1,0:T(8,128)(2,1)S(1)}, u32[]{:S(2)}, u32[]{:S(2)}) collective-permute-start(bf16[2,128,128]{2,1,0:T(8,128)(2,1)S(1)} %fusion.7), channel_id=1, source_target_pairs={{0,8},{8,16},{16,24},{24,32},{32,40},{40,48},{48,56},{56,64},{64,7... | collective-permute-start | bytes 196616 | tf_op jit(solution)/shard_map/ppermute | solution.py:243
  34.2 1.1 fusion
  35.3 5.9 %collective-permute-start.1 = (bf16[2,128,128]{2,1,0:T(8,128)(2,1)S(1)}, bf16[2,128,128]{2,1,0:T(8,128)(2,1)S(1)}, u32[]{:S(2)}, u32[]{:S(2)}) collective-permute-start(bf16[2,128,128]{2,1,0:T(8,128)(2,1)S(1)} %fusion), channel_id=1, source_target_pairs={{0,8},{8,16},{16,24},{24,32},{32,40},{40,48},{48,56},{56,64},{64,7... | collective-permute-start | bytes 196616 | tf_op jit(solution)/shard_map/ppermute | solution.py:243
  41.2 1.1 fusion.8
  42.3 4.7 %collective-permute-start.10 = (bf16[2,128,128]{2,1,0:T(8,128)(2,1)S(1)}, bf16[2,128,128]{2,1,0:T(8,128)(2,1)S(1)}, u32[]{:S(2)}, u32[]{:S(2)}) collective-permute-start(bf16[2,128,128]{2,1,0:T(8,128)(2,1)S(1)} %fusion.8), channel_id=1, source_target_pairs={{0,8},{8,16},{16,24},{24,32},{32,40},{40,48},{48,56},{56,64},{64,7... | collective-permute-start | bytes 196616 | tf_op jit(solution)/shard_map/ppermute | solution.py:243
  47.1 1.1 fusion.1
  48.2 4.7 %collective-permute-start.2 = (bf16[2,128,128]{2,1,0:T(8,128)(2,1)S(1)}, bf16[2,128,128]{2,1,0:T(8,128)(2,1)S(1)}, u32[]{:S(2)}, u32[]{:S(2)}) collective-permute-start(bf16[2,128,128]{2,1,0:T(8,128)(2,1)S(1)} %fusion.1), channel_id=1, source_target_pairs={{0,8},{8,16},{16,24},{24,32},{32,40},{40,48},{48,56},{56,64},{64,7... | collective-permute-start | bytes 196616 | tf_op jit(solution)/shard_map/ppermute | solution.py:243
  52.9 1.1 fusion.9
  54.0 4.7 %collective-permute-start.11 = (bf16[2,128,128]{2,1,0:T(8,128)(2,1)S(1)}, bf16[2,128,128]{2,1,0:T(8,128)(2,1)S(1)}, u32[]{:S(2)}, u32[]{:S(2)}) collective-permute-start(bf16[2,128,128]{2,1,0:T(8,128)(2,1)S(1)} %fusion.9), channel_id=1, source_target_pairs={{0,8},{8,16},{16,24},{24,32},{32,40},{40,48},{48,56},{56,64},{64,7... | collective-permute-start | bytes 196616 | tf_op jit(solution)/shard_map/ppermute | solution.py:243
  58.9 5.9 %collective-permute-start.3 = (bf16[2,128,128]{2,1,0:T(8,128)(2,1)S(1)}, bf16[2,128,128]{2,1,0:T(8,128)(2,1)S(1)}, u32[]{:S(2)}, u32[]{:S(2)}) collective-permute-start(bf16[2,128,128]{2,1,0:T(8,128)(2,1)S(1)} %fusion.2), channel_id=1, source_target_pairs={{0,8},{8,16},{16,24},{24,32},{32,40},{40,48},{48,56},{56,64},{64,7... | collective-permute-start | bytes 196616 | tf_op jit(solution)/shard_map/ppermute | solution.py:243
  65.0 3.8 %collective-permute-start.12 = (bf16[2,128,128]{2,1,0:T(8,128)(2,1)S(1)}, bf16[2,128,128]{2,1,0:T(8,128)(2,1)S(1)}, u32[]{:S(2)}, u32[]{:S(2)}) collective-permute-start(bf16[2,128,128]{2,1,0:T(8,128)(2,1)S(1)} %fusion.10), channel_id=1, source_target_pairs={{0,8},{8,16},{16,24},{24,32},{32,40},{40,48},{48,56},{56,64},{64,7... | collective-permute-start | bytes 196616 | tf_op jit(solution)/shard_map/ppermute | solution.py:243
  69.0 3.8 %collective-permute-start.4 = (bf16[2,128,128]{2,1,0:T(8,128)(2,1)S(1)}, bf16[2,128,128]{2,1,0:T(8,128)(2,1)S(1)}, u32[]{:S(2)}, u32[]{:S(2)}) collective-permute-start(bf16[2,128,128]{2,1,0:T(8,128)(2,1)S(1)} %fusion.3), channel_id=1, source_target_pairs={{0,8},{8,16},{16,24},{24,32},{32,40},{40,48},{48,56},{56,64},{64,7... | collective-permute-start | bytes 196616 | tf_op jit(solution)/shard_map/ppermute | solution.py:243
  73.0 3.8 %collective-permute-start.13 = (bf16[2,128,128]{2,1,0:T(8,128)(2,1)S(1)}, bf16[2,128,128]{2,1,0:T(8,128)(2,1)S(1)}, u32[]{:S(2)}, u32[]{:S(2)}) collective-permute-start(bf16[2,128,128]{2,1,0:T(8,128)(2,1)S(1)} %fusion.11), channel_id=1, source_target_pairs={{0,8},{8,16},{16,24},{24,32},{32,40},{40,48},{48,56},{56,64},{64,7... | collective-permute-start | bytes 196616 | tf_op jit(solution)/shard_map/ppermute | solution.py:243
  77.0 3.8 %collective-permute-start.5 = (bf16[2,128,128]{2,1,0:T(8,128)(2,1)S(1)}, bf16[2,128,128]{2,1,0:T(8,128)(2,1)S(1)}, u32[]{:S(2)}, u32[]{:S(2)}) collective-permute-start(bf16[2,128,128]{2,1,0:T(8,128)(2,1)S(1)} %fusion.4), channel_id=1, source_target_pairs={{0,8},{8,16},{16,24},{24,32},{32,40},{40,48},{48,56},{56,64},{64,7... | collective-permute-start | bytes 196616 | tf_op jit(solution)/shard_map/ppermute | solution.py:243
  81.0 3.8 %collective-permute-start.14 = (bf16[2,128,128]{2,1,0:T(8,128)(2,1)S(1)}, bf16[2,128,128]{2,1,0:T(8,128)(2,1)S(1)}, u32[]{:S(2)}, u32[]{:S(2)}) collective-permute-start(bf16[2,128,128]{2,1,0:T(8,128)(2,1)S(1)} %fusion.12), channel_id=1, source_target_pairs={{0,8},{8,16},{16,24},{24,32},{32,40},{40,48},{48,56},{56,64},{64,7... | collective-permute-start | bytes 196616 | tf_op jit(solution)/shard_map/ppermute | solution.py:243
  84.9 3.8 %collective-permute-start.6 = (bf16[2,128,128]{2,1,0:T(8,128)(2,1)S(1)}, bf16[2,128,128]{2,1,0:T(8,128)(2,1)S(1)}, u32[]{:S(2)}, u32[]{:S(2)}) collective-permute-start(bf16[2,128,128]{2,1,0:T(8,128)(2,1)S(1)} %fusion.5), channel_id=1, source_target_pairs={{0,8},{8,16},{16,24},{24,32},{32,40},{40,48},{48,56},{56,64},{64,7... | collective-permute-start | bytes 196616 | tf_op jit(solution)/shard_map/ppermute | solution.py:243
  88.9 4.0 %collective-permute-start.15 = (bf16[2,128,128]{2,1,0:T(8,128)(2,1)S(1)}, bf16[2,128,128]{2,1,0:T(8,128)(2,1)S(1)}, u32[]{:S(2)}, u32[]{:S(2)}) collective-permute-start(bf16[2,128,128]{2,1,0:T(8,128)(2,1)S(1)} %fusion.13), channel_id=1, source_target_pairs={{0,8},{8,16},{16,24},{24,32},{32,40},{40,48},{48,56},{56,64},{64,7... | collective-permute-start | bytes 196616 | tf_op jit(solution)/shard_map/ppermute | solution.py:243
  93.1 3.8 %collective-permute-start.7 = (bf16[2,128,128]{2,1,0:T(8,128)(2,1)S(1)}, bf16[2,128,128]{2,1,0:T(8,128)(2,1)S(1)}, u32[]{:S(2)}, u32[]{:S(2)}) collective-permute-start(bf16[2,128,128]{2,1,0:T(8,128)(2,1)S(1)} %fusion.6), channel_id=1, source_target_pairs={{0,8},{8,16},{16,24},{24,32},{32,40},{40,48},{48,56},{56,64},{64,7... | collective-permute-start | bytes 196616 | tf_op jit(solution)/shard_map/ppermute | solution.py:243
  96.9 1.9 %collective-permute-done.7.lo_state = bf16[2,128,128]{2,1,0:T(8,128)(2,1)S(1)} collective-permute-done((bf16[2,128,128]{2,1,0:T(8,128)(2,1)S(1)}, bf16[2,128,128]{2,1,0:T(8,128)(2,1)S(1)}, u32[]{:S(2)}, u32[]{:S(2)}) %collective-permute-start.7) | collective-permute-done | bytes 65568 | tf_op jit(solution)/shard_map/ppermute | solution.py:243
  98.7 0.6 copy-done.3
  99.4 6.5 %read_and_project.1 = (bf16[64,2048]{1,0:T(8,128)(2,1)}, bf16[64,2048]{1,0:T(8,128)(2,1)}, bf16[64,2048]{1,0:T(8,128)(2,1)}, bf16[64,2048]{1,0:T(8,128)(2,1)}) custom-call(bf16[2,128,128]{2,1,0:T(8,128)(2,1)} %copy-done.3, bf16[2,128,128]{2,1,0:T(8,128)(2,1)} %copy-done.2, bf16[4,256,128]{2,1,0:T(8,128)(2,1)} %get-tuple-element.17.reads, ...), custom_call_target="tpu_custom_call" | custom-call | tf_op jit(solution)/shard_map/read_and_project/pallas_call | solution.py:311
  105.9 1.6 %collective-permute-start.16 = (bf16[64,2048]{1,0:T(8,128)(2,1)}, bf16[64,2048]{1,0:T(8,128)(2,1)S(1)}, u32[]{:S(2)}, u32[]{:S(2)}) collective-permute-start(bf16[64,2048]{1,0:T(8,128)(2,1)} %get-tuple-element.22), channel_id=1, source_target_pairs={{0,2},{2,4},{4,6},{6,0},{1,3},{3,5},{5,7},{7,1},{8,10},{10,12},{12... | collective-permute-start | bytes 786440 | tf_op jit(solution)/shard_map/ppermute | solution.py:248
  107.5 3.0 %collective-permute-start.17 = (bf16[64,2048]{1,0:T(8,128)(2,1)}, bf16[64,2048]{1,0:T(8,128)(2,1)S(1)}, u32[]{:S(2)}, u32[]{:S(2)}) collective-permute-start(bf16[64,2048]{1,0:T(8,128)(2,1)} %get-tuple-element.23), channel_id=1, source_target_pairs={{0,4},{2,6},{4,0},{6,2},{1,5},{3,7},{5,1},{7,3},{8,12},{10,14},{12... | collective-permute-start | bytes 786440 | tf_op jit(solution)/shard_map/ppermute | solution.py:248
  110.5 1.3 %collective-permute-start.18 = (bf16[64,2048]{1,0:T(8,128)(2,1)}, bf16[64,2048]{1,0:T(8,128)(2,1)S(1)}, u32[]{:S(2)}, u32[]{:S(2)}) collective-permute-start(bf16[64,2048]{1,0:T(8,128)(2,1)} %get-tuple-element.24), channel_id=1, source_target_pairs={{0,6},{2,0},{4,2},{6,4},{1,7},{3,1},{5,3},{7,5},{8,14},{10,8},{12,... | collective-permute-start | bytes 786440 | tf_op jit(solution)/shard_map/ppermute | solution.py:248
  111.8 2.4 %collective-permute-done.16 = bf16[64,2048]{1,0:T(8,128)(2,1)S(1)} collective-permute-done((bf16[64,2048]{1,0:T(8,128)(2,1)}, bf16[64,2048]{1,0:T(8,128)(2,1)S(1)}, u32[]{:S(2)}, u32[]{:S(2)}) %collective-permute-start.16) | collective-permute-done | bytes 262176 | tf_op jit(solution)/shard_map/ppermute | solution.py:248
  114.2 3.7 %collective-permute-done.17 = bf16[64,2048]{1,0:T(8,128)(2,1)S(1)} collective-permute-done((bf16[64,2048]{1,0:T(8,128)(2,1)}, bf16[64,2048]{1,0:T(8,128)(2,1)S(1)}, u32[]{:S(2)}, u32[]{:S(2)}) %collective-permute-start.17) | collective-permute-done | bytes 262176 | tf_op jit(solution)/shard_map/ppermute | solution.py:248
  117.9 1.8 %fusion.14 = bf16[1,64,2048]{2,1,0:T(8,128)(2,1)} fusion(bf16[64,2048]{1,0:T(8,128)(2,1)S(1)} %collective-permute-done.18, bf16[64,2048]{1,0:T(8,128)(2,1)S(1)} %collective-permute-done.17, bf16[64,2048]{1,0:T(8,128)(2,1)S(1)} %collective-permute-done.16, bf16[64,2048]{1,0:T(8,128)(2,1)} %get-tuple-element.21), kind=kLoop, calls=%fused_computation.29 | loop fusion | flops 1048576 | bytes 1310720 | tf_op jit(solution)/shard_map/broadcast_in_dim | solution.py:320
  (32 shorter events, 1.5 us)
Async XLA Ops:
  17.8 40.9 %copy-start = (bf16[4,128,128]{2,1,0:T(8,128)(2,1)S(1)}, bf16[4,128,128]{2,1,0:T(8,128)(2,1)}, u32[]{:S(2)}) copy-start(bf16[4,128,128]{2,1,0:T(8,128)(2,1)} %get-tuple-element.15) | copy-start | bytes 393220
  17.9 40.9 %copy-start.1 = (f32[4,128,128]{2,1,0:T(8,128)S(1)}, f32[4,128,128]{2,1,0:T(8,128)}, u32[]{:S(2)}) copy-start(f32[4,128,128]{2,1,0:T(8,128)} %get-tuple-element.16) | copy-start | bytes 786436
  18.9 9.4 %collective-permute-start.8 = (bf16[2,128,128]{2,1,0:T(8,128)(2,1)S(1)}, bf16[2,128,128]{2,1,0:T(8,128)(2,1)S(1)}, u32[]{:S(2)}, u32[]{:S(2)}) collective-permute-start(bf16[2,128,128]{2,1,0:T(8,128)(2,1)S(1)} %get-tuple-element.25), channel_id=1, source_target_pairs={{0,8},{8,16},{16,24},{24,32},{32,40},{40,48},{48,56},{56,64},{64,7... | collective-permute-start | bytes 196616 | tf_op jit(solution)/shard_map/ppermute | solution.py:243
  23.6 10.6 %collective-permute-start = (bf16[2,128,128]{2,1,0:T(8,128)(2,1)S(1)}, bf16[2,128,128]{2,1,0:T(8,128)(2,1)S(1)}, u32[]{:S(2)}, u32[]{:S(2)}) collective-permute-start(bf16[2,128,128]{2,1,0:T(8,128)(2,1)S(1)} %get-tuple-element.26), channel_id=1, source_target_pairs={{0,8},{8,16},{16,24},{24,32},{32,40},{40,48},{48,56},{56,64},{64,7... | collective-permute-start | bytes 196616 | tf_op jit(solution)/shard_map/ppermute | solution.py:243
  29.5 11.8 %collective-permute-start.9 = (bf16[2,128,128]{2,1,0:T(8,128)(2,1)S(1)}, bf16[2,128,128]{2,1,0:T(8,128)(2,1)S(1)}, u32[]{:S(2)}, u32[]{:S(2)}) collective-permute-start(bf16[2,128,128]{2,1,0:T(8,128)(2,1)S(1)} %fusion.7), channel_id=1, source_target_pairs={{0,8},{8,16},{16,24},{24,32},{32,40},{40,48},{48,56},{56,64},{64,7... | collective-permute-start | bytes 196616 | tf_op jit(solution)/shard_map/ppermute | solution.py:243
  35.3 11.8 %collective-permute-start.1 = (bf16[2,128,128]{2,1,0:T(8,128)(2,1)S(1)}, bf16[2,128,128]{2,1,0:T(8,128)(2,1)S(1)}, u32[]{:S(2)}, u32[]{:S(2)}) collective-permute-start(bf16[2,128,128]{2,1,0:T(8,128)(2,1)S(1)} %fusion), channel_id=1, source_target_pairs={{0,8},{8,16},{16,24},{24,32},{32,40},{40,48},{48,56},{56,64},{64,7... | collective-permute-start | bytes 196616 | tf_op jit(solution)/shard_map/ppermute | solution.py:243
  42.3 10.5 %collective-permute-start.10 = (bf16[2,128,128]{2,1,0:T(8,128)(2,1)S(1)}, bf16[2,128,128]{2,1,0:T(8,128)(2,1)S(1)}, u32[]{:S(2)}, u32[]{:S(2)}) collective-permute-start(bf16[2,128,128]{2,1,0:T(8,128)(2,1)S(1)} %fusion.8), channel_id=1, source_target_pairs={{0,8},{8,16},{16,24},{24,32},{32,40},{40,48},{48,56},{56,64},{64,7... | collective-permute-start | bytes 196616 | tf_op jit(solution)/shard_map/ppermute | solution.py:243
  48.2 10.6 %collective-permute-start.2 = (bf16[2,128,128]{2,1,0:T(8,128)(2,1)S(1)}, bf16[2,128,128]{2,1,0:T(8,128)(2,1)S(1)}, u32[]{:S(2)}, u32[]{:S(2)}) collective-permute-start(bf16[2,128,128]{2,1,0:T(8,128)(2,1)S(1)} %fusion.1), channel_id=1, source_target_pairs={{0,8},{8,16},{16,24},{24,32},{32,40},{40,48},{48,56},{56,64},{64,7... | collective-permute-start | bytes 196616 | tf_op jit(solution)/shard_map/ppermute | solution.py:243
  54.0 10.8 %collective-permute-start.11 = (bf16[2,128,128]{2,1,0:T(8,128)(2,1)S(1)}, bf16[2,128,128]{2,1,0:T(8,128)(2,1)S(1)}, u32[]{:S(2)}, u32[]{:S(2)}) collective-permute-start(bf16[2,128,128]{2,1,0:T(8,128)(2,1)S(1)} %fusion.9), channel_id=1, source_target_pairs={{0,8},{8,16},{16,24},{24,32},{32,40},{40,48},{48,56},{56,64},{64,7... | collective-permute-start | bytes 196616 | tf_op jit(solution)/shard_map/ppermute | solution.py:243
  58.9 9.9 %collective-permute-start.3 = (bf16[2,128,128]{2,1,0:T(8,128)(2,1)S(1)}, bf16[2,128,128]{2,1,0:T(8,128)(2,1)S(1)}, u32[]{:S(2)}, u32[]{:S(2)}) collective-permute-start(bf16[2,128,128]{2,1,0:T(8,128)(2,1)S(1)} %fusion.2), channel_id=1, source_target_pairs={{0,8},{8,16},{16,24},{24,32},{32,40},{40,48},{48,56},{56,64},{64,7... | collective-permute-start | bytes 196616 | tf_op jit(solution)/shard_map/ppermute | solution.py:243
  65.0 7.8 %collective-permute-start.12 = (bf16[2,128,128]{2,1,0:T(8,128)(2,1)S(1)}, bf16[2,128,128]{2,1,0:T(8,128)(2,1)S(1)}, u32[]{:S(2)}, u32[]{:S(2)}) collective-permute-start(bf16[2,128,128]{2,1,0:T(8,128)(2,1)S(1)} %fusion.10), channel_id=1, source_target_pairs={{0,8},{8,16},{16,24},{24,32},{32,40},{40,48},{48,56},{56,64},{64,7... | collective-permute-start | bytes 196616 | tf_op jit(solution)/shard_map/ppermute | solution.py:243
  69.0 7.8 %collective-permute-start.4 = (bf16[2,128,128]{2,1,0:T(8,128)(2,1)S(1)}, bf16[2,128,128]{2,1,0:T(8,128)(2,1)S(1)}, u32[]{:S(2)}, u32[]{:S(2)}) collective-permute-start(bf16[2,128,128]{2,1,0:T(8,128)(2,1)S(1)} %fusion.3), channel_id=1, source_target_pairs={{0,8},{8,16},{16,24},{24,32},{32,40},{40,48},{48,56},{56,64},{64,7... | collective-permute-start | bytes 196616 | tf_op jit(solution)/shard_map/ppermute | solution.py:243
  73.0 7.8 %collective-permute-start.13 = (bf16[2,128,128]{2,1,0:T(8,128)(2,1)S(1)}, bf16[2,128,128]{2,1,0:T(8,128)(2,1)S(1)}, u32[]{:S(2)}, u32[]{:S(2)}) collective-permute-start(bf16[2,128,128]{2,1,0:T(8,128)(2,1)S(1)} %fusion.11), channel_id=1, source_target_pairs={{0,8},{8,16},{16,24},{24,32},{32,40},{40,48},{48,56},{56,64},{64,7... | collective-permute-start | bytes 196616 | tf_op jit(solution)/shard_map/ppermute | solution.py:243
  77.0 7.8 %collective-permute-start.5 = (bf16[2,128,128]{2,1,0:T(8,128)(2,1)S(1)}, bf16[2,128,128]{2,1,0:T(8,128)(2,1)S(1)}, u32[]{:S(2)}, u32[]{:S(2)}) collective-permute-start(bf16[2,128,128]{2,1,0:T(8,128)(2,1)S(1)} %fusion.4), channel_id=1, source_target_pairs={{0,8},{8,16},{16,24},{24,32},{32,40},{40,48},{48,56},{56,64},{64,7... | collective-permute-start | bytes 196616 | tf_op jit(solution)/shard_map/ppermute | solution.py:243
  81.0 7.8 %collective-permute-start.14 = (bf16[2,128,128]{2,1,0:T(8,128)(2,1)S(1)}, bf16[2,128,128]{2,1,0:T(8,128)(2,1)S(1)}, u32[]{:S(2)}, u32[]{:S(2)}) collective-permute-start(bf16[2,128,128]{2,1,0:T(8,128)(2,1)S(1)} %fusion.12), channel_id=1, source_target_pairs={{0,8},{8,16},{16,24},{24,32},{32,40},{40,48},{48,56},{56,64},{64,7... | collective-permute-start | bytes 196616 | tf_op jit(solution)/shard_map/ppermute | solution.py:243
  84.9 8.0 %collective-permute-start.6 = (bf16[2,128,128]{2,1,0:T(8,128)(2,1)S(1)}, bf16[2,128,128]{2,1,0:T(8,128)(2,1)S(1)}, u32[]{:S(2)}, u32[]{:S(2)}) collective-permute-start(bf16[2,128,128]{2,1,0:T(8,128)(2,1)S(1)} %fusion.5), channel_id=1, source_target_pairs={{0,8},{8,16},{16,24},{24,32},{32,40},{40,48},{48,56},{56,64},{64,7... | collective-permute-start | bytes 196616 | tf_op jit(solution)/shard_map/ppermute | solution.py:243
  88.9 7.9 %collective-permute-start.15 = (bf16[2,128,128]{2,1,0:T(8,128)(2,1)S(1)}, bf16[2,128,128]{2,1,0:T(8,128)(2,1)S(1)}, u32[]{:S(2)}, u32[]{:S(2)}) collective-permute-start(bf16[2,128,128]{2,1,0:T(8,128)(2,1)S(1)} %fusion.13), channel_id=1, source_target_pairs={{0,8},{8,16},{16,24},{24,32},{32,40},{40,48},{48,56},{56,64},{64,7... | collective-permute-start | bytes 196616 | tf_op jit(solution)/shard_map/ppermute | solution.py:243
  93.1 5.7 %collective-permute-start.7 = (bf16[2,128,128]{2,1,0:T(8,128)(2,1)S(1)}, bf16[2,128,128]{2,1,0:T(8,128)(2,1)S(1)}, u32[]{:S(2)}, u32[]{:S(2)}) collective-permute-start(bf16[2,128,128]{2,1,0:T(8,128)(2,1)S(1)} %fusion.6), channel_id=1, source_target_pairs={{0,8},{8,16},{16,24},{24,32},{32,40},{40,48},{48,56},{56,64},{64,7... | collective-permute-start | bytes 196616 | tf_op jit(solution)/shard_map/ppermute | solution.py:243
  96.9 1.9 %copy-start.2 = (bf16[2,128,128]{2,1,0:T(8,128)(2,1)}, bf16[2,128,128]{2,1,0:T(8,128)(2,1)S(1)}, u32[]{:S(2)}) copy-start(bf16[2,128,128]{2,1,0:T(8,128)(2,1)S(1)} %collective-permute-done.15.hi_state) | copy-start | bytes 196612
  98.7 0.6 copy-start.3
  105.9 8.3 %collective-permute-start.16 = (bf16[64,2048]{1,0:T(8,128)(2,1)}, bf16[64,2048]{1,0:T(8,128)(2,1)S(1)}, u32[]{:S(2)}, u32[]{:S(2)}) collective-permute-start(bf16[64,2048]{1,0:T(8,128)(2,1)} %get-tuple-element.22), channel_id=1, source_target_pairs={{0,2},{2,4},{4,6},{6,0},{1,3},{3,5},{5,7},{7,1},{8,10},{10,12},{12... | collective-permute-start | bytes 786440 | tf_op jit(solution)/shard_map/ppermute | solution.py:248
  107.5 10.4 %collective-permute-start.17 = (bf16[64,2048]{1,0:T(8,128)(2,1)}, bf16[64,2048]{1,0:T(8,128)(2,1)S(1)}, u32[]{:S(2)}, u32[]{:S(2)}) collective-permute-start(bf16[64,2048]{1,0:T(8,128)(2,1)} %get-tuple-element.23), channel_id=1, source_target_pairs={{0,4},{2,6},{4,0},{6,2},{1,5},{3,7},{5,1},{7,3},{8,12},{10,14},{12... | collective-permute-start | bytes 786440 | tf_op jit(solution)/shard_map/ppermute | solution.py:248
  110.5 7.4 %collective-permute-start.18 = (bf16[64,2048]{1,0:T(8,128)(2,1)}, bf16[64,2048]{1,0:T(8,128)(2,1)S(1)}, u32[]{:S(2)}, u32[]{:S(2)}) collective-permute-start(bf16[64,2048]{1,0:T(8,128)(2,1)} %get-tuple-element.24), channel_id=1, source_target_pairs={{0,6},{2,0},{4,2},{6,4},{1,7},{3,1},{5,3},{7,5},{8,14},{10,8},{12,... | collective-permute-start | bytes 786440 | tf_op jit(solution)/shard_map/ppermute | solution.py:248

commit v2 on v1

v2 whole, which is shorter than its diff:
```python
import jax
import jax.numpy as jnp
from jax import lax
from jax.experimental import pallas as pl
from jax.experimental.pallas import tpu as pltpu
from jax.sharding import PartitionSpec as P

BLOCK = 64
MOST_LEN = 2048
HEADS_PER_STEP = 2
epsilon = 1e-06
f32 = jnp.float32
bf16 = jnp.bfloat16


def dot_nn(left, right):
    return lax.dot_general(left, right, (((1,), (0,)), ((), ())), preferred_element_type=f32)


def dot_nt(left, right):
    return lax.dot_general(left, right, (((1,), (1,)), ((), ())), preferred_element_type=f32)


def dot_tn(left, right):
    return lax.dot_general(left, right, (((0,), (0,)), ((), ())), preferred_element_type=f32)


def halves(value):
    top = value.astype(bf16)
    return top, (value - top.astype(f32)).astype(bf16)


def square_product(left, right):
    width = right[0].shape[1]
    side = jnp.concatenate([right[0], right[1]], axis=1)
    both = dot_nn(
        jnp.concatenate([left[0], left[1]], axis=1), jnp.concatenate([side, side], axis=0)
    )
    return both[:, :width] + both[:, width:]


def iota(shape, dim):
    return lax.broadcasted_iota(jnp.int32, shape, dim)


def local_kernel(
    lengths, query, keys, values, beta, decay, reads, offsets, maps, adds, *rest
):
    sends = rest[:-3]
    inner_mask, read_mask, edge_mask = rest[-3:]
    turn = pl.program_id(0)
    tokens = query.shape[1]
    heads_here = reads.shape[0]
    width = reads.shape[2]
    refl = keys.shape[2]
    steps = BLOCK * refl
    blocks = tokens // BLOCK
    first = lax.axis_index("seq") * tokens
    place = lax.rem(lax.axis_index("seq"), len(sends))
    row = iota((steps, steps), 0)
    col = iota((steps, steps), 1)
    eye = row == col
    unit = jnp.where(eye, 1.0, 0.0).astype(f32)
    step_col = iota((steps, 1), 0)
    token_col = step_col // refl
    refl_col = step_col % refl
    token_lane = iota((steps, BLOCK), 1)
    token_row = iota((1, steps), 1) // refl
    read_col = iota((BLOCK, 1), 0)
    read_lane = iota((BLOCK, BLOCK), 1)
    read_step = iota((BLOCK, steps), 1)
    read_token = read_step // refl
    hidden = -1e30

    @pl.when(turn == 0)
    def _():
        ends, end = [], jnp.int32(0)
        for doc in range(lengths.shape[1]):
            end = end + lengths[0, doc]
            ends.append(end)

        def start_of(position):
            start = jnp.zeros_like(position)
            for end in ends:
                start = jnp.where(end <= position, end, start)
            return start

        for block in range(blocks):
            begin = first + block * BLOCK
            start = start_of(begin + token_col)
            inner_mask[block] = jnp.where(
                (col < row) & (begin + col // refl >= start), 0.0, hidden
            )
            read_start = start_of(begin + read_col)
            read_mask[block] = jnp.where(
                (read_token <= read_col) & (begin + read_token >= read_start), 0.0, hidden
            )
            start_row = start_of(begin + token_row)
            last_start = start_of(begin + token_row * 0 + (BLOCK - 1))
            edge_mask[block, 0:1, :] = jnp.where(start_row < begin, 0.0, hidden)
            edge_mask[block, 1:2, :] = jnp.where(begin + token_row >= last_start, 0.0, hidden)

    def to_row(column):
        return jnp.sum(jnp.where(eye, column, 0.0), axis=0, keepdims=True)

    def to_col(line):
        return jnp.sum(jnp.where(eye, line, 0.0), axis=1, keepdims=True)

    chains = []
    for local in range(heads_here):
        head = turn * heads_here + local
        lanes = slice(local * width, (local + 1) * width)
        key_all = keys[0, :, :, lanes].reshape(tokens * refl, width)
        gate_all = decay[pl.ds(head, 1), :]
        beta_all = [beta[j, pl.ds(head, 1), :] for j in range(refl)]
        for block in range(blocks):
            at = block * BLOCK
            key = key_all[at * refl : at * refl + steps]
            gate = gate_all[:, at : at + BLOCK]
            cum = jnp.sum(jnp.where(token_lane <= token_col, gate, 0.0), axis=1, keepdims=True)
            beta_here = beta_all[refl - 1][:, at : at + BLOCK]
            for j in range(refl - 1):
                beta_here = jnp.where(refl_col == j, beta_all[j][:, at : at + BLOCK], beta_here)
            strength = jnp.sum(
                jnp.where(token_lane == token_col, beta_here, 0.0), axis=1, keepdims=True
            )
            gram = dot_nt(key, key)
            diagonal = jnp.where(eye, gram, 0.0)
            scale = lax.rsqrt(jnp.sum(diagonal, axis=1, keepdims=True) + epsilon)
            scale_row = lax.rsqrt(jnp.sum(diagonal, axis=0, keepdims=True) + epsilon)
            cum_row = to_row(cum)
            ratio = jnp.exp(jnp.minimum(cum - cum_row, inner_mask[block]))
            system = (strength * scale) * ratio * gram * scale_row
            chains.append(
                dict(
                    local=local,
                    block=block,
                    lanes=lanes,
                    key=key,
                    gate=gate,
                    cum_row=cum_row,
                    strength=strength,
                    scale_row=scale_row,
                    system=halves(system),
                    inverse=unit - jnp.where((row ^ col) == 1, system, 0.0),
                )
            )
    size = 2
    while size < steps:
        mask = ((row // size) ^ (col // size)) == 1
        for c in chains:
            inverse = halves(c["inverse"])
            corner = tuple(jnp.where(mask, part, jnp.zeros_like(part)) for part in c["system"])
            moved = square_product(corner, inverse)
            c["inverse"] = c["inverse"] - square_product(inverse, halves(moved))
        size *= 2
    totals = [None] * heads_here
    for c in chains:
        local, block, key = c["local"], c["block"], c["key"]
        at = block * BLOCK
        value = values[0, at : at + BLOCK, :, c["lanes"]].reshape(steps, width)
        strength_row = to_row(c["strength"])
        cum_row, scale_row = c["cum_row"], c["scale_row"]
        carry_row = jnp.exp(jnp.minimum(cum_row, edge_mask[block, 0:1, :]))
        value_side = jnp.concatenate(halves(c["inverse"] * strength_row), axis=1)
        key_side = jnp.concatenate(
            halves(c["inverse"] * (strength_row * carry_row * scale_row)), axis=1
        )
        writes = jnp.concatenate(
            [
                dot_nn(value_side, jnp.concatenate([value, value], axis=0)),
                dot_nn(key_side, jnp.concatenate([key, key], axis=0)),
            ],
            axis=1,
        )
        fade_row = scale_row * jnp.exp(
            jnp.minimum(cum_row[:, steps - 1 :] - cum_row, edge_mask[block, 1:2, :])
        )
        faded = jnp.concatenate(halves(to_col(fade_row) * writes), axis=0)
        summed = dot_tn(jnp.concatenate([key, key], axis=0), faded)
        block_add = summed[:, :width]
        block_map = carry_row[:, steps - 1 :] * unit - summed[:, width:]
        query_here = query[0, at : at + BLOCK, c["lanes"]]
        query_f = query_here.astype(f32)
        query_scale = lax.rsqrt(
            jnp.sum(query_f * query_f, axis=1, keepdims=True) + epsilon
        ) * (width ** (-0.5))
        read_cum = jnp.sum(
            jnp.where(read_lane <= read_col, c["gate"], 0.0), axis=1, keepdims=True
        )
        weights = jnp.exp(jnp.minimum(read_cum - cum_row, read_mask[block]))
        weights = weights * dot_nt(query_here, key) * query_scale * scale_row
        writes_top = writes.astype(bf16)
        seen = dot_nn(
            jnp.concatenate(halves(weights), axis=1),
            jnp.concatenate([writes_top, writes_top], axis=0),
        )
        read_carry = jnp.sum(
            jnp.where(read_step == read_col * refl, carry_row, 0.0), axis=1, keepdims=True
        )
        offsets[local, at : at + BLOCK, :] = seen[:, :width]
        reads[local, at : at + BLOCK, :] = (
            (read_carry * query_scale) * query_f - seen[:, width:]
        ).astype(bf16)
        maps[local, block] = block_map.astype(bf16)
        adds[local, block] = block_add
        if totals[local] is None:
            totals[local] = jnp.concatenate([block_map, block_add], axis=1)
        else:
            top, low = halves(block_map)
            tall = jnp.concatenate(
                [
                    jnp.concatenate([top, top], axis=1),
                    jnp.concatenate([low, jnp.zeros_like(low)], axis=1),
                ],
                axis=0,
            )
            joined = dot_nn(tall, jnp.concatenate(halves(totals[local]), axis=0))
            joined = joined[:width] + joined[width:]
            totals[local] = jnp.concatenate(
                [joined[:, :width], joined[:, width:] + block_add], axis=1
            )
    for local in range(heads_here):
        both = totals[local].astype(bf16)
        slot = (turn * heads_here + local) ^ place
        for other, send in enumerate(sends):

            @pl.when(slot == other)
            def _():
                send[...] = both


def chosen(index, options):
    value = options[0]
    for other in range(1, len(options)):
        value = jnp.where(index == other, options[other], value)
    return value


def run_states(place, parts, state):
    states = []
    width = parts[0].shape[0]
    for member in range(len(parts)):
        states.append(state)
        both = chosen(place ^ member, [part[...] for part in parts])
        top = both[:, :width]
        added = both[:, width:].astype(f32)
        if state is None:
            state = added
        else:
            state = added + dot_nn(
                jnp.concatenate([top, top], axis=1), jnp.concatenate(halves(state), axis=0)
            )
    return states, state


def macro_kernel(*refs):
    count = len(refs) - 1
    place = lax.rem(lax.axis_index("seq"), count)
    states, state = run_states(place, refs[:count], None)
    refs[-1][...] = state.astype(bf16)


def hop_kernel(arrived, *refs):
    count = len(refs) - 1
    place = lax.rem(lax.axis_index("seq"), count)
    states, state = run_states(place, refs[:count], arrived[...].astype(f32))
    refs[-1][...] = state.astype(bf16)


def spread_kernel(arrived, *refs):
    count = len(refs) // 2
    place = lax.rem(lax.axis_index("seq"), count)
    states, state = run_states(place, refs[:count], arrived[...].astype(f32))
    states = [value.astype(bf16) for value in states]
    for turn in range(count):
        refs[count + turn][...] = chosen(place ^ turn, states)


def final_kernel(*refs):
    heads = refs[-1].shape[1] // refs[0].shape[1]
    first_states = refs[:heads]
    reads, offsets, maps, adds, gain, weight = refs[heads : heads + 6]
    outs, normed = refs[heads + 6 : -1], refs[-1]
    heads, tokens, width = reads.shape
    blocks = tokens // BLOCK
    place = lax.rem(lax.axis_index("seq"), heads)
    held = [ref[...] for ref in first_states]
    states = [chosen(place ^ head, held) for head in range(heads)]
    for block in range(blocks):
        at = block * BLOCK
        for head in range(heads):
            state = states[head]
            out = dot_nn(reads[head, at : at + BLOCK, :], state) + offsets[head, at : at + BLOCK, :]
            out = out * lax.rsqrt(jnp.mean(out * out, axis=1, keepdims=True) + epsilon)
            normed[at : at + BLOCK, head * width : (head + 1) * width] = (
                out * gain[...]
            ).astype(bf16)
            if block + 1 < blocks:
                states[head] = (dot_nn(maps[head, block], state) + adds[head, block]).astype(bf16)
    peers = len(outs)
    rows = tokens // peers
    me = lax.axis_index("head")
    for turn in range(peers):
        chunk = me ^ turn
        here = normed[pl.ds(pl.multiple_of(chunk * rows, rows), rows), :]
        outs[turn][...] = dot_nn(here, weight[...]).astype(bf16)


def exchanged(value, axis, mask):
    count = lax.axis_size(axis)
    return lax.ppermute(value, axis, [(source, source ^ mask) for source in range(count)])


def rotated(value, axis, steps):
    count = lax.axis_size(axis)
    return lax.ppermute(value, axis, [(source, (source + steps) % count) for source in range(count)])


def grant(mebibytes):
    return pltpu.CompilerParams(vmem_limit_bytes=mebibytes << 20)


def body(
    queries,
    reflect_keys,
    reflect_values,
    reflect_beta,
    log_decay,
    prompt_lengths,
    norm_gain,
    out_weight,
):
    tokens = queries.shape[1]
    refl = reflect_keys.shape[2]
    heads = reflect_beta.shape[3]
    width = queries.shape[2] // heads
    blocks = tokens // BLOCK
    steps = refl * BLOCK
    beta = reflect_beta[0].transpose(1, 2, 0)
    decay = log_decay[0].transpose(1, 0)
    pair = HEADS_PER_STEP
    rows_spec = pl.BlockSpec((pair, tokens, width), lambda h: (h, 0, 0))
    square_spec = pl.BlockSpec((pair, blocks, width, width), lambda h: (h, 0, 0, 0))
    send_spec = pl.BlockSpec((width, 2 * width), lambda h: (0, 0))
    both_shape = jax.ShapeDtypeStruct((width, 2 * width), bf16)
    reads, offsets, maps, adds, *mine = pl.pallas_call(
        local_kernel,
        grid=(heads // pair,),
        in_specs=[
            pl.BlockSpec(memory_space=pltpu.SMEM),
            pl.BlockSpec((1, tokens, pair * width), lambda h: (0, 0, h)),
            pl.BlockSpec((1, tokens, refl, pair * width), lambda h: (0, 0, 0, h)),
            pl.BlockSpec((1, tokens, refl, pair * width), lambda h: (0, 0, 0, h)),
            pl.BlockSpec((refl, heads, tokens), lambda h: (0, 0, 0)),
            pl.BlockSpec((heads, tokens), lambda h: (0, 0)),
        ],
        out_specs=[rows_spec, rows_spec, square_spec, square_spec] + [send_spec] * heads,
        out_shape=[
            jax.ShapeDtypeStruct((heads, tokens, width), bf16),
            jax.ShapeDtypeStruct((heads, tokens, width), f32),
            jax.ShapeDtypeStruct((heads, blocks, width, width), bf16),
            jax.ShapeDtypeStruct((heads, blocks, width, width), f32),
        ]
        + [both_shape] * heads,
        scratch_shapes=[
            pltpu.VMEM((blocks, steps, steps), f32),
            pltpu.VMEM((blocks, BLOCK, steps), f32),
            pltpu.VMEM((blocks, 8, steps), f32),
        ],
        compiler_params=grant(20),
        name="local_blocks",
    )(prompt_lengths, queries, reflect_keys, reflect_values, beta, decay)

    state_shape = jax.ShapeDtypeStruct((width, width), bf16)
    parts = [mine[0]] + [exchanged(mine[r], "seq", r) for r in range(1, heads)]
    sent = pl.pallas_call(
        macro_kernel, out_shape=state_shape, compiler_params=grant(4), name="macro"
    )(*parts)
    macro_hops = -(-(MOST_LEN - 1) // (tokens * heads))
    arrived = rotated(sent, "seq", heads)
    for hop in range(macro_hops - 1):
        sent = pl.pallas_call(
            hop_kernel, out_shape=state_shape, compiler_params=grant(4), name="hop"
        )(arrived, *parts)
        arrived = rotated(sent, "seq", heads)
    given = pl.pallas_call(
        spread_kernel, out_shape=[state_shape] * heads, compiler_params=grant(4), name="spread"
    )(arrived, *parts)
    states = [given[0]] + [exchanged(given[r], "seq", r) for r in range(1, heads)]

    peers = lax.axis_size("head")
    rows = tokens // peers
    pieces = pl.pallas_call(
        final_kernel,
        out_shape=[jax.ShapeDtypeStruct((rows, out_weight.shape[1]), bf16)] * peers,
        scratch_shapes=[pltpu.VMEM((tokens, heads * width), bf16)],
        compiler_params=grant(16),
        name="read_and_project",
    )(*states, reads, offsets, maps, adds, norm_gain[None], out_weight)
    total = pieces[0].astype(f32)
    for turn in range(1, peers):
        total = total + exchanged(pieces[turn], "head", turn).astype(f32)
    return total.astype(bf16)[None]


def solution(mesh):
    in_specs = (
        P(("parts", "rep"), "seq", "head"),
        P(("parts", "rep"), "seq", None, "head"),
        P(("parts", "rep"), "seq", None, "head"),
        P(("parts", "rep"), "seq", None, "head"),
        P(("parts", "rep"), "seq", "head"),
        P(("parts", "rep"), None),
        P(),
        P("head", None),
    )
    out_specs = P(("parts", "rep"), ("seq", "head"), None)
    return jax.shard_map(body, mesh=mesh, in_specs=in_specs, out_specs=out_specs, check_vma=False)
```

time: 121 us -> 88.4 us (0.73)
  starting transfers between devices: 76.7 us -> 28.1 us
  waiting for transfers between devices: 7.97 us -> 37.4 us
  Pallas kernels: 24.4 us -> 16.5 us
  matrix products: 6.92 us -> 0 us
  local copies, waits for them, and re-layouts: 1.66 us -> 5.23 us
    ppermute x16 -> x9, starting transfers between devices: 70.7 us -> 17.2 us  [exchanged(): lax.ppermute(value, axis, [(source, source ^ mask) for source in range(co...]
    ppermute x16 -> x9, waiting for transfers between devices: 1.9 us -> 19.9 us  [exchanged(): lax.ppermute(value, axis, [(source, source ^ mask) for source in range(co...]
    ppermute x3 -> x2, waiting for transfers between devices: 6.07 us -> 17.5 us  [rotated(): lax.ppermute(value, axis, [(source, (source + steps) % count) for source...]
    dot_general x14 -> x0, matrix products: 6.92 us -> none  [body(): jnp.einsum('hij,hjk->hik', m, s, preferred_element_type=f32) + a]
    ppermute x3 -> x2, starting transfers between devices: 5.93 us -> 10.9 us  [rotated(): lax.ppermute(value, axis, [(source, (source + steps) % count) for source...]
    unnamed x8 -> x16, local copies, waits for them, and re-layouts: 0.63 us -> 5.23 us
    pallas_call x1, Pallas kernels: 6.53 us -> 2.27 us  [body(): pl.pallas_call(final_kernel, out_shape=[jax.ShapeDtypeStruct((rows, out_w...]
    pallas_call x1 -> x4, Pallas kernels: 17.8 us -> 14.2 us  [the longest x1 12.7 us: body(): pl.pallas_call(local_kernel, grid=(heads // pair,), in_specs=[pl.BlockSpe...]
  transfers between devices with their start and end apart: 19 -> 11, of which waited for: 3 -> 9; matrix products, arithmetic and copies ran while one was open for 6% -> 0% of each run, Pallas kernels for 0% -> 0%
where the time goes in v2:
time: 88.4 us; the launch traced here: 88.2 us
  waiting for transfers between devices  37.4 us (42%)
  starting transfers between devices  28.1 us (32%)
  Pallas kernels  16.5 us (19%)
  local copies, waits for them, and re-layouts  5.23 us (6%)
    ppermute x9, waiting for transfers between devices, exchanged(): lax.ppermute(value, axis, [(source, source ^ mask) for source in range(co...  19.9 us
    ppermute x2, waiting for transfers between devices, rotated(): lax.ppermute(value, axis, [(source, (source + steps) % count) for source...  17.5 us
    ppermute x9, starting transfers between devices, exchanged(): lax.ppermute(value, axis, [(source, source ^ mask) for source in range(co...  17.2 us
    pallas_call x1, Pallas kernels, body(): pl.pallas_call(local_kernel, grid=(heads // pair,), in_specs=[pl.BlockSpe...  12.7 us
    ppermute x2, starting transfers between devices, rotated(): lax.ppermute(value, axis, [(source, (source + steps) % count) for source...  10.9 us
    unnamed x16, local copies, waits for them, and re-layouts  5.23 us
    pallas_call x1, Pallas kernels, body(): pl.pallas_call(final_kernel, out_shape=[jax.ShapeDtypeStruct((rows, out_w...  2.27 us
  transfers between devices with their start and end apart: 11, of which 9 were waited for; matrix products, arithmetic and copies ran while one was open for 0% of the time, Pallas kernels for 0%

profile of v2, /device:TPU:40, one launch (start us, length us, event | category | flops | bytes accessed | tf_op | source)
XLA Modules:
  0.0 88.2 jit_solution(16589572309534155803)
XLA Ops:
  0.0 1.2 %copy-done.1 = bf16[1,256,2,512]{3,2,1,0:T(2,128)(2,1)S(1)} copy-done((bf16[1,256,2,512]{3,2,1,0:T(2,128)(2,1)S(1)}, bf16[1,256,2,512]{3,2,1,0:T(2,128)(2,1)}, u32[]{:S(2)}) %copy-start.1) | copy-done | bytes 524312
  1.2 1.0 %copy-done.2 = bf16[1,256,2,512]{3,2,1,0:T(2,128)(2,1)S(1)} copy-done((bf16[1,256,2,512]{3,2,1,0:T(2,128)(2,1)S(1)}, bf16[1,256,2,512]{3,2,1,0:T(2,128)(2,1)}, u32[]{:S(2)}) %copy-start.2) | copy-done | bytes 524312
  2.2 0.9 %copy-done.3 = bf16[1,256,512]{2,1,0:T(8,128)(2,1)S(1)} copy-done((bf16[1,256,512]{2,1,0:T(8,128)(2,1)S(1)}, bf16[1,256,512]{2,1,0:T(8,128)(2,1)}, u32[]{:S(2)}) %copy-start.3) | copy-done | bytes 262168
  3.2 0.7 copy-done.4
  3.9 0.7 copy-done.5
  4.6 0.7 copy-done.6
  5.2 12.7 %local_blocks.1 = (bf16[4,256,128]{2,1,0:T(8,128)(2,1)S(1)}, f32[4,256,128]{2,1,0:T(8,128)S(1)}, bf16[4,4,128,128]{3,2,1,0:T(8,128)(2,1)S(1)}, f32[4,4,128,128]{...) custom-call(s32[1,6]{1,0:T(1,128)S(1)} %copy-done.6, ...), custom_call_target="tpu_custom_call" | custom-call | tf_op jit(solution)/shard_map/local_blocks/pallas_call | solution.py:347
  17.9 2.9 %collective-permute-start = (bf16[128,256]{1,0:T(8,128)(2,1)S(1)}, bf16[128,256]{1,0:T(8,128)(2,1)S(1)}, u32[]{:S(2)}, u32[]{:S(2)}) collective-permute-start(bf16[128,256]{1,0:T(8,128)(2,1)S(1)} %get-tuple-element.22), channel_id=1, source_target_pairs={{0,8},{8,0},{16,24},{24,16},{32,40},{40,32},{48,56},{56,48},{64,72... | collective-permute-start | bytes 196616 | tf_op jit(solution)/shard_map/ppermute | solution.py:312
  20.8 5.0 %collective-permute-start.1 = (bf16[128,256]{1,0:T(8,128)(2,1)S(1)}, bf16[128,256]{1,0:T(8,128)(2,1)S(1)}, u32[]{:S(2)}, u32[]{:S(2)}) collective-permute-start(bf16[128,256]{1,0:T(8,128)(2,1)S(1)} %get-tuple-element.23), channel_id=1, source_target_pairs={{0,16},{8,24},{16,0},{24,8},{32,48},{40,56},{48,32},{56,40},{64,80... | collective-permute-start | bytes 196616 | tf_op jit(solution)/shard_map/ppermute | solution.py:312
  25.8 0.0 collective-permute-start.2
  25.8 4.6 %collective-permute-done.1.refs_2_ = bf16[128,256]{1,0:T(8,128)(2,1)S(1)} collective-permute-done((bf16[128,256]{1,0:T(8,128)(2,1)S(1)}, bf16[128,256]{1,0:T(8,128)(2,1)S(1)}, u32[]{:S(2)}, u32[]{:S(2)}) %collective-permute-start.1) | collective-permute-done | bytes 65568 | tf_op jit(solution)/shard_map/ppermute | solution.py:312
  30.4 1.5 %collective-permute-done.2.refs_3_ = bf16[128,256]{1,0:T(8,128)(2,1)S(1)} collective-permute-done((bf16[128,256]{1,0:T(8,128)(2,1)S(1)}, bf16[128,256]{1,0:T(8,128)(2,1)S(1)}, u32[]{:S(2)}, u32[]{:S(2)}) %collective-permute-start.2) | collective-permute-done | bytes 65568 | tf_op jit(solution)/shard_map/ppermute | solution.py:312
  31.9 0.5 macro.1
  32.4 10.7 %collective-permute-start.3 = (bf16[128,128]{1,0:T(8,128)(2,1)S(1)}, bf16[128,128]{1,0:T(8,128)(2,1)S(1)}, u32[]{:S(2)}, u32[]{:S(2)}) collective-permute-start(bf16[128,128]{1,0:T(8,128)(2,1)S(1)} %macro.1), channel_id=1, source_target_pairs={{0,32},{8,40},{16,48},{24,56},{32,64},{40,72},{48,80},{56,88},{64,... | collective-permute-start | bytes 98312 | tf_op jit(solution)/shard_map/ppermute | solution.py:317
  43.1 9.7 %collective-permute-done.3.arrived = bf16[128,128]{1,0:T(8,128)(2,1)S(1)} collective-permute-done((bf16[128,128]{1,0:T(8,128)(2,1)S(1)}, bf16[128,128]{1,0:T(8,128)(2,1)S(1)}, u32[]{:S(2)}, u32[]{:S(2)}) %collective-permute-start.3) | collective-permute-done | bytes 32800 | tf_op jit(solution)/shard_map/ppermute | solution.py:317
  52.8 0.6 hop.1
  53.5 0.1 collective-permute-start.4
  53.6 7.8 %collective-permute-done.4.arrived = bf16[128,128]{1,0:T(8,128)(2,1)S(1)} collective-permute-done((bf16[128,128]{1,0:T(8,128)(2,1)S(1)}, bf16[128,128]{1,0:T(8,128)(2,1)S(1)}, u32[]{:S(2)}, u32[]{:S(2)}) %collective-permute-start.4) | collective-permute-done | bytes 32800 | tf_op jit(solution)/shard_map/ppermute | solution.py:317
  61.4 0.5 spread.1
  61.9 0.7 collective-permute-start.5
  62.6 2.0 %collective-permute-start.6 = (bf16[128,128]{1,0:T(8,128)(2,1)S(1)}, bf16[128,128]{1,0:T(8,128)(2,1)S(1)}, u32[]{:S(2)}, u32[]{:S(2)}) collective-permute-start(bf16[128,128]{1,0:T(8,128)(2,1)S(1)} %get-tuple-element.27), channel_id=1, source_target_pairs={{0,16},{8,24},{16,0},{24,8},{32,48},{40,56},{48,32},{56,40},{64,80... | collective-permute-start | bytes 98312 | tf_op jit(solution)/shard_map/ppermute | solution.py:312
  64.6 1.8 %collective-permute-start.7 = (bf16[128,128]{1,0:T(8,128)(2,1)S(1)}, bf16[128,128]{1,0:T(8,128)(2,1)S(1)}, u32[]{:S(2)}, u32[]{:S(2)}) collective-permute-start(bf16[128,128]{1,0:T(8,128)(2,1)S(1)} %get-tuple-element.28), channel_id=1, source_target_pairs={{0,24},{8,16},{16,8},{24,0},{32,56},{40,48},{48,40},{56,32},{64,88... | collective-permute-start | bytes 98312 | tf_op jit(solution)/shard_map/ppermute | solution.py:312
  66.4 1.0 %collective-permute-done.6.refs_2_ = bf16[128,128]{1,0:T(8,128)(2,1)S(1)} collective-permute-done((bf16[128,128]{1,0:T(8,128)(2,1)S(1)}, bf16[128,128]{1,0:T(8,128)(2,1)S(1)}, u32[]{:S(2)}, u32[]{:S(2)}) %collective-permute-start.6) | collective-permute-done | bytes 32800 | tf_op jit(solution)/shard_map/ppermute | solution.py:312
  67.4 2.9 %collective-permute-done.7.refs_3_ = bf16[128,128]{1,0:T(8,128)(2,1)S(1)} collective-permute-done((bf16[128,128]{1,0:T(8,128)(2,1)S(1)}, bf16[128,128]{1,0:T(8,128)(2,1)S(1)}, u32[]{:S(2)}, u32[]{:S(2)}) %collective-permute-start.7) | collective-permute-done | bytes 32800 | tf_op jit(solution)/shard_map/ppermute | solution.py:312
  70.3 2.3 %read_and_project.1 = (bf16[64,2048]{1,0:T(8,128)(2,1)S(1)}, bf16[64,2048]{1,0:T(8,128)(2,1)S(1)}, bf16[64,2048]{1,0:T(8,128)(2,1)S(1)}, bf16[64,2048]{1,0:T(8,128)(2,1)S(1)}) custom-call(bf16[128,128]{1,0:T(8,128)(2,1)S(1)} %get-tuple-element.25.refs_0_, bf16[128,128]{1,0:T(8,128)(2,1)S(1)} %collective-permute-done.5.refs_1_, ...), custom_call_target="tpu_custom_call" | custom-call | tf_op jit(solution)/shard_map/read_and_project/pallas_call | solution.py:394
  72.6 1.7 %collective-permute-start.8 = (bf16[64,2048]{1,0:T(8,128)(2,1)S(1)}, bf16[64,2048]{1,0:T(8,128)(2,1)S(1)}, u32[]{:S(2)}, u32[]{:S(2)}) collective-permute-start(bf16[64,2048]{1,0:T(8,128)(2,1)S(1)} %get-tuple-element.34), channel_id=1, source_target_pairs={{0,2},{2,0},{4,6},{6,4},{1,3},{3,1},{5,7},{7,5},{8,10},{10,8},{12,... | collective-permute-start | bytes 786440 | tf_op jit(solution)/shard_map/ppermute | solution.py:312
  74.3 3.0 %collective-permute-start.9 = (bf16[64,2048]{1,0:T(8,128)(2,1)S(1)}, bf16[64,2048]{1,0:T(8,128)(2,1)S(1)}, u32[]{:S(2)}, u32[]{:S(2)}) collective-permute-start(bf16[64,2048]{1,0:T(8,128)(2,1)S(1)} %get-tuple-element.35), channel_id=1, source_target_pairs={{0,4},{2,6},{4,0},{6,2},{1,5},{3,7},{5,1},{7,3},{8,12},{10,14},{12... | collective-permute-start | bytes 786440 | tf_op jit(solution)/shard_map/ppermute | solution.py:312
  77.4 0.1 collective-permute-start.10
  77.4 1.7 %collective-permute-done.8 = bf16[64,2048]{1,0:T(8,128)(2,1)S(1)} collective-permute-done((bf16[64,2048]{1,0:T(8,128)(2,1)S(1)}, bf16[64,2048]{1,0:T(8,128)(2,1)S(1)}, u32[]{:S(2)}, u32[]{:S(2)}) %collective-permute-start.8) | collective-permute-done | bytes 262176 | tf_op jit(solution)/shard_map/ppermute | solution.py:312
  79.1 5.5 %collective-permute-done.9 = bf16[64,2048]{1,0:T(8,128)(2,1)S(1)} collective-permute-done((bf16[64,2048]{1,0:T(8,128)(2,1)S(1)}, bf16[64,2048]{1,0:T(8,128)(2,1)S(1)}, u32[]{:S(2)}, u32[]{:S(2)}) %collective-permute-start.9) | collective-permute-done | bytes 262176 | tf_op jit(solution)/shard_map/ppermute | solution.py:312
  84.6 2.7 %collective-permute-done.10 = bf16[64,2048]{1,0:T(8,128)(2,1)S(1)} collective-permute-done((bf16[64,2048]{1,0:T(8,128)(2,1)S(1)}, bf16[64,2048]{1,0:T(8,128)(2,1)S(1)}, u32[]{:S(2)}, u32[]{:S(2)}) %collective-permute-start.10) | collective-permute-done | bytes 262176 | tf_op jit(solution)/shard_map/ppermute | solution.py:312
  87.3 0.8 fusion
  (12 shorter events, 0.0 us)
Async XLA Ops:
  0.0 70.3 %copy-start = (bf16[512,2048]{1,0:T(8,128)(2,1)S(1)}, bf16[512,2048]{1,0:T(8,128)(2,1)}, u32[]{:S(2)}) copy-start(bf16[512,2048]{1,0:T(8,128)(2,1)} %refs_9_.1) | copy-start | bytes 6291460
  0.0 1.2 %copy-start.1 = (bf16[1,256,2,512]{3,2,1,0:T(2,128)(2,1)S(1)}, bf16[1,256,2,512]{3,2,1,0:T(2,128)(2,1)}, u32[]{:S(2)}) copy-start(bf16[1,256,2,512]{3,2,1,0:T(2,128)(2,1)} %keys.1) | copy-start | bytes 1572868
  1.2 1.0 %copy-start.2 = (bf16[1,256,2,512]{3,2,1,0:T(2,128)(2,1)S(1)}, bf16[1,256,2,512]{3,2,1,0:T(2,128)(2,1)}, u32[]{:S(2)}) copy-start(bf16[1,256,2,512]{3,2,1,0:T(2,128)(2,1)} %values.1) | copy-start | bytes 1572868
  2.2 0.9 %copy-start.3 = (bf16[1,256,512]{2,1,0:T(8,128)(2,1)S(1)}, bf16[1,256,512]{2,1,0:T(8,128)(2,1)}, u32[]{:S(2)}) copy-start(bf16[1,256,512]{2,1,0:T(8,128)(2,1)} %query.1) | copy-start | bytes 786436
  3.2 0.7 copy-start.4
  3.9 0.7 copy-start.5
  4.6 0.7 copy-start.6
  5.2 65.1 %copy-start.7 = (f32[128]{0:T(128)S(1)}, f32[128]{0:T(128)}, u32[]{:S(2)}) copy-start(f32[128]{0:T(128)} %param.14) | copy-start | bytes 1540
  17.9 7.9 %collective-permute-start = (bf16[128,256]{1,0:T(8,128)(2,1)S(1)}, bf16[128,256]{1,0:T(8,128)(2,1)S(1)}, u32[]{:S(2)}, u32[]{:S(2)}) collective-permute-start(bf16[128,256]{1,0:T(8,128)(2,1)S(1)} %get-tuple-element.22), channel_id=1, source_target_pairs={{0,8},{8,0},{16,24},{24,16},{32,40},{40,32},{48,56},{56,48},{64,72... | collective-permute-start | bytes 196616 | tf_op jit(solution)/shard_map/ppermute | solution.py:312
  20.8 9.6 %collective-permute-start.1 = (bf16[128,256]{1,0:T(8,128)(2,1)S(1)}, bf16[128,256]{1,0:T(8,128)(2,1)S(1)}, u32[]{:S(2)}, u32[]{:S(2)}) collective-permute-start(bf16[128,256]{1,0:T(8,128)(2,1)S(1)} %get-tuple-element.23), channel_id=1, source_target_pairs={{0,16},{8,24},{16,0},{24,8},{32,48},{40,56},{48,32},{56,40},{64,80... | collective-permute-start | bytes 196616 | tf_op jit(solution)/shard_map/ppermute | solution.py:312
  25.8 6.1 %collective-permute-start.2 = (bf16[128,256]{1,0:T(8,128)(2,1)S(1)}, bf16[128,256]{1,0:T(8,128)(2,1)S(1)}, u32[]{:S(2)}, u32[]{:S(2)}) collective-permute-start(bf16[128,256]{1,0:T(8,128)(2,1)S(1)} %get-tuple-element.24), channel_id=1, source_target_pairs={{0,24},{8,16},{16,8},{24,0},{32,56},{40,48},{48,40},{56,32},{64,88... | collective-permute-start | bytes 196616 | tf_op jit(solution)/shard_map/ppermute | solution.py:312
  32.4 20.4 %collective-permute-start.3 = (bf16[128,128]{1,0:T(8,128)(2,1)S(1)}, bf16[128,128]{1,0:T(8,128)(2,1)S(1)}, u32[]{:S(2)}, u32[]{:S(2)}) collective-permute-start(bf16[128,128]{1,0:T(8,128)(2,1)S(1)} %macro.1), channel_id=1, source_target_pairs={{0,32},{8,40},{16,48},{24,56},{32,64},{40,72},{48,80},{56,88},{64,... | collective-permute-start | bytes 98312 | tf_op jit(solution)/shard_map/ppermute | solution.py:317
  53.5 7.9 %collective-permute-start.4 = (bf16[128,128]{1,0:T(8,128)(2,1)S(1)}, bf16[128,128]{1,0:T(8,128)(2,1)S(1)}, u32[]{:S(2)}, u32[]{:S(2)}) collective-permute-start(bf16[128,128]{1,0:T(8,128)(2,1)S(1)} %hop.1), channel_id=1, source_target_pairs={{0,32},{8,40},{16,48},{24,56},{32,64},{40,72},{48,80},{56,88},{64,... | collective-permute-start | bytes 98312 | tf_op jit(solution)/shard_map/ppermute | solution.py:317
  61.9 4.5 %collective-permute-start.5 = (bf16[128,128]{1,0:T(8,128)(2,1)S(1)}, bf16[128,128]{1,0:T(8,128)(2,1)S(1)}, u32[]{:S(2)}, u32[]{:S(2)}) collective-permute-start(bf16[128,128]{1,0:T(8,128)(2,1)S(1)} %get-tuple-element.26), channel_id=1, source_target_pairs={{0,8},{8,0},{16,24},{24,16},{32,40},{40,32},{48,56},{56,48},{64,72... | collective-permute-start | bytes 98312 | tf_op jit(solution)/shard_map/ppermute | solution.py:312
  62.6 4.8 %collective-permute-start.6 = (bf16[128,128]{1,0:T(8,128)(2,1)S(1)}, bf16[128,128]{1,0:T(8,128)(2,1)S(1)}, u32[]{:S(2)}, u32[]{:S(2)}) collective-permute-start(bf16[128,128]{1,0:T(8,128)(2,1)S(1)} %get-tuple-element.27), channel_id=1, source_target_pairs={{0,16},{8,24},{16,0},{24,8},{32,48},{40,56},{48,32},{56,40},{64,80... | collective-permute-start | bytes 98312 | tf_op jit(solution)/shard_map/ppermute | solution.py:312
  64.6 5.7 %collective-permute-start.7 = (bf16[128,128]{1,0:T(8,128)(2,1)S(1)}, bf16[128,128]{1,0:T(8,128)(2,1)S(1)}, u32[]{:S(2)}, u32[]{:S(2)}) collective-permute-start(bf16[128,128]{1,0:T(8,128)(2,1)S(1)} %get-tuple-element.28), channel_id=1, source_target_pairs={{0,24},{8,16},{16,8},{24,0},{32,56},{40,48},{48,40},{56,32},{64,88... | collective-permute-start | bytes 98312 | tf_op jit(solution)/shard_map/ppermute | solution.py:312
  72.6 6.5 %collective-permute-start.8 = (bf16[64,2048]{1,0:T(8,128)(2,1)S(1)}, bf16[64,2048]{1,0:T(8,128)(2,1)S(1)}, u32[]{:S(2)}, u32[]{:S(2)}) collective-permute-start(bf16[64,2048]{1,0:T(8,128)(2,1)S(1)} %get-tuple-element.34), channel_id=1, source_target_pairs={{0,2},{2,0},{4,6},{6,4},{1,3},{3,1},{5,7},{7,5},{8,10},{10,8},{12,... | collective-permute-start | bytes 786440 | tf_op jit(solution)/shard_map/ppermute | solution.py:312
  74.3 10.3 %collective-permute-start.9 = (bf16[64,2048]{1,0:T(8,128)(2,1)S(1)}, bf16[64,2048]{1,0:T(8,128)(2,1)S(1)}, u32[]{:S(2)}, u32[]{:S(2)}) collective-permute-start(bf16[64,2048]{1,0:T(8,128)(2,1)S(1)} %get-tuple-element.35), channel_id=1, source_target_pairs={{0,4},{2,6},{4,0},{6,2},{1,5},{3,7},{5,1},{7,3},{8,12},{10,14},{12... | collective-permute-start | bytes 786440 | tf_op jit(solution)/shard_map/ppermute | solution.py:312
  77.4 10.0 %collective-permute-start.10 = (bf16[64,2048]{1,0:T(8,128)(2,1)S(1)}, bf16[64,2048]{1,0:T(8,128)(2,1)S(1)}, u32[]{:S(2)}, u32[]{:S(2)}) collective-permute-start(bf16[64,2048]{1,0:T(8,128)(2,1)S(1)} %get-tuple-element.36), channel_id=1, source_target_pairs={{0,6},{2,4},{4,2},{6,0},{1,7},{3,5},{5,3},{7,1},{8,14},{10,12},{12... | collective-permute-start | bytes 786440 | tf_op jit(solution)/shard_map/ppermute | solution.py:312

commit v3 on v2

--- a/solution.py
+++ b/solution.py
@@ -44,15 +44,18 @@
 
 
 def local_kernel(
-    lengths, query, keys, values, beta, decay, reads, offsets, maps, adds, *rest
+    far_lengths, far_query, far_keys, far_values, far_beta, far_decay, far_weight, far_gain, reads, offsets, maps, adds, *rest
 ):
-    sends = rest[:-3]
-    inner_mask, read_mask, edge_mask = rest[-3:]
+    weight, gain = rest[:2]
+    sends = rest[2:-10]
+    inner_mask, read_mask, edge_mask = rest[-10:-7]
+    lengths, query_all, keys_all, values_all, beta, decay, done = rest[-7:]
     turn = pl.program_id(0)
-    tokens = query.shape[1]
+    turns = query_all.shape[0]
+    tokens = query_all.shape[1]
     heads_here = reads.shape[0]
     width = reads.shape[2]
-    refl = keys.shape[2]
+    refl = keys_all.shape[2]
     steps = BLOCK * refl
     blocks = tokens // BLOCK
     first = lax.axis_index("seq") * tokens
@@ -72,8 +75,39 @@
     read_token = read_step // refl
     hidden = -1e30
 
+    span = heads_here * width
+    copies = [
+        pltpu.make_async_copy(source, target, done.at[index])
+        for index, (source, target) in enumerate(
+            [(far_lengths, lengths), (far_decay, decay), (far_beta, beta)]
+        )
+    ]
+
+    passed = [
+        pltpu.make_async_copy(source, target, done.at[3 + 3 * turns + index])
+        for index, (source, target) in enumerate([(far_weight, weight), (far_gain, gain)])
+    ]
+
+    def fetch(kind, part):
+        lanes = pl.ds(part * span, span)
+        source, target = [
+            (far_keys.at[0, :, :, lanes], keys_all.at[part]),
+            (far_values.at[0, :, :, lanes], values_all.at[part]),
+            (far_query.at[0, :, lanes], query_all.at[part]),
+        ][kind]
+        return pltpu.make_async_copy(source, target, done.at[3 + kind * turns + part])
+
     @pl.when(turn == 0)
     def _():
+        for copy in copies:
+            copy.start()
+        for part in range(turns):
+            for kind in range(3):
+                fetch(kind, part).start()
+        for copy in passed:
+            copy.start()
+        for copy in copies:
+            copy.wait()
         ends, end = [], jnp.int32(0)
         for doc in range(lengths.shape[1]):
             end = end + lengths[0, doc]
@@ -106,11 +140,14 @@
     def to_col(line):
         return jnp.sum(jnp.where(eye, line, 0.0), axis=1, keepdims=True)
 
+    keys, values, query = keys_all.at[turn], values_all.at[turn], query_all.at[turn]
+    for kind in range(3):
+        fetch(kind, turn).wait()
     chains = []
     for local in range(heads_here):
         head = turn * heads_here + local
         lanes = slice(local * width, (local + 1) * width)
-        key_all = keys[0, :, :, lanes].reshape(tokens * refl, width)
+        key_all = keys[:, :, lanes].reshape(tokens * refl, width)
         gate_all = decay[pl.ds(head, 1), :]
         beta_all = [beta[j, pl.ds(head, 1), :] for j in range(refl)]
         for block in range(blocks):
@@ -158,7 +195,7 @@
     for c in chains:
         local, block, key = c["local"], c["block"], c["key"]
         at = block * BLOCK
-        value = values[0, at : at + BLOCK, :, c["lanes"]].reshape(steps, width)
+        value = values[at : at + BLOCK, :, c["lanes"]].reshape(steps, width)
         strength_row = to_row(c["strength"])
         cum_row, scale_row = c["cum_row"], c["scale_row"]
         carry_row = jnp.exp(jnp.minimum(cum_row, edge_mask[block, 0:1, :]))
@@ -180,7 +217,7 @@
         summed = dot_tn(jnp.concatenate([key, key], axis=0), faded)
         block_add = summed[:, :width]
         block_map = carry_row[:, steps - 1 :] * unit - summed[:, width:]
-        query_here = query[0, at : at + BLOCK, c["lanes"]]
+        query_here = query[at : at + BLOCK, c["lanes"]]
         query_f = query_here.astype(f32)
         query_scale = lax.rsqrt(
             jnp.sum(query_f * query_f, axis=1, keepdims=True) + epsilon
@@ -228,6 +265,11 @@
             @pl.when(slot == other)
             def _():
                 send[...] = both
+
+    @pl.when(turn == turns - 1)
+    def _():
+        for copy in passed:
+            copy.wait()
 
 
 def chosen(index, options):
@@ -312,9 +354,9 @@
     return lax.ppermute(value, axis, [(source, source ^ mask) for source in range(count)])
 
 
-def rotated(value, axis, steps):
+def shifted(value, axis, steps):
     count = lax.axis_size(axis)
-    return lax.ppermute(value, axis, [(source, (source + steps) % count) for source in range(count)])
+    return lax.ppermute(value, axis, [(source, source + steps) for source in range(count - steps)])
 
 
 def grant(mebibytes):
@@ -344,33 +386,43 @@
     square_spec = pl.BlockSpec((pair, blocks, width, width), lambda h: (h, 0, 0, 0))
     send_spec = pl.BlockSpec((width, 2 * width), lambda h: (0, 0))
     both_shape = jax.ShapeDtypeStruct((width, 2 * width), bf16)
-    reads, offsets, maps, adds, *mine = pl.pallas_call(
+    reads, offsets, maps, adds, weight, gain, *mine = pl.pallas_call(
         local_kernel,
         grid=(heads // pair,),
-        in_specs=[
-            pl.BlockSpec(memory_space=pltpu.SMEM),
-            pl.BlockSpec((1, tokens, pair * width), lambda h: (0, 0, h)),
-            pl.BlockSpec((1, tokens, refl, pair * width), lambda h: (0, 0, 0, h)),
-            pl.BlockSpec((1, tokens, refl, pair * width), lambda h: (0, 0, 0, h)),
-            pl.BlockSpec((refl, heads, tokens), lambda h: (0, 0, 0)),
-            pl.BlockSpec((heads, tokens), lambda h: (0, 0)),
-        ],
-        out_specs=[rows_spec, rows_spec, square_spec, square_spec] + [send_spec] * heads,
+        in_specs=[pl.BlockSpec(memory_space=pltpu.HBM)] * 8,
+        out_specs=[rows_spec, rows_spec, square_spec, square_spec]
+        + [pl.BlockSpec(memory_space=pl.ANY)] * 2
+        + [send_spec] * heads,
         out_shape=[
             jax.ShapeDtypeStruct((heads, tokens, width), bf16),
             jax.ShapeDtypeStruct((heads, tokens, width), f32),
             jax.ShapeDtypeStruct((heads, blocks, width, width), bf16),
             jax.ShapeDtypeStruct((heads, blocks, width, width), f32),
+            jax.ShapeDtypeStruct(out_weight.shape, bf16),
+            jax.ShapeDtypeStruct((1, width), f32),
         ]
         + [both_shape] * heads,
         scratch_shapes=[
             pltpu.VMEM((blocks, steps, steps), f32),
             pltpu.VMEM((blocks, BLOCK, steps), f32),
             pltpu.VMEM((blocks, 8, steps), f32),
+            pltpu.SMEM(prompt_lengths.shape, jnp.int32),
+            pltpu.VMEM((heads // pair, tokens, pair * width), bf16),
+            pltpu.VMEM((heads // pair, tokens, refl, pair * width), bf16),
+            pltpu.VMEM((heads // pair, tokens, refl, pair * width), bf16),
+            pltpu.VMEM(beta.shape, f32),
+            pltpu.VMEM(decay.shape, f32),
+            pltpu.SemaphoreType.DMA((5 + 3 * (heads // pair),)),
         ],
         compiler_params=grant(20),
         name="local_blocks",
-    )(prompt_lengths, queries, reflect_keys, reflect_values, beta, decay)
+    )(
+        *[
+            pltpu.with_memory_space_constraint(array, pltpu.HBM)
+            for array in (prompt_lengths, queries, reflect_keys, reflect_values, beta, decay)
+            + (out_weight, norm_gain[None])
+        ]
+    )
 
     state_shape = jax.ShapeDtypeStruct((width, width), bf16)
     parts = [mine[0]] + [exchanged(mine[r], "seq", r) for r in range(1, heads)]
@@ -378,12 +430,12 @@
         macro_kernel, out_shape=state_shape, compiler_params=grant(4), name="macro"
     )(*parts)
     macro_hops = -(-(MOST_LEN - 1) // (tokens * heads))
-    arrived = rotated(sent, "seq", heads)
+    arrived = shifted(sent, "seq", heads)
     for hop in range(macro_hops - 1):
         sent = pl.pallas_call(
             hop_kernel, out_shape=state_shape, compiler_params=grant(4), name="hop"
         )(arrived, *parts)
-        arrived = rotated(sent, "seq", heads)
+        arrived = shifted(sent, "seq", heads)
     given = pl.pallas_call(
         spread_kernel, out_shape=[state_shape] * heads, compiler_params=grant(4), name="spread"
     )(arrived, *parts)
@@ -397,9 +449,9 @@
         scratch_shapes=[pltpu.VMEM((tokens, heads * width), bf16)],
         compiler_params=grant(16),
         name="read_and_project",
-    )(*states, reads, offsets, maps, adds, norm_gain[None], out_weight)
+    )(*states, reads, offsets, maps, adds, gain, weight)
     total = pieces[0].astype(f32)
-    for turn in range(1, peers):
+    for turn in (2, 1, 3):
         total = total + exchanged(pieces[turn], "head", turn).astype(f32)
     return total.astype(bf16)[None]
 

time: 88.4 us -> 77.5 us (0.88)
  waiting for transfers between devices: 37.4 us -> 20.4 us
  starting transfers between devices: 28.1 us -> 39.2 us
  local copies, waits for them, and re-layouts: 5.23 us -> 0 us
    ppermute x2, waiting for transfers between devices: 17.5 us -> 3.16 us  [shifted(): lax.ppermute(value, axis, [(source, source + steps) for source in range(c...]
    ppermute x2, starting transfers between devices: 10.9 us -> 22.4 us  [shifted(): lax.ppermute(value, axis, [(source, source + steps) for source in range(c...]
    unnamed x16 -> x0, local copies, waits for them, and re-layouts: 5.23 us -> none
    ppermute x9, waiting for transfers between devices: 19.9 us -> 17.3 us  [exchanged(): lax.ppermute(value, axis, [(source, source ^ mask) for source in range(co...]
where the time goes in v3:
time: 77.5 us; the launch traced here: 77.4 us
  starting transfers between devices  39.2 us (51%)
  waiting for transfers between devices  20.4 us (26%)
  Pallas kernels  16.8 us (22%)
  other arithmetic  0.84 us (1%)
    ppermute x2, starting transfers between devices, shifted(): lax.ppermute(value, axis, [(source, source + steps) for source in range(c...  22.4 us
    ppermute x9, waiting for transfers between devices, exchanged(): lax.ppermute(value, axis, [(source, source ^ mask) for source in range(co...  17.3 us
    ppermute x9, starting transfers between devices, exchanged(): lax.ppermute(value, axis, [(source, source ^ mask) for source in range(co...  16.8 us
    pallas_call x1, Pallas kernels, body(): pl.pallas_call(local_kernel, grid=(heads // pair,), in_specs=[pl.BlockSpe...  12.9 us
    ppermute x2, waiting for transfers between devices, shifted(): lax.ppermute(value, axis, [(source, source + steps) for source in range(c...  3.16 us
    pallas_call x1, Pallas kernels, body(): pl.pallas_call(final_kernel, out_shape=[jax.ShapeDtypeStruct((rows, out_w...  2.27 us
  transfers between devices with their start and end apart: 11, of which 9 were waited for; matrix products, arithmetic and copies ran while one was open for 0% of the time, Pallas kernels for 0%

profile of v3, /device:TPU:40, one launch (start us, length us, event | category | flops | bytes accessed | tf_op | source)
XLA Modules:
  0.0 77.4 jit_solution(6988782135805836760)
XLA Ops:
  0.0 12.9 %local_blocks.1 = (bf16[4,256,128]{2,1,0:T(8,128)(2,1)S(1)}, f32[4,256,128]{2,1,0:T(8,128)S(1)}, bf16[4,4,128,128]{3,2,1,0:T(8,128)(2,1)S(1)}, f32[4,4,128,128]{...) custom-call(s32[1,6]{1,0:T(1,128)} %far_lengths.1, ...), custom_call_target="tpu_custom_call" | custom-call | tf_op jit(solution)/shard_map/local_blocks/pallas_call | solution.py:389
  12.9 2.9 %collective-permute-start = (bf16[128,256]{1,0:T(8,128)(2,1)S(1)}, bf16[128,256]{1,0:T(8,128)(2,1)S(1)}, u32[]{:S(2)}, u32[]{:S(2)}) collective-permute-start(bf16[128,256]{1,0:T(8,128)(2,1)S(1)} %get-tuple-element.24), channel_id=1, source_target_pairs={{0,8},{8,0},{16,24},{24,16},{32,40},{40,32},{48,56},{56,48},{64,72... | collective-permute-start | bytes 196616 | tf_op jit(solution)/shard_map/ppermute | solution.py:354
  15.9 5.0 %collective-permute-start.1 = (bf16[128,256]{1,0:T(8,128)(2,1)S(1)}, bf16[128,256]{1,0:T(8,128)(2,1)S(1)}, u32[]{:S(2)}, u32[]{:S(2)}) collective-permute-start(bf16[128,256]{1,0:T(8,128)(2,1)S(1)} %get-tuple-element.25), channel_id=1, source_target_pairs={{0,16},{8,24},{16,0},{24,8},{32,48},{40,56},{48,32},{56,40},{64,80... | collective-permute-start | bytes 196616 | tf_op jit(solution)/shard_map/ppermute | solution.py:354
  20.8 0.0 collective-permute-start.2
  20.8 0.0 collective-permute-done.refs_1_
  20.8 4.6 %collective-permute-done.1.refs_2_ = bf16[128,256]{1,0:T(8,128)(2,1)S(1)} collective-permute-done((bf16[128,256]{1,0:T(8,128)(2,1)S(1)}, bf16[128,256]{1,0:T(8,128)(2,1)S(1)}, u32[]{:S(2)}, u32[]{:S(2)}) %collective-permute-start.1) | collective-permute-done | bytes 65568 | tf_op jit(solution)/shard_map/ppermute | solution.py:354
  25.4 1.5 %collective-permute-done.2.refs_3_ = bf16[128,256]{1,0:T(8,128)(2,1)S(1)} collective-permute-done((bf16[128,256]{1,0:T(8,128)(2,1)S(1)}, bf16[128,256]{1,0:T(8,128)(2,1)S(1)}, u32[]{:S(2)}, u32[]{:S(2)}) %collective-permute-start.2) | collective-permute-done | bytes 65568 | tf_op jit(solution)/shard_map/ppermute | solution.py:354
  26.9 0.5 macro.1
  27.4 12.6 %collective-permute-start.3 = (bf16[128,128]{1,0:T(8,128)(2,1)S(1)}, bf16[128,128]{1,0:T(8,128)(2,1)S(1)}, u32[]{:S(2)}, u32[]{:S(2)}) collective-permute-start(bf16[128,128]{1,0:T(8,128)(2,1)S(1)} %macro.1), channel_id=1, source_target_pairs={{0,32},{8,40},{16,48},{24,56},{32,64},{40,72},{48,80},{56,88},{64,... | collective-permute-start | bytes 98312 | tf_op jit(solution)/shard_map/ppermute | solution.py:359
  40.0 1.6 %collective-permute-done.3.arrived = bf16[128,128]{1,0:T(8,128)(2,1)S(1)} collective-permute-done((bf16[128,128]{1,0:T(8,128)(2,1)S(1)}, bf16[128,128]{1,0:T(8,128)(2,1)S(1)}, u32[]{:S(2)}, u32[]{:S(2)}) %collective-permute-start.3) | collective-permute-done | bytes 32800 | tf_op jit(solution)/shard_map/ppermute | solution.py:359
  41.6 0.6 hop.1
  42.2 9.9 %collective-permute-start.4 = (bf16[128,128]{1,0:T(8,128)(2,1)S(1)}, bf16[128,128]{1,0:T(8,128)(2,1)S(1)}, u32[]{:S(2)}, u32[]{:S(2)}) collective-permute-start(bf16[128,128]{1,0:T(8,128)(2,1)S(1)} %hop.1), channel_id=1, source_target_pairs={{0,32},{8,40},{16,48},{24,56},{32,64},{40,72},{48,80},{56,88},{64,... | collective-permute-start | bytes 98312 | tf_op jit(solution)/shard_map/ppermute | solution.py:359
  52.1 1.6 %collective-permute-done.4.arrived = bf16[128,128]{1,0:T(8,128)(2,1)S(1)} collective-permute-done((bf16[128,128]{1,0:T(8,128)(2,1)S(1)}, bf16[128,128]{1,0:T(8,128)(2,1)S(1)}, u32[]{:S(2)}, u32[]{:S(2)}) %collective-permute-start.4) | collective-permute-done | bytes 32800 | tf_op jit(solution)/shard_map/ppermute | solution.py:359
  53.7 0.5 spread.1
  54.1 0.1 collective-permute-start.5
  54.3 2.5 %collective-permute-start.6 = (bf16[128,128]{1,0:T(8,128)(2,1)S(1)}, bf16[128,128]{1,0:T(8,128)(2,1)S(1)}, u32[]{:S(2)}, u32[]{:S(2)}) collective-permute-start(bf16[128,128]{1,0:T(8,128)(2,1)S(1)} %get-tuple-element.29), channel_id=1, source_target_pairs={{0,16},{8,24},{16,0},{24,8},{32,48},{40,56},{48,32},{56,40},{64,80... | collective-permute-start | bytes 98312 | tf_op jit(solution)/shard_map/ppermute | solution.py:354
  56.8 1.8 %collective-permute-start.7 = (bf16[128,128]{1,0:T(8,128)(2,1)S(1)}, bf16[128,128]{1,0:T(8,128)(2,1)S(1)}, u32[]{:S(2)}, u32[]{:S(2)}) collective-permute-start(bf16[128,128]{1,0:T(8,128)(2,1)S(1)} %get-tuple-element.30), channel_id=1, source_target_pairs={{0,24},{8,16},{16,8},{24,0},{32,56},{40,48},{48,40},{56,32},{64,88... | collective-permute-start | bytes 98312 | tf_op jit(solution)/shard_map/ppermute | solution.py:354
  58.7 0.0 collective-permute-done.5.refs_1_
  58.7 0.6 collective-permute-done.6.refs_2_
  59.2 3.3 %collective-permute-done.7.refs_3_ = bf16[128,128]{1,0:T(8,128)(2,1)S(1)} collective-permute-done((bf16[128,128]{1,0:T(8,128)(2,1)S(1)}, bf16[128,128]{1,0:T(8,128)(2,1)S(1)}, u32[]{:S(2)}, u32[]{:S(2)}) %collective-permute-start.7) | collective-permute-done | bytes 32800 | tf_op jit(solution)/shard_map/ppermute | solution.py:354
  62.5 2.3 %read_and_project.1 = (bf16[64,2048]{1,0:T(8,128)(2,1)S(1)}, bf16[64,2048]{1,0:T(8,128)(2,1)S(1)}, bf16[64,2048]{1,0:T(8,128)(2,1)S(1)}, bf16[64,2048]{1,0:T(8,128)(2,1)S(1)}) custom-call(bf16[128,128]{1,0:T(8,128)(2,1)S(1)} %get-tuple-element.27.refs_0_, bf16[128,128]{1,0:T(8,128)(2,1)S(1)} %collective-permute-done.5.refs_1_, ...), custom_call_target="tpu_custom_call" | custom-call | tf_op jit(solution)/shard_map/read_and_project/pallas_call | solution.py:446
  64.8 3.4 %collective-permute-start.8 = (bf16[64,2048]{1,0:T(8,128)(2,1)S(1)}, bf16[64,2048]{1,0:T(8,128)(2,1)S(1)}, u32[]{:S(2)}, u32[]{:S(2)}) collective-permute-start(bf16[64,2048]{1,0:T(8,128)(2,1)S(1)} %get-tuple-element.38), channel_id=1, source_target_pairs={{0,4},{2,6},{4,0},{6,2},{1,5},{3,7},{5,1},{7,3},{8,12},{10,14},{12... | collective-permute-start | bytes 786440 | tf_op jit(solution)/shard_map/ppermute | solution.py:354
  68.2 0.7 collective-permute-start.9
  69.0 0.3 collective-permute-start.10
  69.2 3.8 %collective-permute-done.8 = bf16[64,2048]{1,0:T(8,128)(2,1)S(1)} collective-permute-done((bf16[64,2048]{1,0:T(8,128)(2,1)S(1)}, bf16[64,2048]{1,0:T(8,128)(2,1)S(1)}, u32[]{:S(2)}, u32[]{:S(2)}) %collective-permute-start.8) | collective-permute-done | bytes 262176 | tf_op jit(solution)/shard_map/ppermute | solution.py:354
  73.0 3.2 %collective-permute-done.9 = bf16[64,2048]{1,0:T(8,128)(2,1)S(1)} collective-permute-done((bf16[64,2048]{1,0:T(8,128)(2,1)S(1)}, bf16[64,2048]{1,0:T(8,128)(2,1)S(1)}, u32[]{:S(2)}, u32[]{:S(2)}) %collective-permute-start.9) | collective-permute-done | bytes 262176 | tf_op jit(solution)/shard_map/ppermute | solution.py:354
  76.2 0.3 collective-permute-done.10
  76.6 0.8 %fusion = bf16[1,64,2048]{2,1,0:T(8,128)(2,1)} fusion(bf16[64,2048]{1,0:T(8,128)(2,1)S(1)} %collective-permute-done.10, bf16[64,2048]{1,0:T(8,128)(2,1)S(1)} %collective-permute-done.9, bf16[64,2048]{1,0:T(8,128)(2,1)S(1)} %collective-permute-done.8, bf16[64,2048]{1,0:T(8,128)(2,1)S(1)} %get-tuple-element.37), kind=kLoop, calls=%fused_computation.1 | loop fusion | flops 1048576 | bytes 1310720 | tf_op jit(solution)/shard_map/broadcast_in_dim | solution.py:456
Async XLA Ops:
  12.9 7.9 %collective-permute-start = (bf16[128,256]{1,0:T(8,128)(2,1)S(1)}, bf16[128,256]{1,0:T(8,128)(2,1)S(1)}, u32[]{:S(2)}, u32[]{:S(2)}) collective-permute-start(bf16[128,256]{1,0:T(8,128)(2,1)S(1)} %get-tuple-element.24), channel_id=1, source_target_pairs={{0,8},{8,0},{16,24},{24,16},{32,40},{40,32},{48,56},{56,48},{64,72... | collective-permute-start | bytes 196616 | tf_op jit(solution)/shard_map/ppermute | solution.py:354
  15.9 9.5 %collective-permute-start.1 = (bf16[128,256]{1,0:T(8,128)(2,1)S(1)}, bf16[128,256]{1,0:T(8,128)(2,1)S(1)}, u32[]{:S(2)}, u32[]{:S(2)}) collective-permute-start(bf16[128,256]{1,0:T(8,128)(2,1)S(1)} %get-tuple-element.25), channel_id=1, source_target_pairs={{0,16},{8,24},{16,0},{24,8},{32,48},{40,56},{48,32},{56,40},{64,80... | collective-permute-start | bytes 196616 | tf_op jit(solution)/shard_map/ppermute | solution.py:354
  20.8 6.1 %collective-permute-start.2 = (bf16[128,256]{1,0:T(8,128)(2,1)S(1)}, bf16[128,256]{1,0:T(8,128)(2,1)S(1)}, u32[]{:S(2)}, u32[]{:S(2)}) collective-permute-start(bf16[128,256]{1,0:T(8,128)(2,1)S(1)} %get-tuple-element.26), channel_id=1, source_target_pairs={{0,24},{8,16},{16,8},{24,0},{32,56},{40,48},{48,40},{56,32},{64,88... | collective-permute-start | bytes 196616 | tf_op jit(solution)/shard_map/ppermute | solution.py:354
  27.4 14.2 %collective-permute-start.3 = (bf16[128,128]{1,0:T(8,128)(2,1)S(1)}, bf16[128,128]{1,0:T(8,128)(2,1)S(1)}, u32[]{:S(2)}, u32[]{:S(2)}) collective-permute-start(bf16[128,128]{1,0:T(8,128)(2,1)S(1)} %macro.1), channel_id=1, source_target_pairs={{0,32},{8,40},{16,48},{24,56},{32,64},{40,72},{48,80},{56,88},{64,... | collective-permute-start | bytes 98312 | tf_op jit(solution)/shard_map/ppermute | solution.py:359
  42.2 11.4 %collective-permute-start.4 = (bf16[128,128]{1,0:T(8,128)(2,1)S(1)}, bf16[128,128]{1,0:T(8,128)(2,1)S(1)}, u32[]{:S(2)}, u32[]{:S(2)}) collective-permute-start(bf16[128,128]{1,0:T(8,128)(2,1)S(1)} %hop.1), channel_id=1, source_target_pairs={{0,32},{8,40},{16,48},{24,56},{32,64},{40,72},{48,80},{56,88},{64,... | collective-permute-start | bytes 98312 | tf_op jit(solution)/shard_map/ppermute | solution.py:359
  54.1 4.5 %collective-permute-start.5 = (bf16[128,128]{1,0:T(8,128)(2,1)S(1)}, bf16[128,128]{1,0:T(8,128)(2,1)S(1)}, u32[]{:S(2)}, u32[]{:S(2)}) collective-permute-start(bf16[128,128]{1,0:T(8,128)(2,1)S(1)} %get-tuple-element.28), channel_id=1, source_target_pairs={{0,8},{8,0},{16,24},{24,16},{32,40},{40,32},{48,56},{56,48},{64,72... | collective-permute-start | bytes 98312 | tf_op jit(solution)/shard_map/ppermute | solution.py:354
  54.3 4.9 %collective-permute-start.6 = (bf16[128,128]{1,0:T(8,128)(2,1)S(1)}, bf16[128,128]{1,0:T(8,128)(2,1)S(1)}, u32[]{:S(2)}, u32[]{:S(2)}) collective-permute-start(bf16[128,128]{1,0:T(8,128)(2,1)S(1)} %get-tuple-element.29), channel_id=1, source_target_pairs={{0,16},{8,24},{16,0},{24,8},{32,48},{40,56},{48,32},{56,40},{64,80... | collective-permute-start | bytes 98312 | tf_op jit(solution)/shard_map/ppermute | solution.py:354
  56.8 5.7 %collective-permute-start.7 = (bf16[128,128]{1,0:T(8,128)(2,1)S(1)}, bf16[128,128]{1,0:T(8,128)(2,1)S(1)}, u32[]{:S(2)}, u32[]{:S(2)}) collective-permute-start(bf16[128,128]{1,0:T(8,128)(2,1)S(1)} %get-tuple-element.30), channel_id=1, source_target_pairs={{0,24},{8,16},{16,8},{24,0},{32,56},{40,48},{48,40},{56,32},{64,88... | collective-permute-start | bytes 98312 | tf_op jit(solution)/shard_map/ppermute | solution.py:354
  64.8 8.2 %collective-permute-start.8 = (bf16[64,2048]{1,0:T(8,128)(2,1)S(1)}, bf16[64,2048]{1,0:T(8,128)(2,1)S(1)}, u32[]{:S(2)}, u32[]{:S(2)}) collective-permute-start(bf16[64,2048]{1,0:T(8,128)(2,1)S(1)} %get-tuple-element.38), channel_id=1, source_target_pairs={{0,4},{2,6},{4,0},{6,2},{1,5},{3,7},{5,1},{7,3},{8,12},{10,14},{12... | collective-permute-start | bytes 786440 | tf_op jit(solution)/shard_map/ppermute | solution.py:354
  68.2 8.0 %collective-permute-start.9 = (bf16[64,2048]{1,0:T(8,128)(2,1)S(1)}, bf16[64,2048]{1,0:T(8,128)(2,1)S(1)}, u32[]{:S(2)}, u32[]{:S(2)}) collective-permute-start(bf16[64,2048]{1,0:T(8,128)(2,1)S(1)} %get-tuple-element.39), channel_id=1, source_target_pairs={{0,2},{2,0},{4,6},{6,4},{1,3},{3,1},{5,7},{7,5},{8,10},{10,8},{12,... | collective-permute-start | bytes 786440 | tf_op jit(solution)/shard_map/ppermute | solution.py:354
  69.0 7.6 %collective-permute-start.10 = (bf16[64,2048]{1,0:T(8,128)(2,1)S(1)}, bf16[64,2048]{1,0:T(8,128)(2,1)S(1)}, u32[]{:S(2)}, u32[]{:S(2)}) collective-permute-start(bf16[64,2048]{1,0:T(8,128)(2,1)S(1)} %get-tuple-element.40), channel_id=1, source_target_pairs={{0,6},{2,4},{4,2},{6,0},{1,7},{3,5},{5,3},{7,1},{8,14},{10,12},{12... | collective-permute-start | bytes 786440 | tf_op jit(solution)/shard_map/ppermute | solution.py:354

commit v4 on v3

--- a/solution.py
+++ b/solution.py
@@ -1,3 +1,5 @@
+import functools
+
 import jax
 import jax.numpy as jnp
 from jax import lax
@@ -144,107 +146,91 @@
     for kind in range(3):
         fetch(kind, turn).wait()
     chains = []
-    for local in range(heads_here):
-        head = turn * heads_here + local
-        lanes = slice(local * width, (local + 1) * width)
-        key_all = keys[:, :, lanes].reshape(tokens * refl, width)
-        gate_all = decay[pl.ds(head, 1), :]
-        beta_all = [beta[j, pl.ds(head, 1), :] for j in range(refl)]
-        for block in range(blocks):
+    for block in range(blocks):
+        for local in range(heads_here):
+            lanes = slice(local * width, (local + 1) * width)
             at = block * BLOCK
-            key = key_all[at * refl : at * refl + steps]
-            gate = gate_all[:, at : at + BLOCK]
-            cum = jnp.sum(jnp.where(token_lane <= token_col, gate, 0.0), axis=1, keepdims=True)
-            beta_here = beta_all[refl - 1][:, at : at + BLOCK]
-            for j in range(refl - 1):
-                beta_here = jnp.where(refl_col == j, beta_all[j][:, at : at + BLOCK], beta_here)
-            strength = jnp.sum(
-                jnp.where(token_lane == token_col, beta_here, 0.0), axis=1, keepdims=True
-            )
-            gram = dot_nt(key, key)
-            diagonal = jnp.where(eye, gram, 0.0)
-            scale = lax.rsqrt(jnp.sum(diagonal, axis=1, keepdims=True) + epsilon)
-            scale_row = lax.rsqrt(jnp.sum(diagonal, axis=0, keepdims=True) + epsilon)
-            cum_row = to_row(cum)
-            ratio = jnp.exp(jnp.minimum(cum - cum_row, inner_mask[block]))
-            system = (strength * scale) * ratio * gram * scale_row
+            rows = slice(at, at + BLOCK)
             chains.append(
                 dict(
                     local=local,
                     block=block,
+                    rows=rows,
                     lanes=lanes,
-                    key=key,
-                    gate=gate,
-                    cum_row=cum_row,
-                    strength=strength,
-                    scale_row=scale_row,
-                    system=halves(system),
-                    inverse=unit - jnp.where((row ^ col) == 1, system, 0.0),
+                    head=turn * heads_here + local,
+                    key=keys[rows, :, lanes].reshape(steps, width),
                 )
             )
+    for c in chains:
+        c["gram"] = dot_nt(c["key"], c["key"])
+    for c in chains:
+        gate = decay[pl.ds(c["head"], 1), :][:, c["rows"]]
+        cum = jnp.sum(jnp.where(token_lane <= token_col, gate, 0.0), axis=1, keepdims=True)
+        beta_here = beta[refl - 1, pl.ds(c["head"], 1), :][:, c["rows"]]
+        for j in range(refl - 1):
+            beta_here = jnp.where(
+                refl_col == j, beta[j, pl.ds(c["head"], 1), :][:, c["rows"]], beta_here
+            )
+        c["cum"] = cum
+        c["strength"] = jnp.sum(
+            jnp.where(token_lane == token_col, beta_here, 0.0), axis=1, keepdims=True
+        )
+    for c in chains:
+        diagonal = jnp.where(eye, c["gram"], 0.0)
+        c["scale"] = lax.rsqrt(jnp.sum(diagonal, axis=1, keepdims=True) + epsilon)
+        c["scale_row"] = lax.rsqrt(jnp.sum(diagonal, axis=0, keepdims=True) + epsilon)
+        c["cum_row"] = to_row(c["cum"])
+        c["strength_row"] = to_row(c["strength"])
+    for c in chains:
+        ratio = jnp.exp(jnp.minimum(c["cum"] - c["cum_row"], inner_mask[c["block"]]))
+        system = (c["strength"] * c["scale"]) * ratio * c["gram"] * c["scale_row"]
+        c["system"] = halves(system)
+        c["inverse"] = unit - jnp.where((row ^ col) == 1, system, 0.0)
     size = 2
     while size < steps:
         mask = ((row // size) ^ (col // size)) == 1
         for c in chains:
-            inverse = halves(c["inverse"])
+            c["halves"] = halves(c["inverse"])
             corner = tuple(jnp.where(mask, part, jnp.zeros_like(part)) for part in c["system"])
-            moved = square_product(corner, inverse)
-            c["inverse"] = c["inverse"] - square_product(inverse, halves(moved))
+            c["moved"] = square_product(corner, c["halves"])
+        for c in chains:
+            c["inverse"] = c["inverse"] - square_product(c["halves"], halves(c["moved"]))
         size *= 2
-    totals = [None] * heads_here
-    for c in chains:
-        local, block, key = c["local"], c["block"], c["key"]
-        at = block * BLOCK
-        value = values[at : at + BLOCK, :, c["lanes"]].reshape(steps, width)
-        strength_row = to_row(c["strength"])
-        cum_row, scale_row = c["cum_row"], c["scale_row"]
-        carry_row = jnp.exp(jnp.minimum(cum_row, edge_mask[block, 0:1, :]))
-        value_side = jnp.concatenate(halves(c["inverse"] * strength_row), axis=1)
+    for c in chains:
+        value = values[c["rows"], :, c["lanes"]].reshape(steps, width)
+        carry_row = jnp.exp(jnp.minimum(c["cum_row"], edge_mask[c["block"], 0:1, :]))
+        c["carry_row"] = carry_row
+        value_side = jnp.concatenate(halves(c["inverse"] * c["strength_row"]), axis=1)
         key_side = jnp.concatenate(
-            halves(c["inverse"] * (strength_row * carry_row * scale_row)), axis=1
-        )
-        writes = jnp.concatenate(
+            halves(c["inverse"] * (c["strength_row"] * carry_row * c["scale_row"])), axis=1
+        )
+        c["twice"] = jnp.concatenate([c["key"], c["key"]], axis=0)
+        c["writes"] = jnp.concatenate(
             [
                 dot_nn(value_side, jnp.concatenate([value, value], axis=0)),
-                dot_nn(key_side, jnp.concatenate([key, key], axis=0)),
+                dot_nn(key_side, c["twice"]),
             ],
             axis=1,
         )
-        fade_row = scale_row * jnp.exp(
-            jnp.minimum(cum_row[:, steps - 1 :] - cum_row, edge_mask[block, 1:2, :])
-        )
-        faded = jnp.concatenate(halves(to_col(fade_row) * writes), axis=0)
-        summed = dot_tn(jnp.concatenate([key, key], axis=0), faded)
-        block_add = summed[:, :width]
-        block_map = carry_row[:, steps - 1 :] * unit - summed[:, width:]
-        query_here = query[at : at + BLOCK, c["lanes"]]
-        query_f = query_here.astype(f32)
-        query_scale = lax.rsqrt(
-            jnp.sum(query_f * query_f, axis=1, keepdims=True) + epsilon
-        ) * (width ** (-0.5))
-        read_cum = jnp.sum(
-            jnp.where(read_lane <= read_col, c["gate"], 0.0), axis=1, keepdims=True
-        )
-        weights = jnp.exp(jnp.minimum(read_cum - cum_row, read_mask[block]))
-        weights = weights * dot_nt(query_here, key) * query_scale * scale_row
-        writes_top = writes.astype(bf16)
-        seen = dot_nn(
-            jnp.concatenate(halves(weights), axis=1),
-            jnp.concatenate([writes_top, writes_top], axis=0),
-        )
-        read_carry = jnp.sum(
-            jnp.where(read_step == read_col * refl, carry_row, 0.0), axis=1, keepdims=True
-        )
-        offsets[local, at : at + BLOCK, :] = seen[:, :width]
-        reads[local, at : at + BLOCK, :] = (
-            (read_carry * query_scale) * query_f - seen[:, width:]
-        ).astype(bf16)
-        maps[local, block] = block_map.astype(bf16)
-        adds[local, block] = block_add
+    for c in chains:
+        cum_row = c["cum_row"]
+        fade_row = c["scale_row"] * jnp.exp(
+            jnp.minimum(cum_row[:, steps - 1 :] - cum_row, edge_mask[c["block"], 1:2, :])
+        )
+        faded = jnp.concatenate(halves(to_col(fade_row) * c["writes"]), axis=0)
+        summed = dot_tn(c["twice"], faded)
+        c["add"] = summed[:, :width]
+        c["map"] = c["carry_row"][:, steps - 1 :] * unit - summed[:, width:]
+    for c in chains:
+        maps[c["local"], c["block"]] = c["map"].astype(bf16)
+        adds[c["local"], c["block"]] = c["add"]
+    totals = [None] * heads_here
+    for c in chains:
+        local, rows = c["local"], c["rows"]
         if totals[local] is None:
-            totals[local] = jnp.concatenate([block_map, block_add], axis=1)
+            totals[local] = jnp.concatenate([c["map"], c["add"]], axis=1)
         else:
-            top, low = halves(block_map)
+            top, low = halves(c["map"])
             tall = jnp.concatenate(
                 [
                     jnp.concatenate([top, top], axis=1),
@@ -255,8 +241,29 @@
             joined = dot_nn(tall, jnp.concatenate(halves(totals[local]), axis=0))
             joined = joined[:width] + joined[width:]
             totals[local] = jnp.concatenate(
-                [joined[:, :width], joined[:, width:] + block_add], axis=1
-            )
+                [joined[:, :width], joined[:, width:] + c["add"]], axis=1
+            )
+        query_here = query[rows, c["lanes"]]
+        query_f = query_here.astype(f32)
+        query_scale = lax.rsqrt(
+            jnp.sum(query_f * query_f, axis=1, keepdims=True) + epsilon
+        ) * (width ** (-0.5))
+        gate = decay[pl.ds(c["head"], 1), :][:, rows]
+        read_cum = jnp.sum(jnp.where(read_lane <= read_col, gate, 0.0), axis=1, keepdims=True)
+        weights = jnp.exp(jnp.minimum(read_cum - c["cum_row"], read_mask[c["block"]]))
+        weights = weights * dot_nt(query_here, c["key"]) * query_scale * c["scale_row"]
+        writes_top = c["writes"].astype(bf16)
+        seen = dot_nn(
+            jnp.concatenate(halves(weights), axis=1),
+            jnp.concatenate([writes_top, writes_top], axis=0),
+        )
+        read_carry = jnp.sum(
+            jnp.where(read_step == read_col * refl, c["carry_row"], 0.0), axis=1, keepdims=True
+        )
+        offsets[local, rows, :] = seen[:, :width]
+        reads[local, rows, :] = (
+            (read_carry * query_scale) * query_f - seen[:, width:]
+        ).astype(bf16)
     for local in range(heads_here):
         both = totals[local].astype(bf16)
         slot = (turn * heads_here + local) ^ place
@@ -303,20 +310,25 @@
     refs[-1][...] = state.astype(bf16)
 
 
-def hop_kernel(arrived, *refs):
-    count = len(refs) - 1
+def settled(arrivals, count):
+    macro = lax.axis_index("seq") // count
+    last = jnp.clip(macro - 1, 0, len(arrivals) - 1)
+    return chosen(last, [arrived[...] for arrived in arrivals]).astype(f32)
+
+
+def hop_kernel(*refs, count):
     place = lax.rem(lax.axis_index("seq"), count)
-    states, state = run_states(place, refs[:count], arrived[...].astype(f32))
+    states, state = run_states(place, refs[-1 - count : -1], settled(refs[: -1 - count], count))
     refs[-1][...] = state.astype(bf16)
 
 
-def spread_kernel(arrived, *refs):
-    count = len(refs) // 2
+def spread_kernel(*refs, count):
     place = lax.rem(lax.axis_index("seq"), count)
-    states, state = run_states(place, refs[:count], arrived[...].astype(f32))
+    arrivals, parts, outs = refs[: -2 * count], refs[-2 * count : -count], refs[-count:]
+    states, state = run_states(place, parts, settled(arrivals, count))
     states = [value.astype(bf16) for value in states]
     for turn in range(count):
-        refs[count + turn][...] = chosen(place ^ turn, states)
+        outs[turn][...] = chosen(place ^ turn, states)
 
 
 def final_kernel(*refs):
@@ -354,9 +366,10 @@
     return lax.ppermute(value, axis, [(source, source ^ mask) for source in range(count)])
 
 
-def shifted(value, axis, steps):
+def shifted(value, axis, steps, least=0):
     count = lax.axis_size(axis)
-    return lax.ppermute(value, axis, [(source, source + steps) for source in range(count - steps)])
+    pairs = [(source, source + steps) for source in range(least, count - steps)]
+    return lax.ppermute(value, axis, pairs)
 
 
 def grant(mebibytes):
@@ -430,15 +443,21 @@
         macro_kernel, out_shape=state_shape, compiler_params=grant(4), name="macro"
     )(*parts)
     macro_hops = -(-(MOST_LEN - 1) // (tokens * heads))
-    arrived = shifted(sent, "seq", heads)
-    for hop in range(macro_hops - 1):
+    arrivals = [shifted(sent, "seq", heads)]
+    for hop in range(1, macro_hops):
         sent = pl.pallas_call(
-            hop_kernel, out_shape=state_shape, compiler_params=grant(4), name="hop"
-        )(arrived, *parts)
-        arrived = shifted(sent, "seq", heads)
+            functools.partial(hop_kernel, count=heads),
+            out_shape=state_shape,
+            compiler_params=grant(4),
+            name="hop",
+        )(*arrivals, *parts)
+        arrivals.append(shifted(sent, "seq", heads, hop * heads))
     given = pl.pallas_call(
-        spread_kernel, out_shape=[state_shape] * heads, compiler_params=grant(4), name="spread"
-    )(arrived, *parts)
+        functools.partial(spread_kernel, count=heads),
+        out_shape=[state_shape] * heads,
+        compiler_params=grant(4),
+        name="spread",
+    )(*arrivals, *parts)
     states = [given[0]] + [exchanged(given[r], "seq", r) for r in range(1, heads)]
 
     peers = lax.axis_size("head")

time: 77.5 us -> 72.6 us (0.937)
  the two profiles are of different devices: /device:TPU:40 before, /device:TPU:552 now
where the time goes in v4:
time: 72.6 us; the launch traced here: 72.5 us
  starting transfers between devices  34.9 us (48%)
  waiting for transfers between devices  20.5 us (28%)
  Pallas kernels  16.2 us (22%)
  other arithmetic  0.84 us (1%)
    ppermute x2, starting transfers between devices, shifted(): return lax.ppermute(value, axis, pairs)  18 us
    ppermute x9, waiting for transfers between devices, exchanged(): lax.ppermute(value, axis, [(source, source ^ mask) for source in range(co...  17.4 us
    ppermute x9, starting transfers between devices, exchanged(): lax.ppermute(value, axis, [(source, source ^ mask) for source in range(co...  16.8 us
    pallas_call x1, Pallas kernels, body(): pl.pallas_call(local_kernel, grid=(heads // pair,), in_specs=[pl.BlockSpe...  12.3 us
    ppermute x2, waiting for transfers between devices, shifted(): return lax.ppermute(value, axis, pairs)  3.15 us
    pallas_call x1, Pallas kernels, body(): pl.pallas_call(final_kernel, out_shape=[jax.ShapeDtypeStruct((rows, out_w...  2.27 us
  transfers between devices with their start and end apart: 11, of which 9 were waited for; matrix products, arithmetic and copies ran while one was open for 0% of the time, Pallas kernels for 0%

profile of v4, /device:TPU:552, one launch (start us, length us, event | category | flops | bytes accessed | tf_op | source)
XLA Modules:
  0.0 72.5 jit_solution(15338188273484764035)
XLA Ops:
  0.0 12.3 %local_blocks.1 = (bf16[4,256,128]{2,1,0:T(8,128)(2,1)S(1)}, f32[4,256,128]{2,1,0:T(8,128)S(1)}, bf16[4,4,128,128]{3,2,1,0:T(8,128)(2,1)S(1)}, f32[4,4,128,128]{...) custom-call(s32[1,6]{1,0:T(1,128)} %far_lengths.1, ...), custom_call_target="tpu_custom_call" | custom-call | tf_op jit(solution)/shard_map/local_blocks/pallas_call | solution.py:402
  12.3 2.9 %collective-permute-start = (bf16[128,256]{1,0:T(8,128)(2,1)S(1)}, bf16[128,256]{1,0:T(8,128)(2,1)S(1)}, u32[]{:S(2)}, u32[]{:S(2)}) collective-permute-start(bf16[128,256]{1,0:T(8,128)(2,1)S(1)} %get-tuple-element.24), channel_id=1, source_target_pairs={{0,8},{8,0},{16,24},{24,16},{32,40},{40,32},{48,56},{56,48},{64,72... | collective-permute-start | bytes 196616 | tf_op jit(solution)/shard_map/ppermute | solution.py:366
  15.2 5.0 %collective-permute-start.1 = (bf16[128,256]{1,0:T(8,128)(2,1)S(1)}, bf16[128,256]{1,0:T(8,128)(2,1)S(1)}, u32[]{:S(2)}, u32[]{:S(2)}) collective-permute-start(bf16[128,256]{1,0:T(8,128)(2,1)S(1)} %get-tuple-element.25), channel_id=1, source_target_pairs={{0,16},{8,24},{16,0},{24,8},{32,48},{40,56},{48,32},{56,40},{64,80... | collective-permute-start | bytes 196616 | tf_op jit(solution)/shard_map/ppermute | solution.py:366
  20.2 0.0 collective-permute-start.2
  20.2 0.0 collective-permute-done.refs_1_.refs_2_.refs_3_
  20.2 4.6 %collective-permute-done.1.refs_2_.refs_3_.refs_4_ = bf16[128,256]{1,0:T(8,128)(2,1)S(1)} collective-permute-done((bf16[128,256]{1,0:T(8,128)(2,1)S(1)}, bf16[128,256]{1,0:T(8,128)(2,1)S(1)}, u32[]{:S(2)}, u32[]{:S(2)}) %collective-permute-start.1) | collective-permute-done | bytes 65568 | tf_op jit(solution)/shard_map/ppermute | solution.py:366
  24.8 1.5 %collective-permute-done.2.refs_3_.refs_4_.refs_5_ = bf16[128,256]{1,0:T(8,128)(2,1)S(1)} collective-permute-done((bf16[128,256]{1,0:T(8,128)(2,1)S(1)}, bf16[128,256]{1,0:T(8,128)(2,1)S(1)}, u32[]{:S(2)}, u32[]{:S(2)}) %collective-permute-start.2) | collective-permute-done | bytes 65568 | tf_op jit(solution)/shard_map/ppermute | solution.py:366
  26.3 0.5 macro.1
  26.8 9.9 %collective-permute-start.3 = (bf16[128,128]{1,0:T(8,128)(2,1)S(1)}, bf16[128,128]{1,0:T(8,128)(2,1)S(1)}, u32[]{:S(2)}, u32[]{:S(2)}) collective-permute-start(bf16[128,128]{1,0:T(8,128)(2,1)S(1)} %macro.1), channel_id=1, source_target_pairs={{0,32},{8,40},{16,48},{24,56},{32,64},{40,72},{48,80},{56,88},{64,... | collective-permute-start | bytes 98312 | tf_op jit(solution)/shard_map/ppermute | solution.py:372
  36.7 1.6 %collective-permute-done.3.refs_0_ = bf16[128,128]{1,0:T(8,128)(2,1)S(1)} collective-permute-done((bf16[128,128]{1,0:T(8,128)(2,1)S(1)}, bf16[128,128]{1,0:T(8,128)(2,1)S(1)}, u32[]{:S(2)}, u32[]{:S(2)}) %collective-permute-start.3) | collective-permute-done | bytes 32800 | tf_op jit(solution)/shard_map/ppermute | solution.py:372
  38.2 0.6 hop.1
  38.9 8.2 %collective-permute-start.4 = (bf16[128,128]{1,0:T(8,128)(2,1)S(1)}, bf16[128,128]{1,0:T(8,128)(2,1)S(1)}, u32[]{:S(2)}, u32[]{:S(2)}) collective-permute-start(bf16[128,128]{1,0:T(8,128)(2,1)S(1)} %hop.1), channel_id=1, source_target_pairs={{32,64},{40,72},{48,80},{56,88},{64,96},{72,104},{80,112},{88,120}... | collective-permute-start | bytes 98312 | tf_op jit(solution)/shard_map/ppermute | solution.py:372
  47.0 1.6 %collective-permute-done.4.refs_1_ = bf16[128,128]{1,0:T(8,128)(2,1)S(1)} collective-permute-done((bf16[128,128]{1,0:T(8,128)(2,1)S(1)}, bf16[128,128]{1,0:T(8,128)(2,1)S(1)}, u32[]{:S(2)}, u32[]{:S(2)}) %collective-permute-start.4) | collective-permute-done | bytes 32800 | tf_op jit(solution)/shard_map/ppermute | solution.py:372
  48.6 0.5 spread.1
  49.1 0.1 collective-permute-start.5
  49.3 2.6 %collective-permute-start.6 = (bf16[128,128]{1,0:T(8,128)(2,1)S(1)}, bf16[128,128]{1,0:T(8,128)(2,1)S(1)}, u32[]{:S(2)}, u32[]{:S(2)}) collective-permute-start(bf16[128,128]{1,0:T(8,128)(2,1)S(1)} %get-tuple-element.29), channel_id=1, source_target_pairs={{0,16},{8,24},{16,0},{24,8},{32,48},{40,56},{48,32},{56,40},{64,80... | collective-permute-start | bytes 98312 | tf_op jit(solution)/shard_map/ppermute | solution.py:366
  51.9 1.8 %collective-permute-start.7 = (bf16[128,128]{1,0:T(8,128)(2,1)S(1)}, bf16[128,128]{1,0:T(8,128)(2,1)S(1)}, u32[]{:S(2)}, u32[]{:S(2)}) collective-permute-start(bf16[128,128]{1,0:T(8,128)(2,1)S(1)} %get-tuple-element.30), channel_id=1, source_target_pairs={{0,24},{8,16},{16,8},{24,0},{32,56},{40,48},{48,40},{56,32},{64,88... | collective-permute-start | bytes 98312 | tf_op jit(solution)/shard_map/ppermute | solution.py:366
  53.6 0.0 collective-permute-done.5.refs_1_
  53.6 0.6 collective-permute-done.6.refs_2_
  54.2 3.4 %collective-permute-done.7.refs_3_ = bf16[128,128]{1,0:T(8,128)(2,1)S(1)} collective-permute-done((bf16[128,128]{1,0:T(8,128)(2,1)S(1)}, bf16[128,128]{1,0:T(8,128)(2,1)S(1)}, u32[]{:S(2)}, u32[]{:S(2)}) %collective-permute-start.7) | collective-permute-done | bytes 32800 | tf_op jit(solution)/shard_map/ppermute | solution.py:366
  57.6 2.3 %read_and_project.1 = (bf16[64,2048]{1,0:T(8,128)(2,1)S(1)}, bf16[64,2048]{1,0:T(8,128)(2,1)S(1)}, bf16[64,2048]{1,0:T(8,128)(2,1)S(1)}, bf16[64,2048]{1,0:T(8,128)(2,1)S(1)}) custom-call(bf16[128,128]{1,0:T(8,128)(2,1)S(1)} %get-tuple-element.27.refs_0_, bf16[128,128]{1,0:T(8,128)(2,1)S(1)} %collective-permute-done.5.refs_1_, ...), custom_call_target="tpu_custom_call" | custom-call | tf_op jit(solution)/shard_map/read_and_project/pallas_call | solution.py:465
  59.9 3.4 %collective-permute-start.8 = (bf16[64,2048]{1,0:T(8,128)(2,1)S(1)}, bf16[64,2048]{1,0:T(8,128)(2,1)S(1)}, u32[]{:S(2)}, u32[]{:S(2)}) collective-permute-start(bf16[64,2048]{1,0:T(8,128)(2,1)S(1)} %get-tuple-element.38), channel_id=1, source_target_pairs={{0,4},{2,6},{4,0},{6,2},{1,5},{3,7},{5,1},{7,3},{8,12},{10,14},{12... | collective-permute-start | bytes 786440 | tf_op jit(solution)/shard_map/ppermute | solution.py:366
  63.3 0.8 %collective-permute-start.9 = (bf16[64,2048]{1,0:T(8,128)(2,1)S(1)}, bf16[64,2048]{1,0:T(8,128)(2,1)S(1)}, u32[]{:S(2)}, u32[]{:S(2)}) collective-permute-start(bf16[64,2048]{1,0:T(8,128)(2,1)S(1)} %get-tuple-element.39), channel_id=1, source_target_pairs={{0,2},{2,0},{4,6},{6,4},{1,3},{3,1},{5,7},{7,5},{8,10},{10,8},{12,... | collective-permute-start | bytes 786440 | tf_op jit(solution)/shard_map/ppermute | solution.py:366
  64.0 0.3 collective-permute-start.10
  64.3 3.8 %collective-permute-done.8 = bf16[64,2048]{1,0:T(8,128)(2,1)S(1)} collective-permute-done((bf16[64,2048]{1,0:T(8,128)(2,1)S(1)}, bf16[64,2048]{1,0:T(8,128)(2,1)S(1)}, u32[]{:S(2)}, u32[]{:S(2)}) %collective-permute-start.8) | collective-permute-done | bytes 262176 | tf_op jit(solution)/shard_map/ppermute | solution.py:366
  68.1 3.2 %collective-permute-done.9 = bf16[64,2048]{1,0:T(8,128)(2,1)S(1)} collective-permute-done((bf16[64,2048]{1,0:T(8,128)(2,1)S(1)}, bf16[64,2048]{1,0:T(8,128)(2,1)S(1)}, u32[]{:S(2)}, u32[]{:S(2)}) %collective-permute-start.9) | collective-permute-done | bytes 262176 | tf_op jit(solution)/shard_map/ppermute | solution.py:366
  71.3 0.4 collective-permute-done.10
  71.6 0.8 %fusion = bf16[1,64,2048]{2,1,0:T(8,128)(2,1)} fusion(bf16[64,2048]{1,0:T(8,128)(2,1)S(1)} %collective-permute-done.10, bf16[64,2048]{1,0:T(8,128)(2,1)S(1)} %collective-permute-done.9, bf16[64,2048]{1,0:T(8,128)(2,1)S(1)} %collective-permute-done.8, bf16[64,2048]{1,0:T(8,128)(2,1)S(1)} %get-tuple-element.37), kind=kLoop, calls=%fused_computation.1 | loop fusion | flops 1048576 | bytes 1310720 | tf_op jit(solution)/shard_map/broadcast_in_dim | solution.py:475
Async XLA Ops:
  12.3 7.9 %collective-permute-start = (bf16[128,256]{1,0:T(8,128)(2,1)S(1)}, bf16[128,256]{1,0:T(8,128)(2,1)S(1)}, u32[]{:S(2)}, u32[]{:S(2)}) collective-permute-start(bf16[128,256]{1,0:T(8,128)(2,1)S(1)} %get-tuple-element.24), channel_id=1, source_target_pairs={{0,8},{8,0},{16,24},{24,16},{32,40},{40,32},{48,56},{56,48},{64,72... | collective-permute-start | bytes 196616 | tf_op jit(solution)/shard_map/ppermute | solution.py:366
  15.2 9.5 %collective-permute-start.1 = (bf16[128,256]{1,0:T(8,128)(2,1)S(1)}, bf16[128,256]{1,0:T(8,128)(2,1)S(1)}, u32[]{:S(2)}, u32[]{:S(2)}) collective-permute-start(bf16[128,256]{1,0:T(8,128)(2,1)S(1)} %get-tuple-element.25), channel_id=1, source_target_pairs={{0,16},{8,24},{16,0},{24,8},{32,48},{40,56},{48,32},{56,40},{64,80... | collective-permute-start | bytes 196616 | tf_op jit(solution)/shard_map/ppermute | solution.py:366
  20.2 6.1 %collective-permute-start.2 = (bf16[128,256]{1,0:T(8,128)(2,1)S(1)}, bf16[128,256]{1,0:T(8,128)(2,1)S(1)}, u32[]{:S(2)}, u32[]{:S(2)}) collective-permute-start(bf16[128,256]{1,0:T(8,128)(2,1)S(1)} %get-tuple-element.26), channel_id=1, source_target_pairs={{0,24},{8,16},{16,8},{24,0},{32,56},{40,48},{48,40},{56,32},{64,88... | collective-permute-start | bytes 196616 | tf_op jit(solution)/shard_map/ppermute | solution.py:366
  26.8 11.4 %collective-permute-start.3 = (bf16[128,128]{1,0:T(8,128)(2,1)S(1)}, bf16[128,128]{1,0:T(8,128)(2,1)S(1)}, u32[]{:S(2)}, u32[]{:S(2)}) collective-permute-start(bf16[128,128]{1,0:T(8,128)(2,1)S(1)} %macro.1), channel_id=1, source_target_pairs={{0,32},{8,40},{16,48},{24,56},{32,64},{40,72},{48,80},{56,88},{64,... | collective-permute-start | bytes 98312 | tf_op jit(solution)/shard_map/ppermute | solution.py:372
  38.9 9.7 %collective-permute-start.4 = (bf16[128,128]{1,0:T(8,128)(2,1)S(1)}, bf16[128,128]{1,0:T(8,128)(2,1)S(1)}, u32[]{:S(2)}, u32[]{:S(2)}) collective-permute-start(bf16[128,128]{1,0:T(8,128)(2,1)S(1)} %hop.1), channel_id=1, source_target_pairs={{32,64},{40,72},{48,80},{56,88},{64,96},{72,104},{80,112},{88,120}... | collective-permute-start | bytes 98312 | tf_op jit(solution)/shard_map/ppermute | solution.py:372
  49.1 4.5 %collective-permute-start.5 = (bf16[128,128]{1,0:T(8,128)(2,1)S(1)}, bf16[128,128]{1,0:T(8,128)(2,1)S(1)}, u32[]{:S(2)}, u32[]{:S(2)}) collective-permute-start(bf16[128,128]{1,0:T(8,128)(2,1)S(1)} %get-tuple-element.28), channel_id=1, source_target_pairs={{0,8},{8,0},{16,24},{24,16},{32,40},{40,32},{48,56},{56,48},{64,72... | collective-permute-start | bytes 98312 | tf_op jit(solution)/shard_map/ppermute | solution.py:366
  49.3 4.9 %collective-permute-start.6 = (bf16[128,128]{1,0:T(8,128)(2,1)S(1)}, bf16[128,128]{1,0:T(8,128)(2,1)S(1)}, u32[]{:S(2)}, u32[]{:S(2)}) collective-permute-start(bf16[128,128]{1,0:T(8,128)(2,1)S(1)} %get-tuple-element.29), channel_id=1, source_target_pairs={{0,16},{8,24},{16,0},{24,8},{32,48},{40,56},{48,32},{56,40},{64,80... | collective-permute-start | bytes 98312 | tf_op jit(solution)/shard_map/ppermute | solution.py:366
  51.9 5.7 %collective-permute-start.7 = (bf16[128,128]{1,0:T(8,128)(2,1)S(1)}, bf16[128,128]{1,0:T(8,128)(2,1)S(1)}, u32[]{:S(2)}, u32[]{:S(2)}) collective-permute-start(bf16[128,128]{1,0:T(8,128)(2,1)S(1)} %get-tuple-element.30), channel_id=1, source_target_pairs={{0,24},{8,16},{16,8},{24,0},{32,56},{40,48},{48,40},{56,32},{64,88... | collective-permute-start | bytes 98312 | tf_op jit(solution)/shard_map/ppermute | solution.py:366
  59.9 8.2 %collective-permute-start.8 = (bf16[64,2048]{1,0:T(8,128)(2,1)S(1)}, bf16[64,2048]{1,0:T(8,128)(2,1)S(1)}, u32[]{:S(2)}, u32[]{:S(2)}) collective-permute-start(bf16[64,2048]{1,0:T(8,128)(2,1)S(1)} %get-tuple-element.38), channel_id=1, source_target_pairs={{0,4},{2,6},{4,0},{6,2},{1,5},{3,7},{5,1},{7,3},{8,12},{10,14},{12... | collective-permute-start | bytes 786440 | tf_op jit(solution)/shard_map/ppermute | solution.py:366
  63.3 8.0 %collective-permute-start.9 = (bf16[64,2048]{1,0:T(8,128)(2,1)S(1)}, bf16[64,2048]{1,0:T(8,128)(2,1)S(1)}, u32[]{:S(2)}, u32[]{:S(2)}) collective-permute-start(bf16[64,2048]{1,0:T(8,128)(2,1)S(1)} %get-tuple-element.39), channel_id=1, source_target_pairs={{0,2},{2,0},{4,6},{6,4},{1,3},{3,1},{5,7},{7,5},{8,10},{10,8},{12,... | collective-permute-start | bytes 786440 | tf_op jit(solution)/shard_map/ppermute | solution.py:366
  64.0 7.6 %collective-permute-start.10 = (bf16[64,2048]{1,0:T(8,128)(2,1)S(1)}, bf16[64,2048]{1,0:T(8,128)(2,1)S(1)}, u32[]{:S(2)}, u32[]{:S(2)}) collective-permute-start(bf16[64,2048]{1,0:T(8,128)(2,1)S(1)} %get-tuple-element.40), channel_id=1, source_target_pairs={{0,6},{2,4},{4,2},{6,0},{1,7},{3,5},{5,3},{7,1},{8,14},{10,12},{12... | collective-permute-start | bytes 786440 | tf_op jit(solution)/shard_map/ppermute | solution.py:366

commit v5 on v4

v5 whole, which is shorter than its diff:
```python
import functools

import jax
import jax.numpy as jnp
from jax import lax
from jax.experimental import pallas as pl
from jax.experimental.pallas import tpu as pltpu
from jax.sharding import PartitionSpec as P

BLOCK = 64
HEADS_PER_STEP = 4
epsilon = 1e-06
f32 = jnp.float32
bf16 = jnp.bfloat16


def dot_nn(left, right):
    return lax.dot_general(left, right, (((1,), (0,)), ((), ())), preferred_element_type=f32)


def dot_nt(left, right):
    return lax.dot_general(left, right, (((1,), (1,)), ((), ())), preferred_element_type=f32)


def dot_tn(left, right):
    return lax.dot_general(left, right, (((0,), (0,)), ((), ())), preferred_element_type=f32)


def halves(value):
    top = value.astype(bf16)
    return top, (value - top.astype(f32)).astype(bf16)


def square_product(left, right):
    width = right[0].shape[1]
    side = jnp.concatenate([right[0], right[1]], axis=1)
    both = dot_nn(
        jnp.concatenate([left[0], left[1]], axis=1), jnp.concatenate([side, side], axis=0)
    )
    return both[:, :width] + both[:, width:]


def iota(shape, dim):
    return lax.broadcasted_iota(jnp.int32, shape, dim)


def local_kernel(
    far_lengths, far_query, far_keys, far_values, far_beta, far_decay, far_weight, far_gain, reads, offsets, maps, adds, *rest
):
    weight, gain = rest[:2]
    sends = rest[2:-10]
    inner_mask, read_mask, edge_mask = rest[-10:-7]
    lengths, query_all, keys_all, values_all, beta, decay, done = rest[-7:]
    turns = query_all.shape[0]
    tokens = query_all.shape[1]
    heads_here = reads.shape[0] // turns
    width = reads.shape[2]
    refl = keys_all.shape[2]
    steps = BLOCK * refl
    blocks = tokens // BLOCK
    first = lax.axis_index("seq") * tokens
    place = lax.rem(lax.axis_index("seq"), len(sends))
    row = iota((steps, steps), 0)
    col = iota((steps, steps), 1)
    eye = row == col
    unit = jnp.where(eye, 1.0, 0.0).astype(f32)
    step_col = iota((steps, 1), 0)
    token_col = step_col // refl
    refl_col = step_col % refl
    token_lane = iota((steps, BLOCK), 1)
    token_row = iota((1, steps), 1) // refl
    read_col = iota((BLOCK, 1), 0)
    read_lane = iota((BLOCK, BLOCK), 1)
    read_step = iota((BLOCK, steps), 1)
    read_token = read_step // refl
    hidden = -1e30

    span = heads_here * width
    copies = [
        pltpu.make_async_copy(source, target, done.at[index])
        for index, (source, target) in enumerate(
            [(far_lengths, lengths), (far_decay, decay), (far_beta, beta)]
        )
    ]

    passed = [
        pltpu.make_async_copy(source, target, done.at[3 + 3 * turns + index])
        for index, (source, target) in enumerate([(far_weight, weight), (far_gain, gain)])
    ]

    def fetch(kind, part):
        lanes = pl.ds(part * span, span)
        source, target = [
            (far_keys.at[0, :, :, lanes], keys_all.at[part]),
            (far_values.at[0, :, :, lanes], values_all.at[part]),
            (far_query.at[0, :, lanes], query_all.at[part]),
        ][kind]
        return pltpu.make_async_copy(source, target, done.at[3 + kind * turns + part])

    for copy in copies:
        copy.start()
    for part in range(turns):
        for kind in range(3):
            fetch(kind, part).start()
    for copy in passed:
        copy.start()
    for copy in copies:
        copy.wait()
    ends, end = [], jnp.int32(0)
    for doc in range(lengths.shape[1]):
        end = end + lengths[0, doc]
        ends.append(end)

    def start_of(position):
        start = jnp.zeros_like(position)
        for end in ends:
            start = jnp.where(end <= position, end, start)
        return start

    for block in range(blocks):
        begin = first + block * BLOCK
        start = start_of(begin + token_col)
        inner_mask[block] = jnp.where(
            (col < row) & (begin + col // refl >= start), 0.0, hidden
        )
        read_start = start_of(begin + read_col)
        read_mask[block] = jnp.where(
            (read_token <= read_col) & (begin + read_token >= read_start), 0.0, hidden
        )
        start_row = start_of(begin + token_row)
        last_start = start_of(begin + token_row * 0 + (BLOCK - 1))
        edge_mask[block, 0:1, :] = jnp.where(start_row < begin, 0.0, hidden)
        edge_mask[block, 1:2, :] = jnp.where(begin + token_row >= last_start, 0.0, hidden)

    def to_row(column):
        return jnp.sum(jnp.where(eye, column, 0.0), axis=0, keepdims=True)

    def to_col(line):
        return jnp.sum(jnp.where(eye, line, 0.0), axis=1, keepdims=True)

    def run(turn, unused):
        keys, values, query = keys_all.at[turn], values_all.at[turn], query_all.at[turn]
        for kind in range(3):
            fetch(kind, turn).wait()
        chains = []
        for block in range(blocks):
            for local in range(heads_here):
                lanes = slice(local * width, (local + 1) * width)
                at = block * BLOCK
                rows = slice(at, at + BLOCK)
                chains.append(
                    dict(
                        local=local,
                        block=block,
                        rows=rows,
                        lanes=lanes,
                        head=turn * heads_here + local,
                        key=keys[rows, :, lanes].reshape(steps, width),
                    )
                )
        for c in chains:
            c["gram"] = dot_nt(c["key"], c["key"])
        for c in chains:
            gate = decay[pl.ds(c["head"], 1), :][:, c["rows"]]
            cum = jnp.sum(jnp.where(token_lane <= token_col, gate, 0.0), axis=1, keepdims=True)
            beta_here = beta[refl - 1, pl.ds(c["head"], 1), :][:, c["rows"]]
            for j in range(refl - 1):
                beta_here = jnp.where(
                    refl_col == j, beta[j, pl.ds(c["head"], 1), :][:, c["rows"]], beta_here
                )
            c["cum"] = cum
            c["strength"] = jnp.sum(
                jnp.where(token_lane == token_col, beta_here, 0.0), axis=1, keepdims=True
            )
        for c in chains:
            diagonal = jnp.where(eye, c["gram"], 0.0)
            c["scale"] = lax.rsqrt(jnp.sum(diagonal, axis=1, keepdims=True) + epsilon)
            c["scale_row"] = lax.rsqrt(jnp.sum(diagonal, axis=0, keepdims=True) + epsilon)
            c["cum_row"] = to_row(c["cum"])
            c["strength_row"] = to_row(c["strength"])
        for c in chains:
            ratio = jnp.exp(jnp.minimum(c["cum"] - c["cum_row"], inner_mask[c["block"]]))
            system = (c["strength"] * c["scale"]) * ratio * c["gram"] * c["scale_row"]
            c["system"] = halves(system)
            c["inverse"] = unit - jnp.where((row ^ col) == 1, system, 0.0)
        size = 2
        while size < steps:
            mask = ((row // size) ^ (col // size)) == 1
            for c in chains:
                c["halves"] = halves(c["inverse"])
                corner = tuple(jnp.where(mask, part, jnp.zeros_like(part)) for part in c["system"])
                c["moved"] = square_product(corner, c["halves"])
            for c in chains:
                c["inverse"] = c["inverse"] - square_product(c["halves"], halves(c["moved"]))
            size *= 2
        for c in chains:
            value = values[c["rows"], :, c["lanes"]].reshape(steps, width)
            carry_row = jnp.exp(jnp.minimum(c["cum_row"], edge_mask[c["block"], 0:1, :]))
            c["carry_row"] = carry_row
            value_side = jnp.concatenate(halves(c["inverse"] * c["strength_row"]), axis=1)
            key_side = jnp.concatenate(
                halves(c["inverse"] * (c["strength_row"] * carry_row * c["scale_row"])), axis=1
            )
            c["twice"] = jnp.concatenate([c["key"], c["key"]], axis=0)
            c["writes"] = jnp.concatenate(
                [
                    dot_nn(value_side, jnp.concatenate([value, value], axis=0)),
                    dot_nn(key_side, c["twice"]),
                ],
                axis=1,
            )
        for c in chains:
            cum_row = c["cum_row"]
            fade_row = c["scale_row"] * jnp.exp(
                jnp.minimum(cum_row[:, steps - 1 :] - cum_row, edge_mask[c["block"], 1:2, :])
            )
            faded = jnp.concatenate(halves(to_col(fade_row) * c["writes"]), axis=0)
            summed = dot_tn(c["twice"], faded)
            c["add"] = summed[:, :width]
            c["map"] = c["carry_row"][:, steps - 1 :] * unit - summed[:, width:]
        for c in chains:
            maps[c["head"], c["block"]] = c["map"].astype(bf16)
            adds[c["head"], c["block"]] = c["add"]
        totals = [None] * heads_here
        for c in chains:
            local, rows = c["local"], c["rows"]
            if totals[local] is None:
                totals[local] = jnp.concatenate([c["map"], c["add"]], axis=1)
            else:
                top, low = halves(c["map"])
                tall = jnp.concatenate(
                    [
                        jnp.concatenate([top, top], axis=1),
                        jnp.concatenate([low, jnp.zeros_like(low)], axis=1),
                    ],
                    axis=0,
                )
                joined = dot_nn(tall, jnp.concatenate(halves(totals[local]), axis=0))
                joined = joined[:width] + joined[width:]
                totals[local] = jnp.concatenate(
                    [joined[:, :width], joined[:, width:] + c["add"]], axis=1
                )
        for c in chains:
            local, rows = c["local"], c["rows"]
            query_here = query[rows, c["lanes"]]
            query_f = query_here.astype(f32)
            query_scale = lax.rsqrt(
                jnp.sum(query_f * query_f, axis=1, keepdims=True) + epsilon
            ) * (width ** (-0.5))
            gate = decay[pl.ds(c["head"], 1), :][:, rows]
            read_cum = jnp.sum(jnp.where(read_lane <= read_col, gate, 0.0), axis=1, keepdims=True)
            weights = jnp.exp(jnp.minimum(read_cum - c["cum_row"], read_mask[c["block"]]))
            weights = weights * dot_nt(query_here, c["key"]) * query_scale * c["scale_row"]
            writes_top = c["writes"].astype(bf16)
            seen = dot_nn(
                jnp.concatenate(halves(weights), axis=1),
                jnp.concatenate([writes_top, writes_top], axis=0),
            )
            read_carry = jnp.sum(
                jnp.where(read_step == read_col * refl, c["carry_row"], 0.0), axis=1, keepdims=True
            )
            offsets[c["head"], rows, :] = seen[:, :width]
            reads[c["head"], rows, :] = (
                (read_carry * query_scale) * query_f - seen[:, width:]
            ).astype(bf16)
        for local in range(heads_here):
            both = totals[local].astype(bf16)
            slot = (turn * heads_here + local) ^ place
            for other, send in enumerate(sends):

                @pl.when(slot == other)
                def _():
                    send[...] = both
        return unused

    lax.fori_loop(0, turns, run, 0)
    for copy in passed:
        copy.wait()


def chosen(index, options):
    value = options[0]
    for other in range(1, len(options)):
        value = jnp.where(index == other, options[other], value)
    return value


def run_states(place, parts, state):
    states = []
    width = parts[0].shape[0]
    for member in range(len(parts)):
        states.append(state)
        both = chosen(place ^ member, [part[...] for part in parts])
        top = both[:, :width]
        added = both[:, width:].astype(f32)
        if state is None:
            state = added
        else:
            state = added + dot_nn(
                jnp.concatenate([top, top], axis=1), jnp.concatenate(halves(state), axis=0)
            )
    return states, state


def macro_kernel(*refs):
    count = len(refs) - 1
    place = lax.rem(lax.axis_index("seq"), count)
    states, state = run_states(place, refs[:count], None)
    refs[-1][...] = state.astype(bf16)


def settled(arrivals, count):
    macro = lax.axis_index("seq") // count
    last = jnp.clip(macro - 1, 0, len(arrivals) - 1)
    return chosen(last, [arrived[...] for arrived in arrivals]).astype(f32)


def hop_kernel(*refs, count):
    place = lax.rem(lax.axis_index("seq"), count)
    states, state = run_states(place, refs[-1 - count : -1], settled(refs[: -1 - count], count))
    refs[-1][...] = state.astype(bf16)


def spread_kernel(*refs, count):
    place = lax.rem(lax.axis_index("seq"), count)
    arrivals, parts, outs = refs[: -2 * count], refs[-2 * count : -count], refs[-count:]
    states, state = run_states(place, parts, settled(arrivals, count))
    states = [value.astype(bf16) for value in states]
    for turn in range(count):
        outs[turn][...] = chosen(place ^ turn, states)


def final_kernel(*refs):
    heads = refs[-1].shape[1] // refs[0].shape[1]
    first_states = refs[:heads]
    reads, offsets, maps, adds, gain, weight = refs[heads : heads + 6]
    outs, normed = refs[heads + 6 : -1], refs[-1]
    heads, tokens, width = reads.shape
    blocks = tokens // BLOCK
    place = lax.rem(lax.axis_index("seq"), heads)
    held = [ref[...] for ref in first_states]
    states = [chosen(place ^ head, held) for head in range(heads)]
    for block in range(blocks):
        at = block * BLOCK
        for head in range(heads):
            state = states[head]
            out = dot_nn(reads[head, at : at + BLOCK, :], state) + offsets[head, at : at + BLOCK, :]
            out = out * lax.rsqrt(jnp.mean(out * out, axis=1, keepdims=True) + epsilon)
            normed[at : at + BLOCK, head * width : (head + 1) * width] = (
                out * gain[...]
            ).astype(bf16)
            if block + 1 < blocks:
                states[head] = (dot_nn(maps[head, block], state) + adds[head, block]).astype(bf16)
    peers = len(outs)
    rows = tokens // peers
    me = lax.axis_index("head")
    for turn in range(peers):
        chunk = me ^ turn
        here = normed[pl.ds(pl.multiple_of(chunk * rows, rows), rows), :]
        outs[turn][...] = dot_nn(here, weight[...]).astype(bf16)


def exchanged(value, axis, mask):
    count = lax.axis_size(axis)
    return lax.ppermute(value, axis, [(source, source ^ mask) for source in range(count)])


def passed_on(value, axis, size, row):
    pairs = [(row * size + member, (row + 1) * size + member) for member in range(size)]
    return lax.ppermute(value, axis, pairs)


def grant(mebibytes):
    return pltpu.CompilerParams(vmem_limit_bytes=mebibytes << 20)


def body(
    queries,
    reflect_keys,
    reflect_values,
    reflect_beta,
    log_decay,
    prompt_lengths,
    norm_gain,
    out_weight,
):
    tokens = queries.shape[1]
    refl = reflect_keys.shape[2]
    heads = reflect_beta.shape[3]
    width = queries.shape[2] // heads
    blocks = tokens // BLOCK
    steps = refl * BLOCK
    beta = reflect_beta[0].transpose(1, 2, 0)
    decay = log_decay[0].transpose(1, 0)
    pair = HEADS_PER_STEP
    both_shape = jax.ShapeDtypeStruct((width, 2 * width), bf16)
    reads, offsets, maps, adds, weight, gain, *mine = pl.pallas_call(
        local_kernel,
        in_specs=[pl.BlockSpec(memory_space=pltpu.HBM)] * 8,
        out_specs=[pl.BlockSpec(memory_space=pltpu.VMEM)] * 4
        + [pl.BlockSpec(memory_space=pl.ANY)] * 2
        + [pl.BlockSpec(memory_space=pltpu.VMEM)] * heads,
        out_shape=[
            jax.ShapeDtypeStruct((heads, tokens, width), bf16),
            jax.ShapeDtypeStruct((heads, tokens, width), f32),
            jax.ShapeDtypeStruct((heads, blocks, width, width), bf16),
            jax.ShapeDtypeStruct((heads, blocks, width, width), f32),
            jax.ShapeDtypeStruct(out_weight.shape, bf16),
            jax.ShapeDtypeStruct((1, width), f32),
        ]
        + [both_shape] * heads,
        scratch_shapes=[
            pltpu.VMEM((blocks, steps, steps), f32),
            pltpu.VMEM((blocks, BLOCK, steps), f32),
            pltpu.VMEM((blocks, 8, steps), f32),
            pltpu.SMEM(prompt_lengths.shape, jnp.int32),
            pltpu.VMEM((heads // pair, tokens, pair * width), bf16),
            pltpu.VMEM((heads // pair, tokens, refl, pair * width), bf16),
            pltpu.VMEM((heads // pair, tokens, refl, pair * width), bf16),
            pltpu.VMEM(beta.shape, f32),
            pltpu.VMEM(decay.shape, f32),
            pltpu.SemaphoreType.DMA((5 + 3 * (heads // pair),)),
        ],
        compiler_params=grant(20),
        name="local_blocks",
    )(
        *[
            pltpu.with_memory_space_constraint(array, pltpu.HBM)
            for array in (prompt_lengths, queries, reflect_keys, reflect_values, beta, decay)
            + (out_weight, norm_gain[None])
        ]
    )

    state_shape = jax.ShapeDtypeStruct((width, width), bf16)
    parts = [mine[0]] + [exchanged(mine[r], "seq", r) for r in range(1, heads)]
    sent = pl.pallas_call(
        macro_kernel, out_shape=state_shape, compiler_params=grant(4), name="macro"
    )(*parts)
    arrivals = [passed_on(sent, "seq", heads, 0)]
    for hop in range(1, lax.axis_size("seq") // heads - 1):
        sent = pl.pallas_call(
            functools.partial(hop_kernel, count=heads),
            out_shape=state_shape,
            compiler_params=grant(4),
            name="hop",
        )(*arrivals, *parts)
        arrivals.append(passed_on(sent, "seq", heads, hop))
    given = pl.pallas_call(
        functools.partial(spread_kernel, count=heads),
        out_shape=[state_shape] * heads,
        compiler_params=grant(4),
        name="spread",
    )(*arrivals, *parts)
    states = [given[0]] + [exchanged(given[r], "seq", r) for r in range(1, heads)]

    peers = lax.axis_size("head")
    rows = tokens // peers
    pieces = pl.pallas_call(
        final_kernel,
        out_shape=[jax.ShapeDtypeStruct((rows, out_weight.shape[1]), bf16)] * peers,
        scratch_shapes=[pltpu.VMEM((tokens, heads * width), bf16)],
        compiler_params=grant(16),
        name="read_and_project",
    )(*states, reads, offsets, maps, adds, gain, weight)
    total = pieces[0].astype(f32)
    for turn in (2, 1, 3):
        total = total + exchanged(pieces[turn], "head", turn).astype(f32)
    return total.astype(bf16)[None]


def solution(mesh):
    in_specs = (
        P(("parts", "rep"), "seq", "head"),
        P(("parts", "rep"), "seq", None, "head"),
        P(("parts", "rep"), "seq", None, "head"),
        P(("parts", "rep"), "seq", None, "head"),
        P(("parts", "rep"), "seq", "head"),
        P(("parts", "rep"), None),
        P(),
        P("head", None),
    )
    out_specs = P(("parts", "rep"), ("seq", "head"), None)
    return jax.shard_map(body, mesh=mesh, in_specs=in_specs, out_specs=out_specs, check_vma=False)
```

time: 72.6 us -> 65.6 us (0.904)
  the two profiles are of different devices: /device:TPU:552 before, /device:TPU:40 now
where the time goes in v5:
time: 65.6 us; the launch traced here: 65.5 us
  starting transfers between devices  30.9 us (47%)
  waiting for transfers between devices  19.3 us (29%)
  Pallas kernels  14.4 us (22%)
  other arithmetic  0.84 us (1%)
    ppermute x9, waiting for transfers between devices, exchanged(): lax.ppermute(value, axis, [(source, source ^ mask) for source in range(co...  17.7 us
    ppermute x9, starting transfers between devices, exchanged(): lax.ppermute(value, axis, [(source, source ^ mask) for source in range(co...  17 us
    ppermute x3, starting transfers between devices, passed_on(): return lax.ppermute(value, axis, pairs)  13.9 us
    pallas_call x1, Pallas kernels, body(): pl.pallas_call(local_kernel, in_specs=[pl.BlockSpec(memory_space=pltpu.HB...  9.81 us
    pallas_call x1, Pallas kernels, body(): pl.pallas_call(final_kernel, out_shape=[jax.ShapeDtypeStruct((rows, out_w...  2.27 us
    ppermute x3, waiting for transfers between devices, passed_on(): return lax.ppermute(value, axis, pairs)  1.58 us
  transfers between devices with their start and end apart: 12, of which 7 were waited for; matrix products, arithmetic and copies ran while one was open for 0% of the time, Pallas kernels for 0%

profile of v5, /device:TPU:40, one launch (start us, length us, event | category | flops | bytes accessed | tf_op | source)
XLA Modules:
  0.0 65.5 jit_solution(16049287293211493383)
XLA Ops:
  0.0 9.8 %local_blocks.1 = (bf16[4,256,128]{2,1,0:T(8,128)(2,1)S(1)}, f32[4,256,128]{2,1,0:T(8,128)S(1)}, bf16[4,4,128,128]{3,2,1,0:T(8,128)(2,1)S(1)}, f32[4,4,128,128]{...) custom-call(s32[1,6]{1,0:T(1,128)} %far_lengths.1, ...), custom_call_target="tpu_custom_call" | custom-call | tf_op jit(solution)/shard_map/local_blocks/pallas_call | solution.py:397
  9.8 2.9 %collective-permute-start = (bf16[128,256]{1,0:T(8,128)(2,1)S(1)}, bf16[128,256]{1,0:T(8,128)(2,1)S(1)}, u32[]{:S(2)}, u32[]{:S(2)}) collective-permute-start(bf16[128,256]{1,0:T(8,128)(2,1)S(1)} %get-tuple-element.24), channel_id=1, source_target_pairs={{0,8},{8,0},{16,24},{24,16},{32,40},{40,32},{48,56},{56,48},{64,72... | collective-permute-start | bytes 196616 | tf_op jit(solution)/shard_map/ppermute | solution.py:365
  12.7 5.0 %collective-permute-start.1 = (bf16[128,256]{1,0:T(8,128)(2,1)S(1)}, bf16[128,256]{1,0:T(8,128)(2,1)S(1)}, u32[]{:S(2)}, u32[]{:S(2)}) collective-permute-start(bf16[128,256]{1,0:T(8,128)(2,1)S(1)} %get-tuple-element.25), channel_id=1, source_target_pairs={{0,16},{8,24},{16,0},{24,8},{32,48},{40,56},{48,32},{56,40},{64,80... | collective-permute-start | bytes 196616 | tf_op jit(solution)/shard_map/ppermute | solution.py:365
  17.7 0.0 collective-permute-start.2
  17.7 0.0 collective-permute-done.refs_1_.refs_2_.refs_3_.refs_4_
  17.7 4.6 %collective-permute-done.1.refs_2_.refs_3_.refs_4_.refs_5_ = bf16[128,256]{1,0:T(8,128)(2,1)S(1)} collective-permute-done((bf16[128,256]{1,0:T(8,128)(2,1)S(1)}, bf16[128,256]{1,0:T(8,128)(2,1)S(1)}, u32[]{:S(2)}, u32[]{:S(2)}) %collective-permute-start.1) | collective-permute-done | bytes 65568 | tf_op jit(solution)/shard_map/ppermute | solution.py:365
  22.3 1.5 %collective-permute-done.2.refs_3_.refs_4_.refs_5_.refs_6_ = bf16[128,256]{1,0:T(8,128)(2,1)S(1)} collective-permute-done((bf16[128,256]{1,0:T(8,128)(2,1)S(1)}, bf16[128,256]{1,0:T(8,128)(2,1)S(1)}, u32[]{:S(2)}, u32[]{:S(2)}) %collective-permute-start.2) | collective-permute-done | bytes 65568 | tf_op jit(solution)/shard_map/ppermute | solution.py:365
  23.8 0.5 macro.1
  24.3 12.6 %collective-permute-start.3 = (bf16[128,128]{1,0:T(8,128)(2,1)S(1)}, bf16[128,128]{1,0:T(8,128)(2,1)S(1)}, u32[]{:S(2)}, u32[]{:S(2)}) collective-permute-start(bf16[128,128]{1,0:T(8,128)(2,1)S(1)} %macro.1), channel_id=1, source_target_pairs={{0,32},{8,40},{16,48},{24,56},{1,33},{9,41},{17,49},{25,57},{2,34}... | collective-permute-start | bytes 98312 | tf_op jit(solution)/shard_map/ppermute | solution.py:370
  36.9 1.6 %collective-permute-done.3.refs_0_ = bf16[128,128]{1,0:T(8,128)(2,1)S(1)} collective-permute-done((bf16[128,128]{1,0:T(8,128)(2,1)S(1)}, bf16[128,128]{1,0:T(8,128)(2,1)S(1)}, u32[]{:S(2)}, u32[]{:S(2)}) %collective-permute-start.3) | collective-permute-done | bytes 32800 | tf_op jit(solution)/shard_map/ppermute | solution.py:370
  38.4 0.6 hop.2
  39.1 0.7 %collective-permute-start.4 = (bf16[128,128]{1,0:T(8,128)(2,1)S(1)}, bf16[128,128]{1,0:T(8,128)(2,1)S(1)}, u32[]{:S(2)}, u32[]{:S(2)}) collective-permute-start(bf16[128,128]{1,0:T(8,128)(2,1)S(1)} %hop.2), channel_id=1, source_target_pairs={{32,64},{40,72},{48,80},{56,88},{33,65},{41,73},{49,81},{57,89},{3... | collective-permute-start | bytes 98312 | tf_op jit(solution)/shard_map/ppermute | solution.py:370
  39.8 0.0 collective-permute-done.4.refs_1_
  39.8 0.7 %hop.3 = bf16[128,128]{1,0:T(8,128)(2,1)S(1)} custom-call(bf16[128,128]{1,0:T(8,128)(2,1)S(1)} %collective-permute-done.3.refs_0_, bf16[128,128]{1,0:T(8,128)(2,1)S(1)} %collective-permute-done.4.refs_1_, bf16[128,256]{1,0:T(8,128)(2,1)S(1)} %get-tuple-element.23.refs_0_.refs_1_.refs_2_.refs_3_, ...), custom_call_target="tpu_custom_call" | custom-call | tf_op jit(solution)/shard_map/hop/pallas_call | solution.py:441
  40.4 0.7 %collective-permute-start.5 = (bf16[128,128]{1,0:T(8,128)(2,1)S(1)}, bf16[128,128]{1,0:T(8,128)(2,1)S(1)}, u32[]{:S(2)}, u32[]{:S(2)}) collective-permute-start(bf16[128,128]{1,0:T(8,128)(2,1)S(1)} %hop.3), channel_id=1, source_target_pairs={{64,96},{72,104},{80,112},{88,120},{65,97},{73,105},{81,113},{89,1... | collective-permute-start | bytes 98312 | tf_op jit(solution)/shard_map/ppermute | solution.py:370
  41.1 0.0 collective-permute-done.5.refs_2_
  41.1 0.5 spread.1
  41.6 0.3 collective-permute-start.6
  42.0 2.4 %collective-permute-start.7 = (bf16[128,128]{1,0:T(8,128)(2,1)S(1)}, bf16[128,128]{1,0:T(8,128)(2,1)S(1)}, u32[]{:S(2)}, u32[]{:S(2)}) collective-permute-start(bf16[128,128]{1,0:T(8,128)(2,1)S(1)} %get-tuple-element.29), channel_id=1, source_target_pairs={{0,16},{8,24},{16,0},{24,8},{32,48},{40,56},{48,32},{56,40},{64,80... | collective-permute-start | bytes 98312 | tf_op jit(solution)/shard_map/ppermute | solution.py:365
  44.4 1.9 %collective-permute-start.8 = (bf16[128,128]{1,0:T(8,128)(2,1)S(1)}, bf16[128,128]{1,0:T(8,128)(2,1)S(1)}, u32[]{:S(2)}, u32[]{:S(2)}) collective-permute-start(bf16[128,128]{1,0:T(8,128)(2,1)S(1)} %get-tuple-element.30), channel_id=1, source_target_pairs={{0,24},{8,16},{16,8},{24,0},{32,56},{40,48},{48,40},{56,32},{64,88... | collective-permute-start | bytes 98312 | tf_op jit(solution)/shard_map/ppermute | solution.py:365
  46.3 0.0 collective-permute-done.6.refs_1_
  46.3 0.6 collective-permute-done.7.refs_2_
  46.9 3.2 %collective-permute-done.8.refs_3_ = bf16[128,128]{1,0:T(8,128)(2,1)S(1)} collective-permute-done((bf16[128,128]{1,0:T(8,128)(2,1)S(1)}, bf16[128,128]{1,0:T(8,128)(2,1)S(1)}, u32[]{:S(2)}, u32[]{:S(2)}) %collective-permute-start.8) | collective-permute-done | bytes 32800 | tf_op jit(solution)/shard_map/ppermute | solution.py:365
  50.1 2.3 %read_and_project.1 = (bf16[64,2048]{1,0:T(8,128)(2,1)S(1)}, bf16[64,2048]{1,0:T(8,128)(2,1)S(1)}, bf16[64,2048]{1,0:T(8,128)(2,1)S(1)}, bf16[64,2048]{1,0:T(8,128)(2,1)S(1)}) custom-call(bf16[128,128]{1,0:T(8,128)(2,1)S(1)} %get-tuple-element.27.refs_0_, bf16[128,128]{1,0:T(8,128)(2,1)S(1)} %collective-permute-done.6.refs_1_, ...), custom_call_target="tpu_custom_call" | custom-call | tf_op jit(solution)/shard_map/read_and_project/pallas_call | solution.py:458
  52.4 3.4 %collective-permute-start.9 = (bf16[64,2048]{1,0:T(8,128)(2,1)S(1)}, bf16[64,2048]{1,0:T(8,128)(2,1)S(1)}, u32[]{:S(2)}, u32[]{:S(2)}) collective-permute-start(bf16[64,2048]{1,0:T(8,128)(2,1)S(1)} %get-tuple-element.38), channel_id=1, source_target_pairs={{0,4},{2,6},{4,0},{6,2},{1,5},{3,7},{5,1},{7,3},{8,12},{10,14},{12... | collective-permute-start | bytes 786440 | tf_op jit(solution)/shard_map/ppermute | solution.py:365
  55.8 0.7 %collective-permute-start.10 = (bf16[64,2048]{1,0:T(8,128)(2,1)S(1)}, bf16[64,2048]{1,0:T(8,128)(2,1)S(1)}, u32[]{:S(2)}, u32[]{:S(2)}) collective-permute-start(bf16[64,2048]{1,0:T(8,128)(2,1)S(1)} %get-tuple-element.39), channel_id=1, source_target_pairs={{0,2},{2,0},{4,6},{6,4},{1,3},{3,1},{5,7},{7,5},{8,10},{10,8},{12,... | collective-permute-start | bytes 786440 | tf_op jit(solution)/shard_map/ppermute | solution.py:365
  56.5 0.3 collective-permute-start.11
  56.8 4.6 %collective-permute-done.9 = bf16[64,2048]{1,0:T(8,128)(2,1)S(1)} collective-permute-done((bf16[64,2048]{1,0:T(8,128)(2,1)S(1)}, bf16[64,2048]{1,0:T(8,128)(2,1)S(1)}, u32[]{:S(2)}, u32[]{:S(2)}) %collective-permute-start.9) | collective-permute-done | bytes 262176 | tf_op jit(solution)/shard_map/ppermute | solution.py:365
  61.4 3.2 %collective-permute-done.10 = bf16[64,2048]{1,0:T(8,128)(2,1)S(1)} collective-permute-done((bf16[64,2048]{1,0:T(8,128)(2,1)S(1)}, bf16[64,2048]{1,0:T(8,128)(2,1)S(1)}, u32[]{:S(2)}, u32[]{:S(2)}) %collective-permute-start.10) | collective-permute-done | bytes 262176 | tf_op jit(solution)/shard_map/ppermute | solution.py:365
  64.7 0.0 collective-permute-done.11
  64.7 0.8 %fusion = bf16[1,64,2048]{2,1,0:T(8,128)(2,1)} fusion(bf16[64,2048]{1,0:T(8,128)(2,1)S(1)} %collective-permute-done.11, bf16[64,2048]{1,0:T(8,128)(2,1)S(1)} %collective-permute-done.10, bf16[64,2048]{1,0:T(8,128)(2,1)S(1)} %collective-permute-done.9, bf16[64,2048]{1,0:T(8,128)(2,1)S(1)} %get-tuple-element.37), kind=kLoop, calls=%fused_computation.1 | loop fusion | flops 1048576 | bytes 1310720 | tf_op jit(solution)/shard_map/broadcast_in_dim | solution.py:468
Async XLA Ops:
  9.8 7.9 %collective-permute-start = (bf16[128,256]{1,0:T(8,128)(2,1)S(1)}, bf16[128,256]{1,0:T(8,128)(2,1)S(1)}, u32[]{:S(2)}, u32[]{:S(2)}) collective-permute-start(bf16[128,256]{1,0:T(8,128)(2,1)S(1)} %get-tuple-element.24), channel_id=1, source_target_pairs={{0,8},{8,0},{16,24},{24,16},{32,40},{40,32},{48,56},{56,48},{64,72... | collective-permute-start | bytes 196616 | tf_op jit(solution)/shard_map/ppermute | solution.py:365
  12.7 9.5 %collective-permute-start.1 = (bf16[128,256]{1,0:T(8,128)(2,1)S(1)}, bf16[128,256]{1,0:T(8,128)(2,1)S(1)}, u32[]{:S(2)}, u32[]{:S(2)}) collective-permute-start(bf16[128,256]{1,0:T(8,128)(2,1)S(1)} %get-tuple-element.25), channel_id=1, source_target_pairs={{0,16},{8,24},{16,0},{24,8},{32,48},{40,56},{48,32},{56,40},{64,80... | collective-permute-start | bytes 196616 | tf_op jit(solution)/shard_map/ppermute | solution.py:365
  17.7 6.1 %collective-permute-start.2 = (bf16[128,256]{1,0:T(8,128)(2,1)S(1)}, bf16[128,256]{1,0:T(8,128)(2,1)S(1)}, u32[]{:S(2)}, u32[]{:S(2)}) collective-permute-start(bf16[128,256]{1,0:T(8,128)(2,1)S(1)} %get-tuple-element.26), channel_id=1, source_target_pairs={{0,24},{8,16},{16,8},{24,0},{32,56},{40,48},{48,40},{56,32},{64,88... | collective-permute-start | bytes 196616 | tf_op jit(solution)/shard_map/ppermute | solution.py:365
  24.3 14.1 %collective-permute-start.3 = (bf16[128,128]{1,0:T(8,128)(2,1)S(1)}, bf16[128,128]{1,0:T(8,128)(2,1)S(1)}, u32[]{:S(2)}, u32[]{:S(2)}) collective-permute-start(bf16[128,128]{1,0:T(8,128)(2,1)S(1)} %macro.1), channel_id=1, source_target_pairs={{0,32},{8,40},{16,48},{24,56},{1,33},{9,41},{17,49},{25,57},{2,34}... | collective-permute-start | bytes 98312 | tf_op jit(solution)/shard_map/ppermute | solution.py:370
  39.1 0.7 %collective-permute-start.4 = (bf16[128,128]{1,0:T(8,128)(2,1)S(1)}, bf16[128,128]{1,0:T(8,128)(2,1)S(1)}, u32[]{:S(2)}, u32[]{:S(2)}) collective-permute-start(bf16[128,128]{1,0:T(8,128)(2,1)S(1)} %hop.2), channel_id=1, source_target_pairs={{32,64},{40,72},{48,80},{56,88},{33,65},{41,73},{49,81},{57,89},{3... | collective-permute-start | bytes 98312 | tf_op jit(solution)/shard_map/ppermute | solution.py:370
  40.4 0.7 %collective-permute-start.5 = (bf16[128,128]{1,0:T(8,128)(2,1)S(1)}, bf16[128,128]{1,0:T(8,128)(2,1)S(1)}, u32[]{:S(2)}, u32[]{:S(2)}) collective-permute-start(bf16[128,128]{1,0:T(8,128)(2,1)S(1)} %hop.3), channel_id=1, source_target_pairs={{64,96},{72,104},{80,112},{88,120},{65,97},{73,105},{81,113},{89,1... | collective-permute-start | bytes 98312 | tf_op jit(solution)/shard_map/ppermute | solution.py:370
  41.6 4.7 %collective-permute-start.6 = (bf16[128,128]{1,0:T(8,128)(2,1)S(1)}, bf16[128,128]{1,0:T(8,128)(2,1)S(1)}, u32[]{:S(2)}, u32[]{:S(2)}) collective-permute-start(bf16[128,128]{1,0:T(8,128)(2,1)S(1)} %get-tuple-element.28), channel_id=1, source_target_pairs={{0,8},{8,0},{16,24},{24,16},{32,40},{40,32},{48,56},{56,48},{64,72... | collective-permute-start | bytes 98312 | tf_op jit(solution)/shard_map/ppermute | solution.py:365
  42.0 4.9 %collective-permute-start.7 = (bf16[128,128]{1,0:T(8,128)(2,1)S(1)}, bf16[128,128]{1,0:T(8,128)(2,1)S(1)}, u32[]{:S(2)}, u32[]{:S(2)}) collective-permute-start(bf16[128,128]{1,0:T(8,128)(2,1)S(1)} %get-tuple-element.29), channel_id=1, source_target_pairs={{0,16},{8,24},{16,0},{24,8},{32,48},{40,56},{48,32},{56,40},{64,80... | collective-permute-start | bytes 98312 | tf_op jit(solution)/shard_map/ppermute | solution.py:365
  44.4 5.7 %collective-permute-start.8 = (bf16[128,128]{1,0:T(8,128)(2,1)S(1)}, bf16[128,128]{1,0:T(8,128)(2,1)S(1)}, u32[]{:S(2)}, u32[]{:S(2)}) collective-permute-start(bf16[128,128]{1,0:T(8,128)(2,1)S(1)} %get-tuple-element.30), channel_id=1, source_target_pairs={{0,24},{8,16},{16,8},{24,0},{32,56},{40,48},{48,40},{56,32},{64,88... | collective-permute-start | bytes 98312 | tf_op jit(solution)/shard_map/ppermute | solution.py:365
  52.4 9.1 %collective-permute-start.9 = (bf16[64,2048]{1,0:T(8,128)(2,1)S(1)}, bf16[64,2048]{1,0:T(8,128)(2,1)S(1)}, u32[]{:S(2)}, u32[]{:S(2)}) collective-permute-start(bf16[64,2048]{1,0:T(8,128)(2,1)S(1)} %get-tuple-element.38), channel_id=1, source_target_pairs={{0,4},{2,6},{4,0},{6,2},{1,5},{3,7},{5,1},{7,3},{8,12},{10,14},{12... | collective-permute-start | bytes 786440 | tf_op jit(solution)/shard_map/ppermute | solution.py:365
  55.8 8.9 %collective-permute-start.10 = (bf16[64,2048]{1,0:T(8,128)(2,1)S(1)}, bf16[64,2048]{1,0:T(8,128)(2,1)S(1)}, u32[]{:S(2)}, u32[]{:S(2)}) collective-permute-start(bf16[64,2048]{1,0:T(8,128)(2,1)S(1)} %get-tuple-element.39), channel_id=1, source_target_pairs={{0,2},{2,0},{4,6},{6,4},{1,3},{3,1},{5,7},{7,5},{8,10},{10,8},{12,... | collective-permute-start | bytes 786440 | tf_op jit(solution)/shard_map/ppermute | solution.py:365
  56.5 8.1 %collective-permute-start.11 = (bf16[64,2048]{1,0:T(8,128)(2,1)S(1)}, bf16[64,2048]{1,0:T(8,128)(2,1)S(1)}, u32[]{:S(2)}, u32[]{:S(2)}) collective-permute-start(bf16[64,2048]{1,0:T(8,128)(2,1)S(1)} %get-tuple-element.40), channel_id=1, source_target_pairs={{0,6},{2,4},{4,2},{6,0},{1,7},{3,5},{5,3},{7,1},{8,14},{10,12},{12... | collective-permute-start | bytes 786440 | tf_op jit(solution)/shard_map/ppermute | solution.py:365
